TPU v7x, 32 devices: a whole 2x2x4 slice. The times are simulated.
32 devices in a mesh: dp: 4 (over y, core), row: 2 (over x), col: 4 (over z).
Axes of the slice: x: 2, y: 2, z: 4, core: 2. Of those that a mesh axis runs over, the one named last changes fastest.
Arguments:
- block_input: bfloat16 [1536, 4096], P('row', ('dp', 'col')), may hold values from -6 to 6
- position_ids: int32 [4096], P(('dp', 'row')), may hold values from 0 to 2558, as said below
- attention_gain: float32 [1536], P('row'), may hold values from 0.5 to 1.5
- query_weight: bfloat16 [1536, 1536], P('row', 'col'), may hold values from -0.15625 to 0.15625
- query_bias: float32 [1536], P('col'), may hold values from -3 to 3
- key_value_weight: bfloat16 [1536, 512], P('row'), may hold values from -0.15625 to 0.15625
- key_value_bias: float32 [512], replicated, may hold values from -3 to 3
- output_weight: bfloat16 [1536, 1536], P('row', 'col'), may hold values from -0.5 to 0.5
- feedforward_gain: float32 [1536], P('row'), may hold values from 0.5 to 1.5
- gate_weight: bfloat16 [1536, 8960], P('row', 'col'), may hold values from -0.15625 to 0.15625
- upper_weight: bfloat16 [1536, 8960], P('row', 'col'), may hold values from -0.15625 to 0.15625
- down_weight: bfloat16 [1536, 8960], P('row', 'col'), may hold values from -0.0625 to 0.0625
- out_cotangent: bfloat16 [1536, 4096], P('row', ('dp', 'col')), may hold values from -6 to 6
Outputs:
- block_output: float32 [1536, 4096], P('row', ('dp', 'col'))
- input_grad: float32 [1536, 4096], P('row', ('dp', 'col'))
- attention_gain_grad: float32 [1536], P('row')
- query_weight_grad: float32 [1536, 1536], P(('row', 'dp'), 'col')
- query_bias_grad: float32 [1536], P(('col', 'dp'))
- keyval_weight_grad: float32 [1536, 512], P('row')
- key_value_bias_gradient: float32 [512], replicated
- output_weight_grad: float32 [1536, 1536], P(('row', 'dp'), 'col')
- feedforward_gain_grad: float32 [1536], P('row')
- gate_weight_grad: float32 [1536, 8960], P(('row', 'dp'), 'col')
- upper_weight_grad: float32 [1536, 8960], P(('row', 'dp'), 'col')
- down_weight_grad: float32 [1536, 8960], P(('row', 'dp'), 'col')
Inputs may be any that keep to these rules, and one draw needn't show every extreme that they name: `position_ids`: within each sequence of 512 consecutive tokens the ids rise by 1 to 3 from one token to the next. The first sequence starts at 0; the last sequence's ids run from 1025 to 2558 in steps of 3.
All inputs are finite; a program needn't handle non-finite values.
Results may differ from a plain program's by a relative error of at most 0.035.
Values may be sent and summed in bfloat16 or wider, within the bound.
A program may use at most 320 MiB of HBM per device.

v0:
```python
import jax
import jax.numpy as jnp
from jax import lax
from jax.sharding import PartitionSpec as P

MODEL_WIDTH = 1536
KEYVALUE_HEADS = 2
HEAD_SIZE = 128


EPS = 1e-06
THETA = 1000000.0
NEG = -1e30


def rope_tables(position_ids):
    half_dim = HEAD_SIZE // 2
    frequencies = THETA ** (-(jnp.arange(half_dim, dtype=jnp.float32) * 2.0 / HEAD_SIZE))
    angles = position_ids.astype(jnp.float32)[:, None] * frequencies[None, :]
    cosine_values = jnp.cos(angles)
    sine_lookup = jnp.sin(angles)
    return (
        jnp.concatenate([cosine_values, cosine_values], -1),
        jnp.concatenate([sine_lookup, sine_lookup], -1),
    )


def apply_rotation(values, cosine_values, sine_lookup):
    half_dim = HEAD_SIZE // 2
    turned = jnp.concatenate([-values[..., half_dim:], values[..., :half_dim]], -1)
    return values * cosine_values[:, None, :] + turned * sine_lookup[:, None, :]


def unrotate(gradient, cosine_values, sine_lookup):
    half_dim = HEAD_SIZE // 2
    scaled = gradient * sine_lookup[:, None, :]
    turned = jnp.concatenate([scaled[..., half_dim:], -scaled[..., :half_dim]], -1)
    return gradient * cosine_values[:, None, :] + turned


def row_total(partial_value):
    return lax.psum(partial_value, "row")


def norm_forward(x_float, gain):
    squares = jnp.sum(x_float * x_float, -1)
    rinv = lax.rsqrt(row_total(squares) / MODEL_WIDTH + EPS)[:, None]
    return ((x_float * rinv * gain).astype(jnp.bfloat16), rinv)


def norm_backward(normed_grad, x_float, rinv, gain):
    scaled = normed_grad * gain
    inner = row_total(jnp.sum(scaled * x_float, -1))[:, None]
    input_part = rinv * scaled - x_float * rinv**3 * inner / MODEL_WIDTH
    gain_part = jnp.sum(normed_grad * x_float * rinv, 0)
    return (input_part, gain_part)


def column_gather(values):
    return lax.all_gather(values, "col", axis=0, tiled=True)


def column_sum(partial_value):
    return lax.psum_scatter(
        partial_value.astype(jnp.bfloat16), "col", scatter_dimension=0, tiled=True
    ).astype(jnp.float32)


def row_product(gathered, weight):
    return (
        lax.psum_scatter(
            jnp.dot(gathered, weight, preferred_element_type=jnp.float32).astype(jnp.bfloat16),
            "row",
            scatter_dimension=0,
            tiled=True,
        ).astype(jnp.float32),
        gathered,
    )


def row_project(local_part, weight):
    return lax.dot_general(
        lax.all_gather(local_part, "row", axis=0, tiled=True),
        weight,
        (((1,), (1,)), ((), ())),
        preferred_element_type=jnp.float32,
    )


def row_fold(local_part, partner, weight):
    pair_dims = (((0,), (0,)), ((), ()))

    def accumulate(block_rows):
        grad_sum = lax.dot_general(
            partner, block_rows, pair_dims, preferred_element_type=jnp.float32
        )
        if weight is None:
            return (grad_sum,)
        back_proj = lax.dot_general(
            block_rows, weight, (((1,), (1,)), ((), ())), preferred_element_type=jnp.float32
        )
        column_totals = jnp.sum(block_rows, 0, dtype=jnp.float32)
        return (grad_sum, back_proj, column_totals)

    return accumulate(lax.all_gather(local_part, "row", axis=0, tiled=True))


def causal_scores(query_rot, rotated_keys):
    scores = jnp.einsum(
        "ihd,jd->hij", query_rot, rotated_keys, preferred_element_type=jnp.float32
    ) * HEAD_SIZE ** (-0.5)
    length = query_rot.shape[0]
    allowed = jnp.arange(length)[:, None] >= jnp.arange(length)[None, :]
    return jnp.where(allowed[None], scores, NEG)


def attend(query_rot, rotated_keys, value_second_part):
    scores = causal_scores(query_rot, rotated_keys)
    row_max = jnp.max(scores, -1, keepdims=True)
    log_total = row_max + jnp.log(jnp.sum(jnp.exp(scores - row_max), -1, keepdims=True))
    probs_half = jnp.exp(scores - log_total).astype(jnp.bfloat16)
    attended = jnp.einsum(
        "hij,jd->ihd", probs_half, value_second_part, preferred_element_type=jnp.float32
    ).astype(jnp.bfloat16)
    return (attended, log_total)


def attend_back(query_rot, rotated_keys, value_second_part, attended, att_grad, log_total):
    scale = HEAD_SIZE ** (-0.5)
    softmax_probs = jnp.exp(causal_scores(query_rot, rotated_keys) - log_total)
    probs_half = softmax_probs.astype(jnp.bfloat16)
    prob_grad = jnp.einsum(
        "ihd,jd->hij", att_grad, value_second_part, preferred_element_type=jnp.float32
    )
    row_delta = jnp.einsum("ihd,ihd->hi", att_grad, attended, preferred_element_type=jnp.float32)
    score_half = (softmax_probs * (prob_grad - row_delta[:, :, None])).astype(jnp.bfloat16)
    query_grad = (
        jnp.einsum("hij,jd->ihd", score_half, rotated_keys, preferred_element_type=jnp.float32)
        * scale
    )
    key_grad = (
        jnp.einsum("hij,ihd->jd", score_half, query_rot, preferred_element_type=jnp.float32) * scale
    )
    value_grad = jnp.einsum("hij,ihd->jd", probs_half, att_grad, preferred_element_type=jnp.float32)
    return (query_grad, key_grad, value_grad)


def per_device(
    block_input,
    position_ids,
    attention_gain,
    query_weight,
    query_bias,
    key_value_weight,
    key_value_bias,
    output_weight,
    feedforward_gain,
    gate_weight,
    upper_weight,
    down_weight,
    out_cotangent,
):
    single_float_type = jnp.float32
    brain_float_type = jnp.bfloat16
    column_number = lax.axis_size("col")
    seq_len = position_ids.shape[0]
    heads_here = query_weight.shape[1] // HEAD_SIZE
    query_cols = query_weight.shape[1]
    hidden_cols = gate_weight.shape[1]
    key_value_head = lax.axis_index("col") // (column_number // KEYVALUE_HEADS)
    key_start = key_value_head * HEAD_SIZE
    value_offset = KEYVALUE_HEADS * HEAD_SIZE + key_value_head * HEAD_SIZE
    keyval_local = jnp.concatenate(
        [
            lax.dynamic_slice_in_dim(key_value_weight, key_start, HEAD_SIZE, 1),
            lax.dynamic_slice_in_dim(key_value_weight, value_offset, HEAD_SIZE, 1),
        ],
        1,
    )
    bias_local = jnp.concatenate(
        [
            lax.dynamic_slice_in_dim(key_value_bias, key_start, HEAD_SIZE, 0),
            lax.dynamic_slice_in_dim(key_value_bias, value_offset, HEAD_SIZE, 0),
        ],
        0,
    )
    proj_weight = jnp.concatenate([query_weight, keyval_local], 1)
    proj_bias = jnp.concatenate([query_bias, bias_local], 0)
    pair_weight = jnp.concatenate([gate_weight, upper_weight], 1)
    cosine_values, sine_lookup = rope_tables(position_ids)
    x_float = block_input.T.astype(single_float_type)
    cot_local = out_cotangent.T
    normed_one, rinv_one = norm_forward(x_float, attention_gain)
    normed_one_all = column_gather(normed_one)
    proj_out = row_product(normed_one_all, proj_weight)[0] + proj_bias
    query_rot = apply_rotation(
        proj_out[:, :query_cols].reshape(seq_len, heads_here, HEAD_SIZE), cosine_values, sine_lookup
    ).astype(brain_float_type)
    rotated_keys = apply_rotation(
        proj_out[:, query_cols : query_cols + HEAD_SIZE][:, None, :], cosine_values, sine_lookup
    )[:, 0].astype(brain_float_type)
    value_second_part = proj_out[:, query_cols + HEAD_SIZE :].astype(brain_float_type)
    attended, log_total = attend(query_rot, rotated_keys, value_second_part)
    attended_flat = attended.reshape(seq_len, query_cols)
    hidden_res = x_float + column_sum(row_project(attended_flat, output_weight))
    normed_two, rinv_two = norm_forward(hidden_res, feedforward_gain)
    normed_two_all = column_gather(normed_two)
    gate_upper, normed_two_seq = row_product(normed_two_all, pair_weight)
    gate_lin = gate_upper[:, :hidden_cols]
    upper_lin = gate_upper[:, hidden_cols:]
    sigmoid_gate = jax.nn.sigmoid(gate_lin)
    activated = (gate_lin * sigmoid_gate * upper_lin).astype(brain_float_type)
    block_output = hidden_res + column_sum(row_project(activated, down_weight))
    cotangent_all = column_gather(cot_local)
    act_grad = row_product(cotangent_all, down_weight)[0]
    down_grad = row_fold(activated, cotangent_all, None)[0]
    gate_grad = act_grad * upper_lin * sigmoid_gate * (1.0 + gate_lin * (1.0 - sigmoid_gate))
    upper_grad = act_grad * gate_lin * sigmoid_gate
    pair_grad_half = jnp.concatenate([gate_grad, upper_grad], 1).astype(brain_float_type)
    folded_two = row_fold(pair_grad_half, normed_two_all, pair_weight)
    pair_weight_grad = folded_two[0]
    spread_two = folded_two[1]
    normed_two_grad = column_sum(spread_two)
    hidden_part, ffn_gain_part = norm_backward(
        normed_two_grad, hidden_res, rinv_two, feedforward_gain
    )
    hidden_grad = cot_local.astype(single_float_type) + hidden_part
    hidden_half = hidden_grad.astype(brain_float_type)
    hidden_all = column_gather(hidden_half)
    att_grad = (
        row_product(hidden_all, output_weight)[0]
        .astype(brain_float_type)
        .reshape(seq_len, heads_here, HEAD_SIZE)
    )
    output_grad = row_fold(attended_flat, hidden_all, None)[0]
    query_grad, key_grad, value_grad = attend_back(
        query_rot, rotated_keys, value_second_part, attended, att_grad, log_total
    )
    query_half = (
        unrotate(query_grad, cosine_values, sine_lookup)
        .astype(brain_float_type)
        .reshape(seq_len, query_cols)
    )
    key_half = unrotate(key_grad[:, None, :], cosine_values, sine_lookup)[:, 0].astype(
        brain_float_type
    )
    value_grad_half = value_grad.astype(brain_float_type)
    proj_grad_half = jnp.concatenate([query_half, key_half, value_grad_half], 1)
    folded_one = row_fold(proj_grad_half, normed_one_all, proj_weight)
    projection_weight_gradient = folded_one[0]
    normed_one_grad = column_sum(folded_one[1])
    proj_bias_grad = folded_one[2]
    input_part, attn_gain_part = norm_backward(normed_one_grad, x_float, rinv_one, attention_gain)
    input_grad = hidden_grad + input_part
    key_value_gradient = jnp.zeros(
        (projection_weight_gradient.shape[0], 2 * KEYVALUE_HEADS * HEAD_SIZE), single_float_type
    )
    key_value_gradient = lax.dynamic_update_slice_in_dim(
        key_value_gradient,
        projection_weight_gradient[:, query_cols : query_cols + HEAD_SIZE],
        key_start,
        1,
    )
    key_value_gradient = lax.dynamic_update_slice_in_dim(
        key_value_gradient, projection_weight_gradient[:, query_cols + HEAD_SIZE :], value_offset, 1
    )
    key_value_bias_gradient = jnp.zeros((2 * KEYVALUE_HEADS * HEAD_SIZE,), single_float_type)
    key_value_bias_gradient = lax.dynamic_update_slice_in_dim(
        key_value_bias_gradient, proj_bias_grad[query_cols : query_cols + HEAD_SIZE], key_start, 0
    )
    key_value_bias_gradient = lax.dynamic_update_slice_in_dim(
        key_value_bias_gradient, proj_bias_grad[query_cols + HEAD_SIZE :], value_offset, 0
    )
    shared = (
        lax.psum(key_value_gradient.astype(jnp.bfloat16), ("dp", "col")).astype(jnp.float32),
        lax.psum(key_value_bias_gradient.astype(jnp.bfloat16), ("dp", "col")).astype(jnp.float32),
        lax.psum(attn_gain_part.astype(jnp.bfloat16), ("dp", "col")).astype(jnp.float32),
        lax.psum(ffn_gain_part.astype(jnp.bfloat16), ("dp", "col")).astype(jnp.float32),
    )
    summed = (
        lax.psum_scatter(
            projection_weight_gradient[:, :query_cols].astype(jnp.bfloat16),
            "dp",
            scatter_dimension=0,
            tiled=True,
        ).astype(jnp.float32),
        lax.psum_scatter(
            proj_bias_grad[:query_cols].astype(jnp.bfloat16), "dp", scatter_dimension=0, tiled=True
        ).astype(jnp.float32),
        lax.psum_scatter(
            output_grad.astype(jnp.bfloat16), "dp", scatter_dimension=0, tiled=True
        ).astype(jnp.float32),
        lax.psum_scatter(
            pair_weight_grad[:, :hidden_cols].astype(jnp.bfloat16),
            "dp",
            scatter_dimension=0,
            tiled=True,
        ).astype(jnp.float32),
        lax.psum_scatter(
            pair_weight_grad[:, hidden_cols:].astype(jnp.bfloat16),
            "dp",
            scatter_dimension=0,
            tiled=True,
        ).astype(jnp.float32),
        lax.psum_scatter(
            down_grad.astype(jnp.bfloat16), "dp", scatter_dimension=0, tiled=True
        ).astype(jnp.float32),
    )
    return (
        block_output.T,
        input_grad.T,
        shared[2],
        summed[0],
        summed[1],
        shared[0],
        shared[1],
        summed[2],
        shared[3],
        summed[3],
        summed[4],
        summed[5],
    )


def solution(mesh):
    placed = (
        P("row", ("dp", "col")),
        P(("dp", "row")),
        P("row"),
        P("row", "col"),
        P("col"),
        P("row", None),
        P(),
        P("row", "col"),
        P("row"),
        P("row", "col"),
        P("row", "col"),
        P("row", "col"),
        P("row", ("dp", "col")),
    )
    return jax.shard_map(
        per_device,
        mesh=mesh,
        in_specs=placed,
        out_specs=(
            P("row", ("dp", "col")),
            P("row", ("dp", "col")),
            P("row"),
            P(("row", "dp"), "col"),
            P(("col", "dp")),
            P("row", None),
            P(),
            P(("row", "dp"), "col"),
            P("row"),
            P(("row", "dp"), "col"),
            P(("row", "dp"), "col"),
            P(("row", "dp"), "col"),
        ),
        check_vma=False,
    )
```

profile of v0, /device:TPU:0, one launch (start us, length us, event | category | flops | bytes accessed | tf_op | source)
XLA Modules:
  0.0 1142.9 jit_solution(4654503106055565044)
XLA Ops:
  20.2 37.1 %all-gather.8.cloned.1.call-done = bf16[1024,768]{1,0:T(8,128)(2,1)} async-done(((bf16[256,768]{1,0:T(8,128)(2,1)}), bf16[1024,768]{1,0:T(8,128)(2,1)}) %all-gather.8.cloned.1.call-update) | async-done | bytes 1572880 | tf_op jit(solution)/shard_map/all_gather | solution.py:60
  64.2 19.5 %reduce-scatter.16.cloned.1.call-done = bf16[512,640]{1,0:T(8,128)(2,1)} async-done(((bf16[1024,640]{1,0:T(8,128)(2,1)}), bf16[512,640]{1,0:T(8,128)(2,1)}) %reduce-scatter.16.cloned.1.call-update) | async-done | bytes 655376 | tf_op jit(solution)/shard_map/reduce_scatter | solution.py:71
  131.9 35.5 %reduce-scatter.18.cloned.1.call-done = bf16[256,768]{1,0:T(8,128)(2,1)} async-done(((bf16[1024,768]{1,0:T(8,128)(2,1)}), bf16[256,768]{1,0:T(8,128)(2,1)}) %reduce-scatter.18.cloned.1.call-update) | async-done | bytes 393232 | tf_op jit(solution)/shard_map/reduce_scatter | solution.py:64
  184.3 27.5 %all-gather.10.cloned.1.call-done = bf16[1024,768]{1,0:T(8,128)(2,1)} async-done(((bf16[256,768]{1,0:T(8,128)(2,1)}), bf16[1024,768]{1,0:T(8,128)(2,1)}) %all-gather.10.cloned.1.call-update) | async-done | bytes 1572880 | tf_op jit(solution)/shard_map/all_gather | solution.py:60
  211.9 12.1 %convolution_convert_fusion = bf16[1024,4480]{0,1:T(8,128)(2,1)} fusion(bf16[1024,768]{1,0:T(8,128)(2,1)} %all-gather.10.cloned.1.call-done, bf16[768,4480]{0,1:T(8,128)(2,1)} %constant_dynamic-update-slice_fusion), kind=kOutput, calls=%fused_computation | convolution fusion | flops 7051018240 | bytes 17629184 | tf_op jit(solution)/shard_map/dot_general | solution.py:72
  224.1 25.1 %all-gather.14.cloned.1.call-done = bf16[1024,768]{1,0:T(8,128)(2,1)} async-done(((bf16[256,768]{1,0:T(8,128)(2,1)}), bf16[1024,768]{1,0:T(8,128)(2,1)}) %all-gather.14.cloned.1.call-update) | async-done | bytes 1572880 | tf_op jit(solution)/shard_map/all_gather | solution.py:60
  256.1 102.0 %reduce-scatter.20.cloned.1.call-done = bf16[512,4480]{0,1:T(8,128)(2,1)} async-done(((bf16[1024,4480]{0,1:T(8,128)(2,1)}), bf16[512,4480]{0,1:T(8,128)(2,1)}) %reduce-scatter.20.cloned.1.call-update) | async-done | bytes 4587536 | tf_op jit(solution)/shard_map/reduce_scatter | solution.py:71
  365.2 53.8 %reduce-scatter.24.cloned.1.call-done = bf16[512,2240]{0,1:T(8,128)(2,1)} async-done(((bf16[1024,2240]{0,1:T(8,128)(2,1)}), bf16[512,2240]{0,1:T(8,128)(2,1)}) %reduce-scatter.24.cloned.1.call-update) | async-done | bytes 2293776 | tf_op jit(solution)/shard_map/reduce_scatter | solution.py:71
  428.1 115.2 %all-gather.16.cloned.1.call-done = bf16[1024,4480]{0,1:T(8,128)(2,1)} async-done(((bf16[512,4480]{0,1:T(8,128)(2,1)}), bf16[1024,4480]{0,1:T(8,128)(2,1)}) %all-gather.16.cloned.1.call-update) | async-done | bytes 9175056 | tf_op jit(solution)/shard_map/all_gather | solution.py:105
  543.3 13.0 %convolution_convert_fusion.6 = bf16[1024,768]{1,0:T(8,128)(2,1)} fusion(bf16[1024,4480]{0,1:T(8,128)(2,1)} %all-gather.16.cloned.1.call-done, bf16[768,4480]{0,1:T(8,128)(2,1)} %constant_dynamic-update-slice_fusion), kind=kOutput, calls=%fused_computation.26 | convolution fusion | flops 7047217152 | bytes 17629184 | tf_op jit(solution)/shard_map/dot_general | solution.py:99
  556.4 35.5 %reduce-scatter.26.cloned.1.call-done = bf16[256,768]{1,0:T(8,128)(2,1)} async-done(((bf16[1024,768]{1,0:T(8,128)(2,1)}), bf16[256,768]{1,0:T(8,128)(2,1)}) %reduce-scatter.26.cloned.1.call-update) | async-done | bytes 393232 | tf_op jit(solution)/shard_map/reduce_scatter | solution.py:64
  601.1 35.8 %all-gather.18.cloned.1.call-done = bf16[1024,768]{1,0:T(8,128)(2,1)} async-done(((bf16[256,768]{1,0:T(8,128)(2,1)}), bf16[1024,768]{1,0:T(8,128)(2,1)}) %all-gather.18.cloned.1.call-update) | async-done | bytes 1572880 | tf_op jit(solution)/shard_map/all_gather | solution.py:60
  644.6 12.3 %reduce-scatter.28.cloned.1.call-done = bf16[512,384]{1,0:T(8,128)(2,1)} async-done(((bf16[1024,384]{1,0:T(8,128)(2,1)}), bf16[512,384]{1,0:T(8,128)(2,1)}) %reduce-scatter.28.cloned.1.call-update) | async-done | bytes 393232 | tf_op jit(solution)/shard_map/reduce_scatter | solution.py:71
  672.7 46.8 %all-gather.12.cloned.1.call-done = bf16[1024,2240]{0,1:T(8,128)(2,1)} async-done(((bf16[512,2240]{0,1:T(8,128)(2,1)}), bf16[1024,2240]{0,1:T(8,128)(2,1)}) %all-gather.12.cloned.1.call-update) | async-done | bytes 4587536 | tf_op jit(solution)/shard_map/all_gather | solution.py:83
  737.4 11.6 %convolution_convert_fusion.1 = bf16[768,4480]{1,0:T(8,128)(2,1)S(1)} fusion(bf16[1024,768]{1,0:T(8,128)(2,1)} %all-gather.10.cloned.1.call-done, bf16[1024,4480]{0,1:T(8,128)(2,1)} %all-gather.16.cloned.1.call-done), kind=kOutput, calls=%fused_computation.1 | convolution fusion | flops 7049871360 | bytes 17629184 | tf_op jit(solution)/shard_map/dot_general | solution.py:94
  775.5 13.2 %reduce-scatter.40.cloned.1.call-done = bf16[192,2240]{1,0:T(8,128)(2,1)} async-done(((bf16[768,2240]{1,0:T(8,128)(2,1)}), bf16[192,2240]{1,0:T(8,128)(2,1)}) %reduce-scatter.40.cloned.1.call-update) | async-done | bytes 860176
  793.5 20.2 %reduce-scatter.34.cloned.1.call-done = bf16[192,384]{1,0:T(8,128)(2,1)} async-done(((bf16[768,384]{1,0:T(8,128)(2,1)}), bf16[192,384]{1,0:T(8,128)(2,1)}) %reduce-scatter.34.cloned.1.call-update) | async-done | bytes 147472 | tf_op jit(solution)/shard_map/reduce_scatter | solution.py:290
  815.4 41.2 %reduce-scatter.36.cloned.1.call-done = bf16[192,2240]{1,0:T(8,128)(2,1)} async-done(((bf16[768,2240]{1,0:T(8,128)(2,1)}), bf16[192,2240]{1,0:T(8,128)(2,1)}) %reduce-scatter.36.cloned.1.call-update) | async-done | bytes 860176 | tf_op jit(solution)/shard_map/reduce_scatter | solution.py:293
  859.0 40.3 %reduce-scatter.38.cloned.1.call-done = bf16[192,2240]{1,0:T(8,128)(2,1)} async-done(((bf16[768,2240]{1,0:T(8,128)(2,1)}), bf16[192,2240]{1,0:T(8,128)(2,1)}) %reduce-scatter.38.cloned.1.call-update) | async-done | bytes 860176 | tf_op jit(solution)/shard_map/reduce_scatter | solution.py:299
  908.8 87.0 %all-reduce.4.cloned.1.call-done = bf16[768,512]{1,0:T(8,128)(2,1)} async-done(((bf16[768,512]{1,0:T(8,128)(2,1)}), bf16[768,512]{1,0:T(8,128)(2,1)}) %all-reduce.4.cloned.1.call-update) | async-done | bytes 786448 | tf_op jit(solution)/shard_map/psum | solution.py:275
  998.3 21.7 %reduce-scatter.32.cloned.1.call-done = bf16[192,384]{1,0:T(8,128)(2,1)} async-done(((bf16[768,384]{1,0:T(8,128)(2,1)}), bf16[192,384]{1,0:T(8,128)(2,1)}) %reduce-scatter.32.cloned.1.call-update) | async-done | bytes 147472 | tf_op jit(solution)/shard_map/reduce_scatter | solution.py:281
  1021.6 36.0 %reduce-scatter.30.cloned.1.call-done = bf16[256,768]{1,0:T(8,128)(2,1)} async-done(((bf16[1024,768]{1,0:T(8,128)(2,1)}), bf16[256,768]{1,0:T(8,128)(2,1)}) %reduce-scatter.30.cloned.1.call-update) | async-done | bytes 393232 | tf_op jit(solution)/shard_map/reduce_scatter | solution.py:64
  1064.0 30.3 %reduce-scatter.22.cloned.1.call-done = bf16[256,768]{1,0:T(8,128)(2,1)} async-done(((bf16[1024,768]{1,0:T(8,128)(2,1)}), bf16[256,768]{1,0:T(8,128)(2,1)}) %reduce-scatter.22.cloned.1.call-update) | async-done | bytes 393232 | tf_op jit(solution)/shard_map/reduce_scatter | solution.py:64
  1102.1 31.9 %all-reduce.1 = (bf16[768]{0:T(1024)(128)(2,1)S(1)}, bf16[512]{0:T(512)(128)(2,1)S(1)}, bf16[768]{0:T(1024)(128)(2,1)S(1)}) all-reduce(bf16[768]{0:T(1024)(128)(2,1)S(1)} %get-tuple-element.62, bf16[512]{0:T(512)(128)(2,1)S(1)} %convert_element_type.207, ...), channel_id=1, replica_groups=mesh['dp'=4,'row'=2,'col'=4] {'dp','col'}, use_global_device_ids=true, to_apply=%region_19.20 | all-reduce | flops 2048 | bytes 8192 | tf_op jit(solution)/shard_map/psum | solution.py:277
  (197 shorter events, 222.3 us)
Async XLA Ops:
  7.2 242.0 %copy-start = (bf16[768,2240]{0,1:T(8,128)(2,1)S(1)}, bf16[768,2240]{0,1:T(8,128)(2,1)}, u32[]{:S(2)}) copy-start(bf16[768,2240]{0,1:T(8,128)(2,1)} %param.24) | copy-start | bytes 10321924
  7.2 50.1 %all-gather.8.cloned.1.call-start = ((), (), s32[]{:S(2)}) async-start(), calls=%async_computation.13 | async-start | bytes 1966080 | tf_op jit(solution)/shard_map/all_gather | solution.py:60
  18.3 65.5 %reduce-scatter.16.cloned.1.call-start = ((), (), s32[]{:S(2)}) async-start(), calls=%async_computation.14 | async-start | bytes 1966080 | tf_op jit(solution)/shard_map/reduce_scatter | solution.py:71
  61.5 106.0 %reduce-scatter.18.cloned.1.call-start = ((), (), s32[]{:S(2)}) async-start(), calls=%async_computation.15 | async-start | bytes 1966080 | tf_op jit(solution)/shard_map/reduce_scatter | solution.py:64
  117.3 56.4 %copy-start.20 = (f32[768]{0:T(1024)S(1)}, f32[768]{0:T(1024)}, u32[]{:S(2)}) copy-start(f32[768]{0:T(1024)} %param.21) | copy-start | bytes 9220
  131.9 80.0 %all-gather.10.cloned.1.call-start = ((), (), s32[]{:S(2)}) async-start(), calls=%async_computation.16 | async-start | bytes 1966080 | tf_op jit(solution)/shard_map/all_gather | solution.py:60
  175.8 73.4 %all-gather.14.cloned.1.call-start = ((), (), s32[]{:S(2)}) async-start(), calls=%async_computation.20 | async-start | bytes 1966080 | tf_op jit(solution)/shard_map/all_gather | solution.py:60
  177.8 180.3 %reduce-scatter.20.cloned.1.call-start = ((), (), s32[]{:S(2)}) async-start(), calls=%async_computation.17 | async-start | bytes 13762560 | tf_op jit(solution)/shard_map/reduce_scatter | solution.py:71
  224.0 195.0 %reduce-scatter.24.cloned.1.call-start = ((), (), s32[]{:S(2)}) async-start(), calls=%async_computation.21 | async-start | bytes 6881280 | tf_op jit(solution)/shard_map/reduce_scatter | solution.py:71
  256.0 287.3 %all-gather.16.cloned.1.call-start = ((), (), s32[]{:S(2)}) async-start(), calls=%async_computation.22 | async-start | bytes 13762560 | tf_op jit(solution)/shard_map/all_gather | solution.py:105
  428.1 163.9 %reduce-scatter.26.cloned.1.call-start = ((), (), s32[]{:S(2)}) async-start(), calls=%async_computation.23 | async-start | bytes 1966080 | tf_op jit(solution)/shard_map/reduce_scatter | solution.py:64
  556.4 80.6 %all-gather.18.cloned.1.call-start = ((), (), s32[]{:S(2)}) async-start(), calls=%async_computation.24 | async-start | bytes 1966080 | tf_op jit(solution)/shard_map/all_gather | solution.py:60
  600.9 56.0 %reduce-scatter.28.cloned.1.call-start = ((), (), s32[]{:S(2)}) async-start(), calls=%async_computation.25 | async-start | bytes 1179648 | tf_op jit(solution)/shard_map/reduce_scatter | solution.py:71
  640.4 79.1 %all-gather.12.cloned.1.call-start = ((), (), s32[]{:S(2)}) async-start(), calls=%async_computation.18 | async-start | bytes 6881280 | tf_op jit(solution)/shard_map/all_gather | solution.py:83
  641.0 113.3 %all-gather.20.cloned.1.call-start = ((), (), s32[]{:S(2)}) async-start(), calls=%async_computation.26 | async-start | bytes 1966080 | tf_op jit(solution)/shard_map/all_gather | solution.py:105
  672.6 116.1 %reduce-scatter.40.cloned.1.call-start = ((), (), s32[]{:S(2)}) async-start(), calls=%async_computation.33 | async-start | bytes 4423680
  733.6 80.2 %reduce-scatter.34.cloned.1.call-start = ((), (), s32[]{:S(2)}) async-start(), calls=%async_computation.30 | async-start | bytes 737280 | tf_op jit(solution)/shard_map/reduce_scatter | solution.py:290
  737.1 119.4 %reduce-scatter.36.cloned.1.call-start = ((), (), s32[]{:S(2)}) async-start(), calls=%async_computation.31 | async-start | bytes 4423680 | tf_op jit(solution)/shard_map/reduce_scatter | solution.py:293
  753.6 145.8 %reduce-scatter.38.cloned.1.call-start = ((), (), s32[]{:S(2)}) async-start(), calls=%async_computation.32 | async-start | bytes 4423680 | tf_op jit(solution)/shard_map/reduce_scatter | solution.py:299
  754.2 241.6 %all-reduce.4.cloned.1.call-start = ((), (), s32[]{:S(2)}) async-start(), calls=%async_computation.29 | async-start | bytes 1572864 | tf_op jit(solution)/shard_map/psum | solution.py:275
  760.1 259.9 %reduce-scatter.32.cloned.1.call-start = ((), (), s32[]{:S(2)}) async-start(), calls=%async_computation.28 | async-start | bytes 737280 | tf_op jit(solution)/shard_map/reduce_scatter | solution.py:281
  762.1 295.5 %reduce-scatter.30.cloned.1.call-start = ((), (), s32[]{:S(2)}) async-start(), calls=%async_computation.27 | async-start | bytes 1966080 | tf_op jit(solution)/shard_map/reduce_scatter | solution.py:64
  766.5 327.7 %reduce-scatter.22.cloned.1.call-start = ((), (), s32[]{:S(2)}) async-start(), calls=%async_computation.19 | async-start | bytes 1966080 | tf_op jit(solution)/shard_map/reduce_scatter | solution.py:64
  859.0 198.6 %copy-start.21 = (f32[768]{0:T(1024)S(1)}, f32[768]{0:T(1024)}, u32[]{:S(2)}) copy-start(f32[768]{0:T(1024)} %param.15) | copy-start | bytes 9220
  (24 other events, 78.7 us)
Sparse Core Ops, SparseCore 0:
  18.4 38.8 all-gather.7
  61.6 22.1 reduce-scatter.15
  132.0 35.4 reduce-scatter.17
  175.9 35.8 all-gather.9
  213.3 35.8 all-gather.13
  251.4 106.6 reduce-scatter.19
  360.4 58.6 reduce-scatter.23
  428.2 115.0 all-gather.15
  556.5 35.4 reduce-scatter.25
  601.0 35.8 all-gather.17
  640.5 16.3 reduce-scatter.27
  658.3 61.1 all-gather.11
  721.6 24.2 all-gather.19
  748.3 40.3 reduce-scatter.39
  791.7 22.0 reduce-scatter.33
  816.2 40.3 reduce-scatter.35
  859.0 40.3 reduce-scatter.37
  903.2 92.5 all-reduce.3
  998.9 21.0 reduce-scatter.31
  1022.1 35.4 reduce-scatter.29
  1059.9 34.2 reduce-scatter.21
where the time goes:
time: 1150 us; the launch traced here: 1140 us
  waiting for transfers between devices  838 us (73%)
  matrix products  91.4 us (8%)
  blocking collectives  69.8 us (6%)
  local copies, waits for them, and re-layouts  63.2 us (5%)
  other arithmetic  63.2 us (5%)
  between operations  15.7 us (1%)
    reduce_scatter x4, waiting for transfers between devices, row_product(): lax.psum_scatter(jnp.dot(gathered, weight, preferred_element_type=jnp.flo...  188 us
    reduce_scatter x4, waiting for transfers between devices, column_sum(): lax.psum_scatter(partial_value.astype(jnp.bfloat16), 'col', scatter_dimen...  137 us
    all_gather x4, waiting for transfers between devices, column_gather(): return lax.all_gather(values, 'col', axis=0, tiled=True)  126 us
    all_gather x2, waiting for transfers between devices, row_fold(): return accumulate(lax.all_gather(local_part, 'row', axis=0, tiled=True))  115 us
    psum x1, waiting for transfers between devices, per_device(): lax.psum(key_value_gradient.astype(jnp.bfloat16), ('dp', 'col'))  87 us
    all_gather x1, waiting for transfers between devices, row_project(): lax.all_gather(local_part, 'row', axis=0, tiled=True)  46.8 us
    reduce_scatter x1, waiting for transfers between devices, per_device(): lax.psum_scatter(pair_weight_grad[:, :hidden_cols].astype(jnp.bfloat16),...  41.2 us
    reduce_scatter x1, waiting for transfers between devices, per_device(): lax.psum_scatter(pair_weight_grad[:, hidden_cols:].astype(jnp.bfloat16),...  40.3 us
  transfers between devices with their start and end apart: 21, of which 20 were waited for; matrix products, arithmetic and copies ran while one was open for 11% of the time, Pallas kernels for 0%

commit v1 on v0

--- a/solution.py
+++ b/solution.py
@@ -1,6 +1,8 @@
 import jax
 import jax.numpy as jnp
 from jax import lax
+from jax.experimental import pallas as pl
+from jax.experimental.pallas import tpu as pltpu
 from jax.sharding import PartitionSpec as P
 
 MODEL_WIDTH = 1536
@@ -145,7 +147,7 @@
     return (query_grad, key_grad, value_grad)
 
 
-def per_device(
+def general_device(
     block_input,
     position_ids,
     attention_gain,
@@ -322,6 +324,702 @@
     )
 
 
+MESH_ID = pl.DeviceIdType.MESH
+F32 = jnp.float32
+BF16 = jnp.bfloat16
+LINE = 4
+BLOCK = 128
+LOCAL = LINE * BLOCK
+HALF = MODEL_WIDTH // 2
+VMEM_SPEC = pl.BlockSpec(memory_space=pltpu.VMEM)
+ANY_SPEC = pl.BlockSpec(memory_space=pl.ANY)
+PAIR_ROWS = (((0,), (0,)), ((), ()))
+PAIR_COLS = (((1,), (1,)), ((), ()))
+SCALE = HEAD_SIZE ** (-0.5)
+
+
+def line_barrier(me):
+    barrier = pltpu.get_barrier_semaphore()
+
+    @pl.when(me > 0)
+    def _():
+        pl.semaphore_signal(barrier, 1, device_id={"col": me - 1}, device_id_type=MESH_ID)
+
+    @pl.when(me < LINE - 1)
+    def _():
+        pl.semaphore_signal(barrier, 1, device_id={"col": me + 1}, device_id_type=MESH_ID)
+
+    @pl.when((me > 0) & (me < LINE - 1))
+    def _():
+        pl.semaphore_wait(barrier, 2)
+
+    @pl.when((me == 0) | (me == LINE - 1))
+    def _():
+        pl.semaphore_wait(barrier, 1)
+
+
+def block_rows(index):
+    return pl.ds(pl.multiple_of(index * BLOCK, BLOCK), BLOCK)
+
+
+def gather_line(me, all_ref, sends, recv, each):
+    def copy(j, to, sem):
+        rows = all_ref.at[block_rows(j)]
+        return pltpu.make_async_remote_copy(
+            rows, rows, sem, recv.at[j], device_id={"col": to}, device_id_type=MESH_ID
+        )
+
+    def arrived(j):
+        rows = all_ref.at[block_rows(j)]
+        pltpu.make_async_copy(rows, rows, recv.at[j]).wait()
+
+    for s in range(LINE):
+        left, right = me - s, me + s
+
+        @pl.when(left >= 0)
+        def _():
+            if s:
+                arrived(left)
+
+            @pl.when(me < LINE - 1)
+            def _():
+                copy(left, me + 1, sends.at[0, s]).start()
+
+        @pl.when(right < LINE)
+        def _():
+            if s:
+                arrived(right)
+
+            @pl.when(me > 0)
+            def _():
+                copy(right, me - 1, sends.at[1, s]).start()
+
+        @pl.when(left >= 0)
+        def _():
+            each(left)
+
+        if s:
+
+            @pl.when(right < LINE)
+            def _():
+                each(right)
+
+    for s in range(LINE):
+
+        @pl.when((me - s >= 0) & (me < LINE - 1))
+        def _():
+            copy(me, me + 1, sends.at[0, s]).wait_send()
+
+        @pl.when((me + s < LINE) & (me > 0))
+        def _():
+            copy(me, me - 1, sends.at[1, s]).wait_send()
+
+
+def scatter_line(me, block_of, out_ref, from_left, from_right, going, sends, recv):
+    def copy(j, to, side, landing):
+        return pltpu.make_async_remote_copy(
+            going.at[j],
+            landing.at[j],
+            sends.at[side, j],
+            recv.at[side, j],
+            device_id={"col": to},
+            device_id_type=MESH_ID,
+        )
+
+    def arrived(j, side, landing):
+        pltpu.make_async_copy(landing.at[j], landing.at[j], recv.at[side, j]).wait()
+
+    for s in range(LINE - 1, 0, -1):
+        ahead, behind = me + s, me - s
+
+        @pl.when(ahead < LINE)
+        def _():
+            mine = block_of(ahead)
+
+            @pl.when(me > 0)
+            def _():
+                arrived(ahead, 0, from_left)
+                going[ahead] = (mine + from_left[ahead].astype(F32)).astype(BF16)
+
+            @pl.when(me == 0)
+            def _():
+                going[ahead] = mine.astype(BF16)
+
+            copy(ahead, me + 1, 0, from_left).start()
+
+        @pl.when(behind >= 0)
+        def _():
+            mine = block_of(behind)
+
+            @pl.when(me < LINE - 1)
+            def _():
+                arrived(behind, 1, from_right)
+                going[behind] = (mine + from_right[behind].astype(F32)).astype(BF16)
+
+            @pl.when(me == LINE - 1)
+            def _():
+                going[behind] = mine.astype(BF16)
+
+            copy(behind, me - 1, 1, from_right).start()
+
+    out_ref[...] = block_of(me)
+
+    @pl.when(me > 0)
+    def _():
+        arrived(me, 0, from_left)
+        out_ref[...] += from_left[me].astype(F32)
+
+    @pl.when(me < LINE - 1)
+    def _():
+        arrived(me, 1, from_right)
+        out_ref[...] += from_right[me].astype(F32)
+
+    for s in range(1, LINE):
+
+        @pl.when(me + s < LINE)
+        def _():
+            copy(me + s, me + 1, 0, from_left).wait_send()
+
+        @pl.when(me - s >= 0)
+        def _():
+            copy(me - s, me - 1, 1, from_right).wait_send()
+
+
+def dot(a, b, dims=(((1,), (0,)), ((), ()))):
+    return lax.dot_general(a, b, dims, preferred_element_type=F32)
+
+
+def turn(values):
+    return pltpu.roll(values, HEAD_SIZE // 2, 1)
+
+
+def norm_scale(values):
+    return lax.rsqrt(jnp.sum(values * values, -1, keepdims=True) / MODEL_WIDTH + EPS)
+
+
+def comm_call(body, outs, n_in, scratch, collective_id, flops, name):
+    return pl.pallas_call(
+        body,
+        out_shape=outs,
+        in_specs=[VMEM_SPEC] * n_in,
+        out_specs=[VMEM_SPEC] * len(outs),
+        scratch_shapes=scratch,
+        compiler_params=pltpu.CompilerParams(collective_id=collective_id, has_side_effects=True),
+        cost_estimate=pl.CostEstimate(flops=flops, bytes_accessed=40_000_000, transcendentals=0),
+        name=name,
+    )
+
+
+def gather_scratch():
+    return [pltpu.SemaphoreType.DMA((2, LINE)), pltpu.SemaphoreType.DMA((LINE,))]
+
+
+def scatter_scratch(width=MODEL_WIDTH):
+    return [pltpu.VMEM((LINE, BLOCK, width), BF16)] * 3 + [pltpu.SemaphoreType.DMA((2, LINE))] * 2
+
+
+def project_body(
+    x_ref, gain_ref, own_ref, other_ref, bias_ref, cos_ref, sin_ref, all_ref, query_ref, kv_ref, sends, recv
+):
+    me = lax.axis_index("col")
+    line_barrier(me)
+    x = x_ref[...].astype(F32)
+    all_ref[block_rows(me)] = (x * norm_scale(x) * gain_ref[...]).astype(BF16)
+    query_cols = query_ref.shape[1]
+
+    def each(j):
+        rows = block_rows(j)
+        block = all_ref[rows]
+        out = dot(block[:, :HALF], own_ref[...]) + dot(block[:, HALF:], other_ref[...])
+        out = out + bias_ref[...]
+        cosine, sine = cos_ref[rows], sin_ref[rows]
+        for h in range(query_cols // HEAD_SIZE + 1):
+            head = out[:, h * HEAD_SIZE : (h + 1) * HEAD_SIZE]
+            turned = (head * cosine + turn(head) * sine).astype(BF16)
+            if h * HEAD_SIZE < query_cols:
+                query_ref[rows, h * HEAD_SIZE : (h + 1) * HEAD_SIZE] = turned
+            else:
+                kv_ref[rows, :HEAD_SIZE] = turned
+        kv_ref[rows, HEAD_SIZE:] = out[:, query_cols + HEAD_SIZE :].astype(BF16)
+
+    gather_line(me, all_ref, sends, recv, each)
+
+
+def attend_body(query_ref, own_ref, other_ref, attended_ref, probs_ref):
+    r = lax.axis_index("row")
+    rows = 2 * BLOCK
+    shape = (rows, rows)
+    at_row = lax.broadcasted_iota(jnp.int32, shape, 0)
+    at_col = lax.broadcasted_iota(jnp.int32, shape, 1)
+    own_mask = at_row >= at_col
+    other_mask = at_col // BLOCK < at_row // BLOCK + r
+    heads = query_ref.shape[1] // HEAD_SIZE
+    for s in range(2):
+        part = slice(s * rows, (s + 1) * rows)
+        for h in range(heads):
+            cols = slice(h * HEAD_SIZE, (h + 1) * HEAD_SIZE)
+            query = query_ref[part, cols]
+            own = jnp.where(own_mask, dot(query, own_ref[part, :HEAD_SIZE], PAIR_COLS) * SCALE, NEG)
+            other = jnp.where(
+                other_mask, dot(query, other_ref[part, :HEAD_SIZE], PAIR_COLS) * SCALE, NEG
+            )
+            top = jnp.maximum(
+                jnp.max(own, -1, keepdims=True), jnp.max(other, -1, keepdims=True)
+            )
+            total = jnp.sum(jnp.exp(own - top), -1, keepdims=True) + jnp.sum(
+                jnp.exp(other - top), -1, keepdims=True
+            )
+            log_total = top + jnp.log(total)
+            own = jnp.exp(own - log_total).astype(BF16)
+            other = jnp.exp(other - log_total).astype(BF16)
+            attended_ref[part, cols] = (
+                dot(own, own_ref[part, HEAD_SIZE:]) + dot(other, other_ref[part, HEAD_SIZE:])
+            ).astype(BF16)
+            probs_ref[s * heads + h, :, :rows] = own
+            probs_ref[s * heads + h, :, rows:] = other
+
+
+def attend_back_body(
+    query_ref, own_ref, other_ref, attended_ref, probs_ref, grad_ref, cos_ref, sin_ref,
+    query_grad_ref, own_grad_ref, other_grad_ref,
+):
+    rows = 2 * BLOCK
+    heads = query_ref.shape[1] // HEAD_SIZE
+    for s in range(2):
+        part = slice(s * rows, (s + 1) * rows)
+        own_key, other_key = own_ref[part, :HEAD_SIZE], other_ref[part, :HEAD_SIZE]
+        own_value, other_value = own_ref[part, HEAD_SIZE:], other_ref[part, HEAD_SIZE:]
+        sums = [jnp.zeros((rows, HEAD_SIZE), F32) for _ in range(4)]
+        for h in range(heads):
+            cols = slice(h * HEAD_SIZE, (h + 1) * HEAD_SIZE)
+            query, grad = query_ref[part, cols], grad_ref[part, cols]
+            own_p = probs_ref[s * heads + h, :, :rows]
+            other_p = probs_ref[s * heads + h, :, rows:]
+            delta = jnp.sum(
+                grad.astype(F32) * attended_ref[part, cols].astype(F32), -1, keepdims=True
+            )
+            own_s = (own_p.astype(F32) * (dot(grad, own_value, PAIR_COLS) - delta)).astype(BF16)
+            other_s = (other_p.astype(F32) * (dot(grad, other_value, PAIR_COLS) - delta)).astype(BF16)
+            query_grad = (dot(own_s, own_key) + dot(other_s, other_key)) * SCALE
+            query_grad_ref[part, cols] = (
+                query_grad * cos_ref[part] - turn(query_grad) * sin_ref[part]
+            ).astype(BF16)
+            for i, (weights, partner) in enumerate(
+                ((own_s, query), (own_p, grad), (other_s, query), (other_p, grad))
+            ):
+                sums[i] = sums[i] + dot(weights, partner, PAIR_ROWS)
+        own_grad_ref[part, :HEAD_SIZE] = sums[0] * SCALE
+        own_grad_ref[part, HEAD_SIZE:] = sums[1]
+        other_grad_ref[part, :HEAD_SIZE] = (sums[2] * SCALE).astype(BF16)
+        other_grad_ref[part, HEAD_SIZE:] = sums[3].astype(BF16)
+
+
+def residual_body(
+    attended_ref, own_ref, other_ref, x_ref, gain_ref, mid_ref, all_ref,
+    from_left, from_right, going, s_sends, s_recv, sends, recv,
+):
+    me = lax.axis_index("col")
+    line_barrier(me)
+
+    def block_of(j):
+        block = attended_ref[block_rows(j)]
+        return jnp.concatenate(
+            [dot(block, own_ref[...], PAIR_COLS), dot(block, other_ref[...], PAIR_COLS)], 1
+        )
+
+    scatter_line(me, block_of, mid_ref, from_left, from_right, going, s_sends, s_recv)
+    mid = mid_ref[...] + x_ref[...].astype(F32)
+    mid_ref[...] = mid
+    all_ref[block_rows(me)] = (mid * norm_scale(mid) * gain_ref[...]).astype(BF16)
+    gather_line(me, all_ref, sends, recv, lambda j: None)
+
+
+def middle_back_body(
+    part_ref, mid_ref, cot_ref, gain_ref, own_ref, other_ref,
+    mid_grad_ref, gain_grad_ref, all_ref, att_grad_ref,
+    from_left, from_right, going, s_sends, s_recv, sends, recv,
+):
+    me = lax.axis_index("col")
+    line_barrier(me)
+    scatter_line(
+        me, lambda j: part_ref[block_rows(j)].astype(F32), mid_grad_ref,
+        from_left, from_right, going, s_sends, s_recv,
+    )
+    mid, grad = mid_ref[...], mid_grad_ref[...]
+    rinv = norm_scale(mid)
+    gain_grad_ref[...] = jnp.sum(grad * mid * rinv, 0, keepdims=True)
+    scaled = grad * gain_ref[...]
+    inner = jnp.sum(scaled * mid, -1, keepdims=True)
+    mid_grad = cot_ref[...].astype(F32) + rinv * scaled - mid * rinv**3 * inner / MODEL_WIDTH
+    mid_grad_ref[...] = mid_grad
+    all_ref[block_rows(me)] = mid_grad.astype(BF16)
+
+    def each(j):
+        block = all_ref[block_rows(j)]
+        att_grad_ref[block_rows(j)] = (
+            dot(block[:, :HALF], own_ref[...]) + dot(block[:, HALF:], other_ref[...])
+        ).astype(BF16)
+
+    gather_line(me, all_ref, sends, recv, each)
+
+
+def input_back_body(
+    query_grad_ref, own_kv_ref, got_kv_ref, cos_ref, sin_ref, own_ref, other_ref, x_ref, gain_ref,
+    mid_grad_ref, proj_grad_ref, bias_ref, input_grad_ref, gain_grad_ref,
+    from_left, from_right, going, s_sends, s_recv,
+):
+    me = lax.axis_index("col")
+    line_barrier(me)
+    query_cols = query_grad_ref.shape[1]
+    kv = own_kv_ref[...] + got_kv_ref[...].astype(F32)
+    key = kv[:, :HEAD_SIZE]
+    proj_grad_ref[:, :query_cols] = query_grad_ref[...]
+    proj_grad_ref[:, query_cols : query_cols + HEAD_SIZE] = (
+        key * cos_ref[...] - turn(key) * sin_ref[...]
+    ).astype(BF16)
+    proj_grad_ref[:, query_cols + HEAD_SIZE :] = kv[:, HEAD_SIZE:].astype(BF16)
+
+    def block_of(j):
+        block = proj_grad_ref[block_rows(j)]
+        return jnp.concatenate(
+            [dot(block, own_ref[...], PAIR_COLS), dot(block, other_ref[...], PAIR_COLS)], 1
+        )
+
+    scatter_line(me, block_of, input_grad_ref, from_left, from_right, going, s_sends, s_recv)
+    bias_ref[...] = jnp.sum(proj_grad_ref[...].astype(F32), 0, keepdims=True)
+    x, grad = x_ref[...].astype(F32), input_grad_ref[...]
+    rinv = norm_scale(x)
+    gain_grad_ref[...] = jnp.sum(grad * x * rinv, 0, keepdims=True)
+    scaled = grad * gain_ref[...]
+    inner = jnp.sum(scaled * x, -1, keepdims=True)
+    input_grad_ref[...] = mid_grad_ref[...] + rinv * scaled - x * rinv**3 * inner / MODEL_WIDTH
+
+
+def feed_body(
+    normed_ref, cot_ref, gate_hbm, upper_hbm, down_hbm, other_hbm, partner_hbm,
+    activated_ref, gate_grad_ref, upper_grad_ref, back_ref, out_ref,
+    weights, back_sum, out_sum, sems,
+):
+    core = lax.rem(lax.axis_index("dp"), 2)
+    hidden = activated_ref.shape[1]
+    quarter = HALF // 2
+    here = pl.ds(pl.multiple_of(HALF + core * quarter, quarter), quarter)
+    there = pl.ds(pl.multiple_of(HALF + (1 - core) * quarter, quarter), quarter)
+    copies = []
+    for i, own in enumerate((gate_hbm, upper_hbm, down_hbm)):
+        copies.append(pltpu.make_async_copy(own, weights.at[i, pl.ds(0, HALF)], sems.at[i, 0]))
+        copies.append(pltpu.make_async_copy(other_hbm.at[i], weights.at[i, here], sems.at[i, 1]))
+        copies.append(pltpu.make_async_copy(partner_hbm.at[i], weights.at[i, there], sems.at[i, 2]))
+    for copy in copies:
+        copy.start()
+    for copy in copies:
+        copy.wait()
+    tile = 256
+    for i, low in enumerate(range(0, hidden, tile)):
+        cols = slice(low, min(low + tile, hidden))
+        gate_w, upper_w, down_w = weights[0, :, cols], weights[1, :, cols], weights[2, :, cols]
+        gate = dot(normed_ref[...], gate_w)
+        upper = dot(normed_ref[...], upper_w)
+        act_grad = dot(cot_ref[...], down_w)
+        sig = jax.nn.sigmoid(gate)
+        silu = gate * sig
+        activated = (silu * upper).astype(BF16)
+        gate_grad = (act_grad * upper * sig * (1.0 + gate * (1.0 - sig))).astype(BF16)
+        upper_grad = (act_grad * silu).astype(BF16)
+        activated_ref[:, cols] = activated
+        gate_grad_ref[:, cols] = gate_grad
+        upper_grad_ref[:, cols] = upper_grad
+        back = dot(gate_grad, gate_w, PAIR_COLS) + dot(upper_grad, upper_w, PAIR_COLS)
+        out = dot(activated, down_w, PAIR_COLS)
+        if i == 0:
+            back_sum[...] = back
+            out_sum[...] = out
+        else:
+            back_sum[...] += back
+            out_sum[...] += out
+    back_ref[...] = back_sum[...].astype(BF16)
+    out_ref[...] = out_sum[...].astype(BF16)
+
+
+def shape(rows, cols, dtype=BF16):
+    return jax.ShapeDtypeStruct((rows, cols), dtype)
+
+
+def swap(values, axis, bit):
+    size = lax.axis_size(axis)
+    return lax.ppermute(values, axis, [(i, i ^ bit) for i in range(size)])
+
+
+def reduce_blocks(grad, x_first):
+    y, core = lax.axis_index("dp") // 2, lax.axis_index("dp") % 2
+    width = grad.shape[1]
+    parts = grad.reshape(2, 2, 2, MODEL_WIDTH // 8, width)
+    pick = lambda index: lax.dynamic_index_in_dim(parts, index, 2, keepdims=False)
+    part = pick(core).astype(F32) + swap(pick(1 - core), "dp", 1).astype(F32)
+    part = part.astype(BF16)
+    choose = lambda index: lax.dynamic_index_in_dim(part, index, 1, keepdims=False)
+    if x_first:
+        half = (part[0].astype(F32) + swap(part[1], "row", 1).astype(F32)).astype(BF16)
+        choose = lambda index: lax.dynamic_index_in_dim(half, index, 0, keepdims=False)
+        return choose(y).astype(F32) + swap(choose(1 - y), "dp", 2).astype(F32)
+    half = (choose(y).astype(F32) + swap(choose(1 - y), "dp", 2).astype(F32)).astype(BF16)
+    return half[0].astype(F32) + swap(half[1], "row", 1).astype(F32)
+
+
+def fast_device(
+    block_input,
+    position_ids,
+    attention_gain,
+    query_weight,
+    query_bias,
+    key_value_weight,
+    key_value_bias,
+    output_weight,
+    feedforward_gain,
+    gate_weight,
+    upper_weight,
+    down_weight,
+    out_cotangent,
+):
+    r, c = lax.axis_index("row"), lax.axis_index("col")
+    core = lax.axis_index("dp") % 2
+    query_cols = query_weight.shape[1]
+    hidden = gate_weight.shape[1]
+    proj_cols = query_cols + 2 * HEAD_SIZE
+    quarter = HALF // 2
+    kv_head = c // (LINE // KEYVALUE_HEADS)
+    key_start = kv_head * HEAD_SIZE
+    value_start = (KEYVALUE_HEADS + kv_head) * HEAD_SIZE
+
+    def mine(values):
+        keep = lax.dynamic_slice_in_dim(values, r * BLOCK, BLOCK, 1).T
+        send = lax.dynamic_slice_in_dim(values, (1 - r) * BLOCK, BLOCK, 1).T
+        return jnp.concatenate([keep, swap(send, "row", 1)], 1)
+
+    x_own = mine(block_input)
+    small = jnp.concatenate([attention_gain, feedforward_gain, position_ids.astype(F32)])
+    got_small = swap(small, "row", 1)
+    attn_gain = jnp.concatenate([attention_gain, got_small[:HALF]])[None]
+    ffn_gain = jnp.concatenate([feedforward_gain, got_small[HALF : 2 * HALF]])[None]
+    own_ids, other_ids = small[2 * HALF :], got_small[2 * HALF :]
+    ids = jnp.stack([jnp.where(r == 0, own_ids, other_ids), jnp.where(r == 0, other_ids, own_ids)])
+    ids = lax.dynamic_index_in_dim(ids.reshape(2, 2, 2, BLOCK), r, 2, keepdims=False).reshape(LOCAL)
+    frequencies = THETA ** (-(jnp.arange(HEAD_SIZE // 2, dtype=F32) * 2.0 / HEAD_SIZE))
+    angles = ids[:, None] * frequencies[None, :]
+    cosine, sine = jnp.cos(angles), jnp.sin(angles)
+    cosine = jnp.concatenate([cosine, cosine], -1)
+    sine = jnp.concatenate([-sine, sine], -1)
+
+    own_proj = jnp.concatenate(
+        [
+            query_weight,
+            lax.dynamic_slice_in_dim(key_value_weight, key_start, HEAD_SIZE, 1),
+            lax.dynamic_slice_in_dim(key_value_weight, value_start, HEAD_SIZE, 1),
+            output_weight,
+        ],
+        1,
+    )
+    proj_bias = jnp.concatenate(
+        [
+            query_bias,
+            lax.dynamic_slice_in_dim(key_value_bias, key_start, HEAD_SIZE, 0),
+            lax.dynamic_slice_in_dim(key_value_bias, value_start, HEAD_SIZE, 0),
+        ]
+    )[None]
+    here = swap(lax.dynamic_slice_in_dim(own_proj, core * quarter, quarter, 0), "row", 1)
+    there = swap(here, "dp", 1)
+    other_proj = jnp.where(
+        core == 0, jnp.concatenate([here, there]), jnp.concatenate([there, here])
+    )
+    own_in, own_out = own_proj[:, :proj_cols], own_proj[:, proj_cols:]
+    other_in, other_out = other_proj[:, :proj_cols], other_proj[:, proj_cols:]
+
+    ffn_send = jnp.stack(
+        [
+            lax.dynamic_slice_in_dim(w, core * quarter, quarter, 0)
+            for w in (gate_weight, upper_weight, down_weight)
+        ]
+    )
+    ffn_other = swap(ffn_send, "row", 1)
+    ffn_partner = swap(ffn_other, "dp", 1)
+
+    normed_one, query_rot, kv_own = comm_call(
+        project_body,
+        [shape(LOCAL, MODEL_WIDTH), shape(LOCAL, query_cols), shape(LOCAL, 2 * HEAD_SIZE)],
+        7,
+        gather_scratch(),
+        1,
+        10**9,
+        "project",
+    )(x_own, attn_gain, own_in, other_in, proj_bias, cosine, sine)
+    kv_other = swap(kv_own, "row", 1)
+    heads = query_cols // HEAD_SIZE
+    attended, probs = pl.pallas_call(
+        attend_body,
+        out_shape=[
+            shape(LOCAL, query_cols),
+            jax.ShapeDtypeStruct((2 * heads, 2 * BLOCK, 4 * BLOCK), BF16),
+        ],
+        in_specs=[VMEM_SPEC] * 3,
+        out_specs=[VMEM_SPEC] * 2,
+        cost_estimate=pl.CostEstimate(flops=10**9, bytes_accessed=20_000_000, transcendentals=0),
+        name="attend",
+    )(query_rot, kv_own, kv_other)
+    cot_own = mine(out_cotangent)
+    cot_all = lax.all_gather(cot_own, "col", axis=0, tiled=True)
+    mid, normed_two = comm_call(
+        residual_body,
+        [shape(BLOCK, MODEL_WIDTH, F32), shape(LOCAL, MODEL_WIDTH)],
+        5,
+        scatter_scratch() + gather_scratch(),
+        2,
+        10**9,
+        "residual",
+    )(attended, own_out, other_out, x_own, ffn_gain)
+    activated, gate_grad, upper_grad, back_part, out_part = pl.pallas_call(
+        feed_body,
+        out_shape=[shape(LOCAL, hidden)] * 3 + [shape(LOCAL, MODEL_WIDTH)] * 2,
+        in_specs=[VMEM_SPEC] * 2 + [ANY_SPEC] * 5,
+        out_specs=[VMEM_SPEC] * 5,
+        scratch_shapes=[
+            pltpu.VMEM((3, MODEL_WIDTH, hidden), BF16),
+            pltpu.VMEM((LOCAL, MODEL_WIDTH), F32),
+            pltpu.VMEM((LOCAL, MODEL_WIDTH), F32),
+            pltpu.SemaphoreType.DMA((3, 3)),
+        ],
+        cost_estimate=pl.CostEstimate(
+            flops=2 * 10**10, bytes_accessed=40_000_000, transcendentals=0
+        ),
+        name="feed",
+    )(normed_two, cot_all, gate_weight, upper_weight, down_weight, ffn_other, ffn_partner)
+    out_own = lax.psum_scatter(out_part, "col", scatter_dimension=0, tiled=True).astype(F32) + mid
+    down_grad = lax.dot_general(cot_all, activated, PAIR_ROWS, preferred_element_type=F32).astype(
+        BF16
+    )
+    gate_w_grad = lax.dot_general(
+        normed_two, gate_grad, PAIR_ROWS, preferred_element_type=F32
+    ).astype(BF16)
+    upper_w_grad = lax.dot_general(
+        normed_two, upper_grad, PAIR_ROWS, preferred_element_type=F32
+    ).astype(BF16)
+    mid_grad, ffn_gain_part, mid_half, att_grad = comm_call(
+        middle_back_body,
+        [
+            shape(BLOCK, MODEL_WIDTH, F32),
+            shape(1, MODEL_WIDTH, F32),
+            shape(LOCAL, MODEL_WIDTH),
+            shape(LOCAL, query_cols),
+        ],
+        6,
+        scatter_scratch() + gather_scratch(),
+        3,
+        10**9,
+        "middle_back",
+    )(back_part, mid, cot_own, ffn_gain, own_out, other_out)
+    query_grad, kv_grad_own, kv_grad_other = pl.pallas_call(
+        attend_back_body,
+        out_shape=[
+            shape(LOCAL, query_cols),
+            shape(LOCAL, 2 * HEAD_SIZE, F32),
+            shape(LOCAL, 2 * HEAD_SIZE),
+        ],
+        in_specs=[VMEM_SPEC] * 8,
+        out_specs=[VMEM_SPEC] * 3,
+        cost_estimate=pl.CostEstimate(flops=10**9, bytes_accessed=20_000_000, transcendentals=0),
+        name="attend_back",
+    )(query_rot, kv_own, kv_other, attended, probs, att_grad, cosine, sine)
+    kv_grad_got = swap(kv_grad_other, "row", 1)
+    output_w_grad = lax.dot_general(
+        mid_half, attended, PAIR_ROWS, preferred_element_type=F32
+    ).astype(BF16)
+    proj_grad, bias_part, input_grad, attn_gain_part = comm_call(
+        input_back_body,
+        [
+            shape(LOCAL, proj_cols),
+            shape(1, proj_cols, F32),
+            shape(BLOCK, MODEL_WIDTH, F32),
+            shape(1, MODEL_WIDTH, F32),
+        ],
+        10,
+        scatter_scratch(),
+        4,
+        10**9,
+        "input_back",
+    )(
+        query_grad, kv_grad_own, kv_grad_got, cosine, sine, own_in, other_in, x_own, attn_gain,
+        mid_grad,
+    )
+    proj_w_grad = lax.dot_general(
+        normed_one, proj_grad, PAIR_ROWS, preferred_element_type=F32
+    ).astype(BF16)
+
+    down_sum = reduce_blocks(down_grad, True)
+    gate_sum = reduce_blocks(gate_w_grad, False)
+    upper_sum = reduce_blocks(upper_w_grad, True)
+    output_sum = reduce_blocks(output_w_grad, False)
+    proj_sum = reduce_blocks(proj_w_grad, True)
+
+    kv_sum = lax.all_gather(proj_sum[:, query_cols:].astype(BF16), "col", axis=0, tiled=False)
+    group = LINE // KEYVALUE_HEADS
+    kv_sum = kv_sum.reshape(KEYVALUE_HEADS, group, -1, 2, HEAD_SIZE).astype(F32).sum(1)
+    kv_sum = jnp.transpose(kv_sum, (1, 2, 0, 3)).reshape(-1, 2 * KEYVALUE_HEADS * HEAD_SIZE)
+    kv_weight_grad = lax.all_gather(kv_sum.astype(BF16), "dp", axis=0, tiled=True).astype(F32)
+
+    swapped = lambda v: jnp.where(r == 0, v, jnp.roll(v, HALF))
+    spread = jnp.zeros((2 * KEYVALUE_HEADS * HEAD_SIZE,), F32)
+    spread = lax.dynamic_update_slice(
+        spread, bias_part[0, query_cols : query_cols + HEAD_SIZE], (key_start,)
+    )
+    spread = lax.dynamic_update_slice(spread, bias_part[0, query_cols + HEAD_SIZE :], (value_start,))
+    query_spread = lax.dynamic_update_slice(
+        jnp.zeros((LINE * query_cols,), F32), bias_part[0, :query_cols], (c * query_cols,)
+    )
+    vector = jnp.concatenate(
+        [swapped(attn_gain_part[0]), swapped(ffn_gain_part[0]), spread, query_spread]
+    )
+    vector = lax.psum(vector, ("dp", "row", "col"))
+    attn_gain_grad = lax.dynamic_slice_in_dim(vector, r * HALF, HALF, 0)
+    ffn_gain_grad = lax.dynamic_slice_in_dim(vector, MODEL_WIDTH + r * HALF, HALF, 0)
+    kv_bias_grad = vector[2 * MODEL_WIDTH : 2 * MODEL_WIDTH + spread.shape[0]]
+    bias_rows = query_cols // lax.axis_size("dp")
+    query_bias_grad = lax.dynamic_slice_in_dim(
+        vector,
+        2 * MODEL_WIDTH + spread.shape[0] + c * query_cols + lax.axis_index("dp") * bias_rows,
+        bias_rows,
+        0,
+    )
+
+    def returned(values):
+        got = swap(values[:, HALF:].astype(BF16), "row", 1).astype(F32)
+        keep = values[:, :HALF]
+        pair = jnp.where(
+            r == 0, jnp.concatenate([keep, got]), jnp.concatenate([got, keep])
+        )
+        return pair.T
+
+    return (
+        returned(out_own),
+        returned(input_grad),
+        attn_gain_grad,
+        proj_sum[:, :query_cols],
+        query_bias_grad,
+        kv_weight_grad,
+        kv_bias_grad,
+        output_sum,
+        ffn_gain_grad,
+        gate_sum,
+        upper_sum,
+        down_sum,
+    )
+
+
+def per_device(*arrays):
+    sizes = tuple(lax.axis_size(axis) for axis in ("dp", "row", "col"))
+    if sizes == (4, 2, LINE) and arrays[0].shape == (HALF, 2 * BLOCK):
+        return fast_device(*arrays)
+    return general_device(*arrays)
+
+
 def solution(mesh):
     placed = (
         P("row", ("dp", "col")),

time: 1150 us -> 763 us (0.66)
  waiting for transfers between devices: 838 us -> 227 us
  Pallas kernels: 0 us -> 262 us
  matrix products: 91.4 us -> 21.5 us
  local copies, waits for them, and re-layouts: 63.2 us -> 105 us
  other arithmetic: 63.2 us -> 35.2 us
  starting transfers between devices: 1.97 us -> 23.5 us
    reduce_scatter x12 -> x1, waiting for transfers between devices: 448 us -> 0.02 us  [fast_device(): lax.psum_scatter(out_part, 'col', scatter_dimension=0, tiled=True)]
    all_gather x7 -> x1, waiting for transfers between devices: 288 us -> 0.02 us  [fast_device(): cot_all = lax.all_gather(cot_own, 'col', axis=0, tiled=True)]
    pallas_call x0 -> x7, Pallas kernels: none -> 262 us  [the longest x1 80.1 us: fast_device(): comm_call(middle_back_body, [shape(BLOCK, MODEL_WIDTH, F32), shape(1, MOD...]
    ppermute x0 -> x26, waiting for transfers between devices: none -> 227 us  [swap(): return lax.ppermute(values, axis, [(i, i ^ bit) for i in range(size)])]
    psum x1 -> x0, waiting for transfers between devices: 87 us -> none  [per_device(): lax.psum(key_value_gradient.astype(jnp.bfloat16), ('dp', 'col'))]
    dot_general x18 -> x5, matrix products: 91.4 us -> 21.5 us  [the longest x1 5.86 us: fast_device(): lax.dot_general(cot_all, activated, PAIR_ROWS, preferred_element_type=F32)]
    convert_element_type x2 -> x6, local copies, waits for them, and re-layouts: 3.61 us -> 29.6 us  [the longest x1 9.77 us: fast_device(): gate_w_grad = lax.dot_general(normed_two, gate_grad, PAIR_ROWS, preferred...]
    ppermute x0 -> x26, starting transfers between devices: none -> 23.5 us  [swap(): return lax.ppermute(values, axis, [(i, i ^ bit) for i in range(size)])]
  transfers between devices with their start and end apart: 21 -> 28, of which waited for: 20 -> 11; matrix products, arithmetic and copies ran while one was open for 11% -> 20% of each run, Pallas kernels for 0% -> 30%
where the time goes in v1:
time: 763 us; the launch traced here: 753 us
  Pallas kernels  262 us (34%)
  waiting for transfers between devices  227 us (30%)
  local copies, waits for them, and re-layouts  105 us (14%)
  blocking collectives  63.2 us (8%)
  other arithmetic  35.2 us (5%)
  starting transfers between devices  23.5 us (3%)
  matrix products  21.5 us (3%)
  between operations  14.9 us (2%)
    ppermute x26, waiting for transfers between devices, swap(): return lax.ppermute(values, axis, [(i, i ^ bit) for i in range(size)])  227 us
    pallas_call x1, Pallas kernels, fast_device(): comm_call(middle_back_body, [shape(BLOCK, MODEL_WIDTH, F32), shape(1, MOD...  80.1 us
    pallas_call x1, Pallas kernels, fast_device(): comm_call(residual_body, [shape(BLOCK, MODEL_WIDTH, F32), shape(LOCAL, MO...  55.8 us
    pallas_call x1, Pallas kernels, fast_device(): comm_call(project_body, [shape(LOCAL, MODEL_WIDTH), shape(LOCAL, query_co...  45.5 us
    psum x1, blocking collectives, fast_device(): vector = lax.psum(vector, ('dp', 'row', 'col'))  39.4 us
    pallas_call x1, Pallas kernels, fast_device(): pl.pallas_call(feed_body, out_shape=[shape(LOCAL, hidden)] * 3 + [shape(L...  35.1 us
    pallas_call x1, Pallas kernels, fast_device(): comm_call(input_back_body, [shape(LOCAL, proj_cols), shape(1, proj_cols,...  35.1 us
    ppermute x26, starting transfers between devices, swap(): return lax.ppermute(values, axis, [(i, i ^ bit) for i in range(size)])  23.5 us
  transfers between devices with their start and end apart: 28, of which 11 were waited for; matrix products, arithmetic and copies ran while one was open for 20% of the time, Pallas kernels for 30%

profile of v1, /device:TPU:0, one launch (start us, length us, event | category | flops | bytes accessed | tf_op | source)
XLA Modules:
  0.0 752.7 jit_solution(15501847271102990626)
XLA Ops:
  15.6 111.4 %collective-permute-done.6 = bf16[3,384,2240]{1,2,0:T(8,128)(2,1)} collective-permute-done((bf16[3,384,2240]{1,2,0:T(8,128)(2,1)S(1)}, bf16[3,384,2240]{1,2,0:T(8,128)(2,1)}, u32[]{:S(2)}, u32[]{:S(2)}) %collective-permute-start.6) | collective-permute-done | bytes 5160992 | tf_op jit(solution)/shard_map/ppermute | solution.py:750
  134.0 6.6 collective-permute-done.5
  147.0 9.8 %collective-permute-done.2 = bf16[384,1024]{1,0:T(8,128)(2,1)S(1)} collective-permute-done((bf16[384,1024]{1,0:T(8,128)(2,1)S(1)}, bf16[384,1024]{1,0:T(8,128)(2,1)S(1)}, u32[]{:S(2)}, u32[]{:S(2)}) %collective-permute-start.2) | collective-permute-done | bytes 786464 | tf_op jit(solution)/shard_map/ppermute | solution.py:750
  164.1 45.5 %project.1 = (bf16[512,1536]{1,0:T(8,128)(2,1)}, bf16[512,384]{1,0:T(8,128)(2,1)}, bf16[512,256]{1,0:T(8,128)(2,1)}) custom-call(bf16[128,1536]{1,0:T(8,128)(2,1)} %pad_maximum_fusion.2.x_ref, f32[1,1536]{1,0:T(1,128)} %broadcast_in_dim.16.gain_ref, bf16[768,640]{1,0:T(8,128)(2,1)} %pad_maximum_fusion.1.own_ref, bf16[768,640]{1,0:T(8,128)(2,1)} %slice.140.other_ref, ...), custom_call_target="tpu_custom_call" | custom-call | flops 1000000000 | bytes 40000000 | tf_op jit(solution)/shard_map/project/pallas_call | solution.py:846
  215.5 5.9 copy.86.upper_hbm
  232.9 55.8 %residual.1 = (f32[128,1536]{1,0:T(8,128)}, bf16[512,1536]{1,0:T(8,128)(2,1)}) custom-call(bf16[512,384]{1,0:T(8,128)(2,1)} %get-tuple-element.37.attended_ref, bf16[768,384]{1,0:T(8,128)(2,1)} %own_ref.3, bf16[768,384]{1,0:T(8,128)(2,1)} %slice.142.other_ref, bf16[128,1536]{1,0:T(8,128)(2,1)} %pad_maximum_fusion.2.x_ref, f32[1,1536]{1,0:T(1,128)} %broadcast_in_dim.18.gain_ref), custom_call_target="tpu_custom_call" | custom-call | flops 1000000000 | bytes 40000000 | tf_op jit(solution)/shard_map/residual/pallas_call | solution.py:870
  288.8 8.5 %copy.88.other_hbm = bf16[3,384,2240]{2,1,0:T(8,128)(2,1)} copy(bf16[3,384,2240]{1,2,0:T(8,128)(2,1)} %collective-permute-done.6) | data formatting | bytes 10321920 | tf_op jit(solution)/shard_map/ppermute | solution.py:750
  297.3 9.0 %copy.89.partner_hbm = bf16[3,384,2240]{2,1,0:T(8,128)(2,1)} copy(bf16[3,384,2240]{1,2,0:T(8,128)(2,1)} %collective-permute-done.7) | data formatting | bytes 10321920 | tf_op jit(solution)/shard_map/ppermute | solution.py:750
  306.3 35.1 %feed.1 = (bf16[512,2240]{1,0:T(8,128)(2,1)}, bf16[512,2240]{1,0:T(8,128)(2,1)}, bf16[512,2240]{1,0:T(8,128)(2,1)}, bf16[512,1536]{1,0:T(8,128)(2,1)}, bf16[512,1536]{1,0:T(8,128)(2,1)}) custom-call(bf16[512,1536]{1,0:T(8,128)(2,1)} %get-tuple-element.38.normed_ref, bf16[512,1536]{1,0:T(8,128)(2,1)} %all-gather.3.cloned.1.call-done.cot_ref, ...), custom_call_target="tpu_custom_call" | custom-call | flops 20000000000 | bytes 40000000 | tf_op jit(solution)/shard_map/feed/pallas_call | solution.py:879
  341.5 80.1 %middle_back.1 = (f32[128,1536]{1,0:T(8,128)}, f32[1,1536]{1,0:T(1,128)}, bf16[512,1536]{1,0:T(8,128)(2,1)}, bf16[512,384]{1,0:T(8,128)(2,1)}) custom-call(bf16[512,1536]{1,0:T(8,128)(2,1)} %get-tuple-element.42.part_ref, f32[128,1536]{1,0:T(8,128)} %get-tuple-element.40.mid_ref, bf16[128,1536]{1,0:T(8,128)(2,1)} %pad_maximum_fusion.3.cot_ref, ...), custom_call_target="tpu_custom_call" | custom-call | flops 1000000000 | bytes 40000000 | tf_op jit(solution)/shard_map/middle_back/pallas_call | solution.py:905
  429.9 5.8 convolution_convert_fusion.2
  435.7 9.8 %copy.94 = bf16[1536,2240]{1,0:T(8,128)(2,1)} copy(bf16[1536,2240]{0,1:T(8,128)(2,1)} %convolution_convert_fusion.2) | data formatting | bytes 13762560 | tf_op jit(solution)/shard_map/convert_element_type | solution.py:901
  449.6 5.8 convolution_convert_fusion.1
  455.4 9.7 %copy.95 = bf16[1536,2240]{1,0:T(8,128)(2,1)} copy(bf16[1536,2240]{0,1:T(8,128)(2,1)} %convolution_convert_fusion.1) | data formatting | bytes 13762560 | tf_op jit(solution)/shard_map/convert_element_type | solution.py:904
  469.8 5.9 convolution_convert_fusion
  475.7 9.6 %copy.96 = bf16[1536,2240]{1,0:T(8,128)(2,1)} copy(bf16[1536,2240]{0,1:T(8,128)(2,1)} %convolution_convert_fusion) | data formatting | bytes 13762560 | tf_op jit(solution)/shard_map/convert_element_type | solution.py:896
  490.2 35.1 %input_back.1 = (bf16[512,640]{1,0:T(8,128)(2,1)}, f32[1,640]{1,0:T(1,128)}, f32[128,1536]{1,0:T(8,128)}, f32[1,1536]{1,0:T(1,128)}) custom-call(bf16[512,384]{1,0:T(8,128)(2,1)} %get-tuple-element.44.query_grad_ref, f32[512,256]{1,0:T(8,128)} %get-tuple-element.45.own_kv_ref, bf16[512,256]{1,0:T(8,128)(2,1)} %copy-done.11, ...), custom_call_target="tpu_custom_call" | custom-call | flops 1000000000 | bytes 40000000 | tf_op jit(solution)/shard_map/input_back/pallas_call | solution.py:935
  538.6 39.4 %psum.7 = f32[5120]{0:T(1024)} all-reduce(f32[5120]{0:T(1024)} %pad_maximum_fusion.6), channel_id=1, replica_groups=mesh['dp'=4,'row'=2,'col'=4] {'dp','row','col'}, use_global_device_ids=true, to_apply=%region_1.2 | all-reduce | flops 5120 | bytes 40960 | tf_op jit(solution)/shard_map/psum | solution.py:980
  590.1 5.7 collective-permute-done.12
  603.1 15.1 %all-gather = bf16[768,256]{1,0:T(8,128)(2,1)S(1)} all-gather(bf16[192,256]{1,0:T(8,128)(2,1)S(1)} %slice.194), channel_id=2, replica_groups=mesh['dp'=4,'row'=2,'col'=4] {'col'}, dimensions={0}, use_global_device_ids=true | all-gather | bytes 491520 | tf_op jit(solution)/shard_map/all_gather | solution.py:962
  621.3 8.6 %all_gather.15 = bf16[768,512]{1,0:T(8,128)(2,1)S(1)} all-gather(bf16[192,512]{1,0:T(8,128)(2,1)S(1)} %convert_element_type.233), channel_id=1, replica_groups=mesh['dp'=4,'row'=2,'col'=4] {'dp'}, dimensions={0}, use_global_device_ids=true | all-gather | bytes 983040 | tf_op jit(solution)/shard_map/all_gather | solution.py:966
  649.7 31.6 %collective-permute-done.18 = bf16[2,192,2240]{2,1,0:T(8,128)(2,1)S(1)} collective-permute-done((bf16[2,192,2240]{2,1,0:T(8,128)(2,1)}, bf16[2,192,2240]{2,1,0:T(8,128)(2,1)S(1)}, u32[]{:S(2)}, u32[]{:S(2)}) %collective-permute-start.18) | collective-permute-done | bytes 1720352 | tf_op jit(solution)/shard_map/ppermute | solution.py:750
  687.3 36.6 %collective-permute-done.24 = bf16[2,192,2240]{2,1,0:T(8,128)(2,1)S(1)} collective-permute-done((bf16[2,192,2240]{2,1,0:T(8,128)(2,1)S(1)}, bf16[2,192,2240]{2,1,0:T(8,128)(2,1)S(1)}, u32[]{:S(2)}, u32[]{:S(2)}) %collective-permute-start.24) | collective-permute-done | bytes 1720352 | tf_op jit(solution)/shard_map/ppermute | solution.py:750
  726.6 15.4 %collective-permute-done.19 = bf16[192,2240]{1,0:T(8,128)(2,1)S(1)} collective-permute-done((bf16[192,2240]{1,0:T(8,128)(2,1)S(1)}, bf16[192,2240]{1,0:T(8,128)(2,1)S(1)}, u32[]{:S(2)}, u32[]{:S(2)}) %collective-permute-start.19) | collective-permute-done | bytes 860192 | tf_op jit(solution)/shard_map/ppermute | solution.py:750
  (219 shorter events, 135.8 us)
Async XLA Ops:
  7.2 299.1 %all-gather.3.cloned.1.call-start = ((), (), s32[]{:S(2)}) async-start(), calls=%async_computation.1 | async-start | bytes 1966080 | tf_op jit(solution)/shard_map/all_gather | solution.py:869
  12.6 114.5 %collective-permute-start.6 = (bf16[3,384,2240]{1,2,0:T(8,128)(2,1)S(1)}, bf16[3,384,2240]{1,2,0:T(8,128)(2,1)}, u32[]{:S(2)}, u32[]{:S(2)}) collective-permute-start(bf16[3,384,2240]{1,2,0:T(8,128)(2,1)S(1)} %pad_maximum_fusion), channel_id=1, source_target_pairs={{0,4},{4,0},{1,5},{5,1},{2,6},{6,2},{3,7},{7,3},{8,12},{12,8},{9,1... | collective-permute-start | bytes 15482888 | tf_op jit(solution)/shard_map/ppermute | solution.py:750
  127.1 170.2 %collective-permute-start.7 = (bf16[3,384,2240]{1,2,0:T(8,128)(2,1)}, bf16[3,384,2240]{1,2,0:T(8,128)(2,1)}, u32[]{:S(2)}, u32[]{:S(2)}) collective-permute-start(bf16[3,384,2240]{1,2,0:T(8,128)(2,1)} %collective-permute-done.6), channel_id=1, source_target_pairs={{0,8},{8,0},{16,24},{24,16},{1,9},{9,1},{17,25},{25,17},{2,10},{10... | collective-permute-start | bytes 15482888 | tf_op jit(solution)/shard_map/ppermute | solution.py:750
  128.1 31.4 %collective-permute-start = (bf16[128,768]{1,0:T(8,128)(2,1)}, bf16[128,768]{1,0:T(8,128)(2,1)}, u32[]{:S(2)}, u32[]{:S(2)}) collective-permute-start(bf16[128,768]{1,0:T(8,128)(2,1)} %bitcast.1), channel_id=1, source_target_pairs={{0,4},{4,0},{1,5},{5,1},{2,6},{6,2},{3,7},{7,3},{8,12},{12,8},{9,1... | collective-permute-start | bytes 589832 | tf_op jit(solution)/shard_map/ppermute | solution.py:750
  130.4 15.2 %collective-permute-start.1 = (f32[2048]{0:T(1024)}, f32[2048]{0:T(1024)S(1)}, u32[]{:S(2)}, u32[]{:S(2)}) collective-permute-start(f32[2048]{0:T(1024)} %pad_maximum_fusion.7), channel_id=1, source_target_pairs={{0,4},{4,0},{1,5},{5,1},{2,6},{6,2},{3,7},{7,3},{8,12},{12,8},{9,1... | collective-permute-start | bytes 24584 | tf_op jit(solution)/shard_map/ppermute | solution.py:750
  133.5 23.4 %collective-permute-start.2 = (bf16[384,1024]{1,0:T(8,128)(2,1)S(1)}, bf16[384,1024]{1,0:T(8,128)(2,1)S(1)}, u32[]{:S(2)}, u32[]{:S(2)}) collective-permute-start(bf16[384,1024]{1,0:T(8,128)(2,1)S(1)} %fusion.11), channel_id=1, source_target_pairs={{0,4},{4,0},{1,5},{5,1},{2,6},{6,2},{3,7},{7,3},{8,12},{12,8},{9,1... | collective-permute-start | bytes 2359304 | tf_op jit(solution)/shard_map/ppermute | solution.py:750
  142.3 477.3 %reduce-scatter.2.cloned.1.call-start = ((), (), s32[]{:S(2)}) async-start(), calls=%async_computation.2 | async-start | bytes 1966080 | tf_op jit(solution)/shard_map/reduce_scatter | solution.py:895
  209.6 18.4 %collective-permute-start.4 = (bf16[512,256]{1,0:T(8,128)(2,1)}, bf16[512,256]{1,0:T(8,128)(2,1)}, u32[]{:S(2)}, u32[]{:S(2)}) collective-permute-start(bf16[512,256]{1,0:T(8,128)(2,1)} %get-tuple-element.36.own_ref), channel_id=1, source_target_pairs={{0,4},{4,0},{1,5},{5,1},{2,6},{6,2},{3,7},{7,3},{8,12},{12,8},{9,1... | collective-permute-start | bytes 786440 | tf_op jit(solution)/shard_map/ppermute | solution.py:750
  427.1 62.4 %collective-permute-start.9 = (bf16[512,256]{1,0:T(8,128)(2,1)}, bf16[512,256]{1,0:T(8,128)(2,1)S(1)}, u32[]{:S(2)}, u32[]{:S(2)}) collective-permute-start(bf16[512,256]{1,0:T(8,128)(2,1)} %get-tuple-element.46), channel_id=1, source_target_pairs={{0,4},{4,0},{1,5},{5,1},{2,6},{6,2},{3,7},{7,3},{8,12},{12,8},{9,1... | collective-permute-start | bytes 786440 | tf_op jit(solution)/shard_map/ppermute | solution.py:750
  429.2 148.9 %collective-permute-start.14 = (bf16[2,2,192,384]{3,2,0,1:T(8,128)(2,1)}, bf16[2,2,192,384]{3,2,0,1:T(8,128)(2,1)}, u32[]{:S(2)}, u32[]{:S(2)}) collective-permute-start(bf16[2,2,192,384]{3,2,0,1:T(8,128)(2,1)} %bitcast.126), channel_id=1, source_target_pairs={{0,8},{8,0},{16,24},{24,16},{1,9},{9,1},{17,25},{25,17},{2,10},{10... | collective-permute-start | bytes 1769480 | tf_op jit(solution)/shard_map/ppermute | solution.py:750
  449.6 185.2 %collective-permute-start.17 = (bf16[2,2,192,2240]{3,2,1,0:T(8,128)(2,1)}, bf16[2,2,192,2240]{3,2,1,0:T(8,128)(2,1)}, u32[]{:S(2)}, u32[]{:S(2)}) collective-permute-start(bf16[2,2,192,2240]{3,2,1,0:T(8,128)(2,1)} %dynamic-slice_bitcast_fusion.2), channel_id=1, source_target_pairs={{0,8},{8,0},{16,24},{24,16},{1,9},{9,1},{17,25},{25,17},{2,10},{10... | collective-permute-start | bytes 10321928 | tf_op jit(solution)/shard_map/ppermute | solution.py:750
  469.3 171.5 %collective-permute-start.20 = (bf16[2,2,192,2240]{3,2,1,0:T(8,128)(2,1)}, bf16[2,2,192,2240]{3,2,1,0:T(8,128)(2,1)}, u32[]{:S(2)}, u32[]{:S(2)}) collective-permute-start(bf16[2,2,192,2240]{3,2,1,0:T(8,128)(2,1)} %dynamic-slice_bitcast_fusion.1), channel_id=1, source_target_pairs={{0,8},{8,0},{16,24},{24,16},{1,9},{9,1},{17,25},{25,17},{2,10},{10... | collective-permute-start | bytes 10321928 | tf_op jit(solution)/shard_map/ppermute | solution.py:750
  527.0 58.7 %collective-permute-start.10 = (bf16[128,768]{1,0:T(8,128)(2,1)}, bf16[128,768]{1,0:T(8,128)(2,1)}, u32[]{:S(2)}, u32[]{:S(2)}) collective-permute-start(bf16[128,768]{1,0:T(8,128)(2,1)} %slice.192), channel_id=1, source_target_pairs={{0,4},{4,0},{1,5},{5,1},{2,6},{6,2},{3,7},{7,3},{8,12},{12,8},{9,1... | collective-permute-start | bytes 589832 | tf_op jit(solution)/shard_map/ppermute | solution.py:750
  533.0 49.0 %collective-permute-start.11 = (bf16[2,2,192,640]{3,2,1,0:T(8,128)(2,1)}, bf16[2,2,192,640]{3,2,1,0:T(8,128)(2,1)S(1)}, u32[]{:S(2)}, u32[]{:S(2)}) collective-permute-start(bf16[2,2,192,640]{3,2,1,0:T(8,128)(2,1)} %dynamic-slice_bitcast_fusion.7), channel_id=1, source_target_pairs={{0,8},{8,0},{16,24},{24,16},{1,9},{9,1},{17,25},{25,17},{2,10},{10... | collective-permute-start | bytes 2949128 | tf_op jit(solution)/shard_map/ppermute | solution.py:750
  582.3 13.5 %collective-permute-start.12 = (bf16[2,192,640]{2,1,0:T(8,128)(2,1)S(1)}, bf16[2,192,640]{2,1,0:T(8,128)(2,1)S(1)}, u32[]{:S(2)}, u32[]{:S(2)}) collective-permute-start(bf16[2,192,640]{2,1,0:T(8,128)(2,1)S(1)} %slice_bitcast_fusion.6), channel_id=1, source_target_pairs={{0,4},{4,0},{1,5},{5,1},{2,6},{6,2},{3,7},{7,3},{8,12},{12,8},{9,1... | collective-permute-start | bytes 1474568 | tf_op jit(solution)/shard_map/ppermute | solution.py:750
  585.7 59.6 %collective-permute-start.23 = (bf16[2,2,192,2240]{3,2,1,0:T(8,128)(2,1)}, bf16[2,2,192,2240]{3,2,1,0:T(8,128)(2,1)}, u32[]{:S(2)}, u32[]{:S(2)}) collective-permute-start(bf16[2,2,192,2240]{3,2,1,0:T(8,128)(2,1)} %dynamic-slice_bitcast_fusion), channel_id=1, source_target_pairs={{0,8},{8,0},{16,24},{24,16},{1,9},{9,1},{17,25},{25,17},{2,10},{10... | collective-permute-start | bytes 10321928 | tf_op jit(solution)/shard_map/ppermute | solution.py:750
  588.3 9.3 %collective-permute-start.16 = (bf16[192,384]{1,0:T(8,128)(2,1)S(1)}, bf16[192,384]{1,0:T(8,128)(2,1)S(1)}, u32[]{:S(2)}, u32[]{:S(2)}) collective-permute-start(bf16[192,384]{1,0:T(8,128)(2,1)S(1)} %slice_bitcast_fusion.8), channel_id=1, source_target_pairs={{0,4},{4,0},{1,5},{5,1},{2,6},{6,2},{3,7},{7,3},{8,12},{12,8},{9,1... | collective-permute-start | bytes 442376 | tf_op jit(solution)/shard_map/ppermute | solution.py:750
  620.7 10.7 %collective-permute-start.8 = (bf16[128,768]{1,0:T(8,128)(2,1)S(1)}, bf16[128,768]{1,0:T(8,128)(2,1)S(1)}, u32[]{:S(2)}, u32[]{:S(2)}) collective-permute-start(bf16[128,768]{1,0:T(8,128)(2,1)S(1)} %slice.193), channel_id=1, source_target_pairs={{0,4},{4,0},{1,5},{5,1},{2,6},{6,2},{3,7},{7,3},{8,12},{12,8},{9,1... | collective-permute-start | bytes 589832 | tf_op jit(solution)/shard_map/ppermute | solution.py:750
  640.2 41.1 %collective-permute-start.18 = (bf16[2,192,2240]{2,1,0:T(8,128)(2,1)}, bf16[2,192,2240]{2,1,0:T(8,128)(2,1)S(1)}, u32[]{:S(2)}, u32[]{:S(2)}) collective-permute-start(bf16[2,192,2240]{2,1,0:T(8,128)(2,1)} %dynamic-slice_bitcast_fusion.3), channel_id=1, source_target_pairs={{0,16},{8,24},{16,0},{24,8},{1,17},{9,25},{17,1},{25,9},{2,18},{10... | collective-permute-start | bytes 5160968 | tf_op jit(solution)/shard_map/ppermute | solution.py:750
  644.4 41.5 %collective-permute-start.21 = (bf16[2,192,2240]{2,1,0:T(8,128)(2,1)S(1)}, bf16[2,192,2240]{2,1,0:T(8,128)(2,1)S(1)}, u32[]{:S(2)}, u32[]{:S(2)}) collective-permute-start(bf16[2,192,2240]{2,1,0:T(8,128)(2,1)S(1)} %slice_bitcast_fusion.2), channel_id=1, source_target_pairs={{0,4},{4,0},{1,5},{5,1},{2,6},{6,2},{3,7},{7,3},{8,12},{12,8},{9,1... | collective-permute-start | bytes 5160968 | tf_op jit(solution)/shard_map/ppermute | solution.py:750
  648.4 75.5 %collective-permute-start.24 = (bf16[2,192,2240]{2,1,0:T(8,128)(2,1)S(1)}, bf16[2,192,2240]{2,1,0:T(8,128)(2,1)S(1)}, u32[]{:S(2)}, u32[]{:S(2)}) collective-permute-start(bf16[2,192,2240]{2,1,0:T(8,128)(2,1)S(1)} %slice_bitcast_fusion), channel_id=1, source_target_pairs={{0,4},{4,0},{1,5},{5,1},{2,6},{6,2},{3,7},{7,3},{8,12},{12,8},{9,1... | collective-permute-start | bytes 5160968 | tf_op jit(solution)/shard_map/ppermute | solution.py:750
  681.7 60.2 %collective-permute-start.19 = (bf16[192,2240]{1,0:T(8,128)(2,1)S(1)}, bf16[192,2240]{1,0:T(8,128)(2,1)S(1)}, u32[]{:S(2)}, u32[]{:S(2)}) collective-permute-start(bf16[192,2240]{1,0:T(8,128)(2,1)S(1)} %slice_bitcast_fusion.4), channel_id=1, source_target_pairs={{0,4},{4,0},{1,5},{5,1},{2,6},{6,2},{3,7},{7,3},{8,12},{12,8},{9,1... | collective-permute-start | bytes 2580488 | tf_op jit(solution)/shard_map/ppermute | solution.py:750
  686.5 38.7 %collective-permute-start.22 = (bf16[192,2240]{1,0:T(8,128)(2,1)S(1)}, bf16[192,2240]{1,0:T(8,128)(2,1)S(1)}, u32[]{:S(2)}, u32[]{:S(2)}) collective-permute-start(bf16[192,2240]{1,0:T(8,128)(2,1)S(1)} %dynamic-slice_bitcast_fusion.9), channel_id=1, source_target_pairs={{0,16},{8,24},{16,0},{24,8},{1,17},{9,25},{17,1},{25,9},{2,18},{10... | collective-permute-start | bytes 2580488 | tf_op jit(solution)/shard_map/ppermute | solution.py:750
  724.4 20.0 %collective-permute-start.25 = (bf16[192,2240]{1,0:T(8,128)(2,1)S(1)}, bf16[192,2240]{1,0:T(8,128)(2,1)S(1)}, u32[]{:S(2)}, u32[]{:S(2)}) collective-permute-start(bf16[192,2240]{1,0:T(8,128)(2,1)S(1)} %dynamic-slice_bitcast_fusion.8), channel_id=1, source_target_pairs={{0,16},{8,24},{16,0},{24,8},{1,17},{9,25},{17,1},{25,9},{2,18},{10... | collective-permute-start | bytes 2580488 | tf_op jit(solution)/shard_map/ppermute | solution.py:750
  (36 other events, 1131.7 us)
Sparse Core Ops, SparseCore 0:
  142.4 43.4 all-gather.2
  341.6 57.6 reduce-scatter.1

commit v2 on v1

--- a/solution.py
+++ b/solution.py
@@ -338,8 +338,10 @@
 SCALE = HEAD_SIZE ** (-0.5)
 
 
-def line_barrier(me):
+def greet(me, others):
     barrier = pltpu.get_barrier_semaphore()
+    for axis, index in others:
+        pl.semaphore_signal(barrier, 1, device_id={axis: index}, device_id_type=MESH_ID)
 
     @pl.when(me > 0)
     def _():
@@ -351,138 +353,183 @@
 
     @pl.when((me > 0) & (me < LINE - 1))
     def _():
-        pl.semaphore_wait(barrier, 2)
+        pl.semaphore_wait(barrier, 2 + len(others))
 
     @pl.when((me == 0) | (me == LINE - 1))
     def _():
-        pl.semaphore_wait(barrier, 1)
+        pl.semaphore_wait(barrier, 1 + len(others))
+
+
+def line_barrier(me):
+    greet(me, [])
 
 
 def block_rows(index):
     return pl.ds(pl.multiple_of(index * BLOCK, BLOCK), BLOCK)
 
 
-def gather_line(me, all_ref, sends, recv, each):
-    def copy(j, to, sem):
-        rows = all_ref.at[block_rows(j)]
-        return pltpu.make_async_remote_copy(
-            rows, rows, sem, recv.at[j], device_id={"col": to}, device_id_type=MESH_ID
-        )
-
-    def arrived(j):
-        rows = all_ref.at[block_rows(j)]
-        pltpu.make_async_copy(rows, rows, recv.at[j]).wait()
-
-    for s in range(LINE):
+def nothing(*_):
+    return None
+
+
+def send(src, dst, send_sem, recv_sem, axis, to):
+    return pltpu.make_async_remote_copy(
+        src, dst, send_sem, recv_sem, device_id={axis: to}, device_id_type=MESH_ID
+    )
+
+
+def landed(ref, sem):
+    pltpu.make_async_copy(ref, ref, sem).wait()
+
+
+class Gather:
+    def __init__(self, me, rows_of, sends, recv):
+        self.me, self.rows_of, self.sends, self.recv = me, rows_of, sends, recv
+
+    def copy(self, j, to, sem):
+        rows = self.rows_of(j)
+        return send(rows, rows, sem, self.recv.at[j], "col", to)
+
+    def step(self, s):
+        me = self.me
         left, right = me - s, me + s
 
         @pl.when(left >= 0)
         def _():
             if s:
-                arrived(left)
+                landed(self.rows_of(left), self.recv.at[left])
 
             @pl.when(me < LINE - 1)
             def _():
-                copy(left, me + 1, sends.at[0, s]).start()
+                self.copy(left, me + 1, self.sends.at[0, s]).start()
 
         @pl.when(right < LINE)
         def _():
             if s:
-                arrived(right)
+                landed(self.rows_of(right), self.recv.at[right])
 
             @pl.when(me > 0)
             def _():
-                copy(right, me - 1, sends.at[1, s]).start()
-
-        @pl.when(left >= 0)
+                self.copy(right, me - 1, self.sends.at[1, s]).start()
+
+    def run_each(self, s, each):
+        me = self.me
+
+        @pl.when(me - s >= 0)
         def _():
-            each(left)
+            each(me - s)
 
         if s:
 
-            @pl.when(right < LINE)
+            @pl.when(me + s < LINE)
             def _():
-                each(right)
-
+                each(me + s)
+
+    def drain(self):
+        me = self.me
+        for s in range(LINE):
+
+            @pl.when((me - s >= 0) & (me < LINE - 1))
+            def _():
+                self.copy(me, me + 1, self.sends.at[0, s]).wait_send()
+
+            @pl.when((me + s < LINE) & (me > 0))
+            def _():
+                self.copy(me, me - 1, self.sends.at[1, s]).wait_send()
+
+
+def gather_line(me, all_ref, sends, recv, each, between=nothing):
+    gather = Gather(me, lambda j: all_ref.at[block_rows(j)], sends, recv)
     for s in range(LINE):
-
-        @pl.when((me - s >= 0) & (me < LINE - 1))
-        def _():
-            copy(me, me + 1, sends.at[0, s]).wait_send()
-
-        @pl.when((me + s < LINE) & (me > 0))
-        def _():
-            copy(me, me - 1, sends.at[1, s]).wait_send()
-
-
-def scatter_line(me, block_of, out_ref, from_left, from_right, going, sends, recv):
-    def copy(j, to, side, landing):
-        return pltpu.make_async_remote_copy(
-            going.at[j],
-            landing.at[j],
-            sends.at[side, j],
-            recv.at[side, j],
-            device_id={"col": to},
-            device_id_type=MESH_ID,
+        gather.step(s)
+        gather.run_each(s, each)
+        between(s)
+    gather.drain()
+
+
+class Scatter:
+    def __init__(self, me, block_of, from_left, from_right, sends, recv):
+        self.me, self.block_of = me, block_of
+        self.from_left, self.from_right, self.sends, self.recv = from_left, from_right, sends, recv
+
+    def copy(self, j, to, side):
+        landing = self.from_right if side else self.from_left
+        return send(
+            landing.at[j], landing.at[j], self.sends.at[side, j], self.recv.at[side, j], "col", to
         )
 
-    def arrived(j, side, landing):
-        pltpu.make_async_copy(landing.at[j], landing.at[j], recv.at[side, j]).wait()
-
-    for s in range(LINE - 1, 0, -1):
+    def arrived(self, j, side):
+        landing = self.from_right if side else self.from_left
+        landed(landing.at[j], self.recv.at[side, j])
+
+    def step(self, s):
+        me = self.me
         ahead, behind = me + s, me - s
 
         @pl.when(ahead < LINE)
         def _():
-            mine = block_of(ahead)
+            mine = self.block_of(ahead)
 
             @pl.when(me > 0)
             def _():
-                arrived(ahead, 0, from_left)
-                going[ahead] = (mine + from_left[ahead].astype(F32)).astype(BF16)
+                self.arrived(ahead, 0)
+                self.from_left[ahead] = (mine + self.from_left[ahead].astype(F32)).astype(BF16)
 
             @pl.when(me == 0)
             def _():
-                going[ahead] = mine.astype(BF16)
-
-            copy(ahead, me + 1, 0, from_left).start()
+                self.from_left[ahead] = mine.astype(BF16)
+
+            self.copy(ahead, me + 1, 0).start()
 
         @pl.when(behind >= 0)
         def _():
-            mine = block_of(behind)
+            mine = self.block_of(behind)
 
             @pl.when(me < LINE - 1)
             def _():
-                arrived(behind, 1, from_right)
-                going[behind] = (mine + from_right[behind].astype(F32)).astype(BF16)
+                self.arrived(behind, 1)
+                self.from_right[behind] = (mine + self.from_right[behind].astype(F32)).astype(BF16)
 
             @pl.when(me == LINE - 1)
             def _():
-                going[behind] = mine.astype(BF16)
-
-            copy(behind, me - 1, 1, from_right).start()
-
-    out_ref[...] = block_of(me)
-
-    @pl.when(me > 0)
-    def _():
-        arrived(me, 0, from_left)
-        out_ref[...] += from_left[me].astype(F32)
-
-    @pl.when(me < LINE - 1)
-    def _():
-        arrived(me, 1, from_right)
-        out_ref[...] += from_right[me].astype(F32)
-
-    for s in range(1, LINE):
-
-        @pl.when(me + s < LINE)
+                self.from_right[behind] = mine.astype(BF16)
+
+            self.copy(behind, me - 1, 1).start()
+
+    def finish(self, out_ref):
+        me = self.me
+        out_ref[...] = self.block_of(me)
+
+        @pl.when(me > 0)
         def _():
-            copy(me + s, me + 1, 0, from_left).wait_send()
-
-        @pl.when(me - s >= 0)
+            self.arrived(me, 0)
+            out_ref[...] += self.from_left[me].astype(F32)
+
+        @pl.when(me < LINE - 1)
         def _():
-            copy(me - s, me - 1, 1, from_right).wait_send()
+            self.arrived(me, 1)
+            out_ref[...] += self.from_right[me].astype(F32)
+
+    def drain(self):
+        me = self.me
+        for s in range(1, LINE):
+
+            @pl.when(me + s < LINE)
+            def _():
+                self.copy(me + s, me + 1, 0).wait_send()
+
+            @pl.when(me - s >= 0)
+            def _():
+                self.copy(me - s, me - 1, 1).wait_send()
+
+
+def scatter_line(me, block_of, out_ref, from_left, from_right, sends, recv, between=nothing):
+    scatter = Scatter(me, block_of, from_left, from_right, sends, recv)
+    for s in range(LINE - 1, 0, -1):
+        scatter.step(s)
+        between(s)
+    scatter.finish(out_ref)
+    scatter.drain()
 
 
 def dot(a, b, dims=(((1,), (0,)), ((), ()))):
@@ -515,38 +562,10 @@
 
 
 def scatter_scratch(width=MODEL_WIDTH):
-    return [pltpu.VMEM((LINE, BLOCK, width), BF16)] * 3 + [pltpu.SemaphoreType.DMA((2, LINE))] * 2
-
-
-def project_body(
-    x_ref, gain_ref, own_ref, other_ref, bias_ref, cos_ref, sin_ref, all_ref, query_ref, kv_ref, sends, recv
-):
-    me = lax.axis_index("col")
-    line_barrier(me)
-    x = x_ref[...].astype(F32)
-    all_ref[block_rows(me)] = (x * norm_scale(x) * gain_ref[...]).astype(BF16)
-    query_cols = query_ref.shape[1]
-
-    def each(j):
-        rows = block_rows(j)
-        block = all_ref[rows]
-        out = dot(block[:, :HALF], own_ref[...]) + dot(block[:, HALF:], other_ref[...])
-        out = out + bias_ref[...]
-        cosine, sine = cos_ref[rows], sin_ref[rows]
-        for h in range(query_cols // HEAD_SIZE + 1):
-            head = out[:, h * HEAD_SIZE : (h + 1) * HEAD_SIZE]
-            turned = (head * cosine + turn(head) * sine).astype(BF16)
-            if h * HEAD_SIZE < query_cols:
-                query_ref[rows, h * HEAD_SIZE : (h + 1) * HEAD_SIZE] = turned
-            else:
-                kv_ref[rows, :HEAD_SIZE] = turned
-        kv_ref[rows, HEAD_SIZE:] = out[:, query_cols + HEAD_SIZE :].astype(BF16)
-
-    gather_line(me, all_ref, sends, recv, each)
-
-
-def attend_body(query_ref, own_ref, other_ref, attended_ref, probs_ref):
-    r = lax.axis_index("row")
+    return [pltpu.VMEM((LINE, BLOCK, width), BF16)] * 2 + [pltpu.SemaphoreType.DMA((2, LINE))] * 2
+
+
+def attend_local(query_ref, own_ref, other_ref, attended_ref, probs_ref, r):
     rows = 2 * BLOCK
     shape = (rows, rows)
     at_row = lax.broadcasted_iota(jnp.int32, shape, 0)
@@ -614,36 +633,16 @@
         other_grad_ref[part, HEAD_SIZE:] = sums[3].astype(BF16)
 
 
-def residual_body(
-    attended_ref, own_ref, other_ref, x_ref, gain_ref, mid_ref, all_ref,
-    from_left, from_right, going, s_sends, s_recv, sends, recv,
-):
-    me = lax.axis_index("col")
-    line_barrier(me)
-
-    def block_of(j):
-        block = attended_ref[block_rows(j)]
-        return jnp.concatenate(
-            [dot(block, own_ref[...], PAIR_COLS), dot(block, other_ref[...], PAIR_COLS)], 1
-        )
-
-    scatter_line(me, block_of, mid_ref, from_left, from_right, going, s_sends, s_recv)
-    mid = mid_ref[...] + x_ref[...].astype(F32)
-    mid_ref[...] = mid
-    all_ref[block_rows(me)] = (mid * norm_scale(mid) * gain_ref[...]).astype(BF16)
-    gather_line(me, all_ref, sends, recv, lambda j: None)
-
-
 def middle_back_body(
     part_ref, mid_ref, cot_ref, gain_ref, own_ref, other_ref,
     mid_grad_ref, gain_grad_ref, all_ref, att_grad_ref,
-    from_left, from_right, going, s_sends, s_recv, sends, recv,
+    from_left, from_right, s_sends, s_recv, sends, recv,
 ):
     me = lax.axis_index("col")
     line_barrier(me)
     scatter_line(
         me, lambda j: part_ref[block_rows(j)].astype(F32), mid_grad_ref,
-        from_left, from_right, going, s_sends, s_recv,
+        from_left, from_right, s_sends, s_recv,
     )
     mid, grad = mid_ref[...], mid_grad_ref[...]
     rinv = norm_scale(mid)
@@ -666,7 +665,7 @@
 def input_back_body(
     query_grad_ref, own_kv_ref, got_kv_ref, cos_ref, sin_ref, own_ref, other_ref, x_ref, gain_ref,
     mid_grad_ref, proj_grad_ref, bias_ref, input_grad_ref, gain_grad_ref,
-    from_left, from_right, going, s_sends, s_recv,
+    from_left, from_right, s_sends, s_recv,
 ):
     me = lax.axis_index("col")
     line_barrier(me)
@@ -685,7 +684,7 @@
             [dot(block, own_ref[...], PAIR_COLS), dot(block, other_ref[...], PAIR_COLS)], 1
         )
 
-    scatter_line(me, block_of, input_grad_ref, from_left, from_right, going, s_sends, s_recv)
+    scatter_line(me, block_of, input_grad_ref, from_left, from_right, s_sends, s_recv)
     bias_ref[...] = jnp.sum(proj_grad_ref[...].astype(F32), 0, keepdims=True)
     x, grad = x_ref[...].astype(F32), input_grad_ref[...]
     rinv = norm_scale(x)
@@ -696,47 +695,57 @@
 
 
 def feed_body(
-    normed_ref, cot_ref, gate_hbm, upper_hbm, down_hbm, other_hbm, partner_hbm,
+    normed_ref, cot_ref, gate_hbm, upper_hbm, down_hbm, other_hbm,
     activated_ref, gate_grad_ref, upper_grad_ref, back_ref, out_ref,
     weights, back_sum, out_sum, sems,
 ):
-    core = lax.rem(lax.axis_index("dp"), 2)
     hidden = activated_ref.shape[1]
-    quarter = HALF // 2
-    here = pl.ds(pl.multiple_of(HALF + core * quarter, quarter), quarter)
-    there = pl.ds(pl.multiple_of(HALF + (1 - core) * quarter, quarter), quarter)
-    copies = []
-    for i, own in enumerate((gate_hbm, upper_hbm, down_hbm)):
-        copies.append(pltpu.make_async_copy(own, weights.at[i, pl.ds(0, HALF)], sems.at[i, 0]))
-        copies.append(pltpu.make_async_copy(other_hbm.at[i], weights.at[i, here], sems.at[i, 1]))
-        copies.append(pltpu.make_async_copy(partner_hbm.at[i], weights.at[i, there], sems.at[i, 2]))
-    for copy in copies:
-        copy.start()
-    for copy in copies:
-        copy.wait()
     tile = 256
-    for i, low in enumerate(range(0, hidden, tile)):
-        cols = slice(low, min(low + tile, hidden))
-        gate_w, upper_w, down_w = weights[0, :, cols], weights[1, :, cols], weights[2, :, cols]
-        gate = dot(normed_ref[...], gate_w)
-        upper = dot(normed_ref[...], upper_w)
-        act_grad = dot(cot_ref[...], down_w)
+    chunk = 2 * tile
+    lows = list(range(0, hidden, chunk))
+
+    def copies(k):
+        rows = pl.ds(lows[k], min(chunk, hidden - lows[k]))
+        for i, own in enumerate((gate_hbm, upper_hbm, down_hbm)):
+            yield pltpu.make_async_copy(
+                own.at[rows], weights.at[i, rows, pl.ds(0, HALF)], sems.at[k, i, 0]
+            )
+            yield pltpu.make_async_copy(
+                other_hbm.at[i, rows], weights.at[i, rows, pl.ds(HALF, HALF)], sems.at[k, i, 1]
+            )
+
+    for k in range(len(lows)):
+        for copy in copies(k):
+            copy.start()
+    back_sum[...] = jnp.zeros_like(back_sum)
+    out_sum[...] = jnp.zeros_like(out_sum)
+
+    def run(low, size):
+        rows = pl.ds(low, size)
+        gate = dot(normed_ref[...], weights[0, rows], PAIR_COLS)
+        upper = dot(normed_ref[...], weights[1, rows], PAIR_COLS)
+        act_grad = dot(cot_ref[...], weights[2, rows], PAIR_COLS)
         sig = jax.nn.sigmoid(gate)
         silu = gate * sig
         activated = (silu * upper).astype(BF16)
         gate_grad = (act_grad * upper * sig * (1.0 + gate * (1.0 - sig))).astype(BF16)
         upper_grad = (act_grad * silu).astype(BF16)
-        activated_ref[:, cols] = activated
-        gate_grad_ref[:, cols] = gate_grad
-        upper_grad_ref[:, cols] = upper_grad
-        back = dot(gate_grad, gate_w, PAIR_COLS) + dot(upper_grad, upper_w, PAIR_COLS)
-        out = dot(activated, down_w, PAIR_COLS)
-        if i == 0:
-            back_sum[...] = back
-            out_sum[...] = out
+        activated_ref[:, rows] = activated
+        gate_grad_ref[:, rows] = gate_grad
+        upper_grad_ref[:, rows] = upper_grad
+        back_sum[...] += dot(gate_grad, weights[0, rows]) + dot(upper_grad, weights[1, rows])
+        out_sum[...] += dot(activated, weights[2, rows])
+
+    for k, low in enumerate(lows):
+        for copy in copies(k):
+            copy.wait()
+        if low + chunk <= hidden:
+
+            @pl.loop(0, 2)
+            def _(t):
+                run(pl.multiple_of(low + t * tile, tile), tile)
         else:
-            back_sum[...] += back
-            out_sum[...] += out
+            run(low, hidden - low)
     back_ref[...] = back_sum[...].astype(BF16)
     out_ref[...] = out_sum[...].astype(BF16)
 
@@ -764,6 +773,245 @@
         return choose(y).astype(F32) + swap(choose(1 - y), "dp", 2).astype(F32)
     half = (choose(y).astype(F32) + swap(choose(1 - y), "dp", 2).astype(F32)).astype(BF16)
     return half[0].astype(F32) + swap(half[1], "row", 1).astype(F32)
+
+
+PIECES = 6
+
+
+def front_body(
+    keep_ref, pass_ref, cot_keep_ref, cot_pass_ref, table_ref, gains_ref, bias_ref, proj_ref,
+    gate_hbm, upper_hbm, down_hbm,
+    x_ref, normed_ref, query_ref, kv_ref, kv_other_ref, cos_ref, sin_ref, all_gains_ref,
+    attended_ref, probs_ref, mid_ref, normed_two_ref, cot_ref, proj_other_ref, weights_other_hbm,
+    tables, from_left, from_right,
+    swap_sends, swap_recv, piece_sends, piece_recv, kv_sends, kv_recv,
+    g_sends, g_recv, c_sends, c_recv, n_sends, n_recv, s_sends, s_recv,
+):
+    me, r, d = lax.axis_index("col"), lax.axis_index("row"), lax.axis_index("dp")
+    y, core = d // 2, lax.rem(d, 2)
+    x_to, y_to, core_to = 1 - r, 2 * (1 - y) + core, 2 * y + 1 - core
+    greet(me, [("row", x_to), ("dp", y_to), ("dp", core_to)])
+    proj_cols = bias_ref.shape[1]
+    query_cols = query_ref.shape[1]
+    quarter = HALF // 2
+    my_rows = pl.ds(pl.multiple_of(core * quarter, quarter), quarter)
+    its_rows = pl.ds(pl.multiple_of((1 - core) * quarter, quarter), quarter)
+
+    swaps = [
+        (pass_ref, x_ref.at[:, HALF:], "row", x_to),
+        (table_ref.at[1], tables.at[1], "row", x_to),
+        (gains_ref, all_gains_ref.at[:, HALF:], "row", x_to),
+        (proj_ref.at[my_rows, :proj_cols], proj_other_ref.at[my_rows, :proj_cols], "row", x_to),
+        (cot_pass_ref, cot_ref.at[block_rows(me), HALF:], "row", x_to),
+        (proj_ref.at[my_rows, proj_cols:], proj_other_ref.at[my_rows, proj_cols:], "row", x_to),
+        (
+            proj_other_ref.at[my_rows, :proj_cols], proj_other_ref.at[my_rows, :proj_cols],
+            "dp", core_to,
+        ),
+        (
+            proj_other_ref.at[my_rows, proj_cols:], proj_other_ref.at[my_rows, proj_cols:],
+            "dp", core_to,
+        ),
+    ]
+
+    def swap_copy(i):
+        src, dst, axis, to = swaps[i]
+        return send(src, dst, swap_sends.at[i], swap_recv.at[i], axis, to)
+
+    def swap_landed(i):
+        swap_copy(i).wait_recv()
+
+    rows = gate_hbm.shape[0] // 4
+    owns = (gate_hbm, upper_hbm, down_hbm)
+    my_cols = my_rows
+
+    def piece(i, of_y):
+        return pl.ds(pl.multiple_of((of_y * 2 + i % 2) * rows, rows), rows)
+
+    def piece_copy(i, way):
+        m = i // 2
+        of_y = y if way in (0, 1, 2) else 1 - y
+        at = weights_other_hbm.at[m, piece(i, of_y), my_cols]
+        src = owns[m].at[piece(i, of_y), my_cols] if way == 0 else at
+        axis, to = (("row", x_to), ("dp", y_to), ("dp", core_to), ("dp", core_to))[way]
+        return send(src, at, piece_sends.at[way, i], piece_recv.at[way, i], axis, to)
+
+    def relay_x(i):
+        piece_copy(i, 0).wait_recv()
+        piece_copy(i, 1).start()
+        piece_copy(i, 2).start()
+
+    def relay_y(i):
+        piece_copy(i, 1).wait_recv()
+        piece_copy(i, 3).start()
+
+    for i in range(5):
+        swap_copy(i).start()
+    piece_copy(0, 0).start()
+    x_ref[:, :HALF] = keep_ref[...]
+    tables[0] = table_ref[0]
+    all_gains_ref[:, :HALF] = gains_ref[...]
+    cot_ref[block_rows(me), :HALF] = cot_keep_ref[...]
+    swap_landed(0)
+    swap_landed(1)
+    swap_landed(2)
+    x = x_ref[...].astype(F32)
+    normed_ref[block_rows(me)] = (x * norm_scale(x) * all_gains_ref[0:1]).astype(BF16)
+    gather = Gather(me, lambda j: normed_ref.at[block_rows(j)], g_sends, g_recv)
+    gather.step(0)
+
+    lane = lax.broadcasted_iota(jnp.int32, (2 * BLOCK, HEAD_SIZE), 1)
+    first = lane < HEAD_SIZE // 2
+    for i in range(2):
+        table = tables[i]
+        turned = turn(table)
+        at = pl.ds(pl.multiple_of((r if i == 0 else 1 - r) * 2 * BLOCK, BLOCK), 2 * BLOCK)
+        cos_ref[at] = jnp.where(first, table, turned)
+        sin_ref[at] = jnp.where(first, -turned, table)
+
+    swap_landed(3)
+    swap_copy(6).start()
+    swap_landed(6)
+
+    def kv_copy(j):
+        at = block_rows(j)
+        return send(
+            kv_ref.at[at], kv_other_ref.at[at], kv_sends.at[j], kv_recv.at[j], "row", x_to
+        )
+
+    def each(j):
+        at = block_rows(j)
+        block = normed_ref[at]
+        out = dot(block[:, :HALF], proj_ref[:, :proj_cols])
+        out = out + dot(block[:, HALF:], proj_other_ref[:, :proj_cols]) + bias_ref[...]
+        cosine, sine = cos_ref[at], sin_ref[at]
+        for h in range(query_cols // HEAD_SIZE + 1):
+            head = out[:, h * HEAD_SIZE : (h + 1) * HEAD_SIZE]
+            turned = (head * cosine + turn(head) * sine).astype(BF16)
+            if h * HEAD_SIZE < query_cols:
+                query_ref[at, h * HEAD_SIZE : (h + 1) * HEAD_SIZE] = turned
+            else:
+                kv_ref[at, :HEAD_SIZE] = turned
+        kv_ref[at, HEAD_SIZE:] = out[:, query_cols + HEAD_SIZE :].astype(BF16)
+        kv_copy(j).start()
+
+    for s in range(LINE):
+        if s:
+            gather.step(s)
+        gather.run_each(s, each)
+    swap_copy(5).start()
+    for i in range(1, PIECES):
+        piece_copy(i, 0).start()
+    swap_landed(4)
+    cot_gather = Gather(me, lambda j: cot_ref.at[block_rows(j)], c_sends, c_recv)
+    cot_gather.step(0)
+    relay_x(0)
+    for j in range(LINE):
+        kv_copy(j).wait_recv()
+    attend_local(query_ref, kv_ref, kv_other_ref, attended_ref, probs_ref, r)
+    swap_landed(5)
+    swap_copy(7).start()
+    relay_y(0)
+    swap_landed(7)
+
+    def block_of(j):
+        block = attended_ref[block_rows(j)]
+        return jnp.concatenate(
+            [
+                dot(block, proj_ref[:, proj_cols:], PAIR_COLS),
+                dot(block, proj_other_ref[:, proj_cols:], PAIR_COLS),
+            ],
+            1,
+        )
+
+    scatter = Scatter(me, block_of, from_left, from_right, s_sends, s_recv)
+    scatter.step(3)
+    scatter.step(2)
+    relay_x(1)
+    scatter.step(1)
+    scatter.finish(mid_ref)
+    mid = mid_ref[...] + x_ref[...].astype(F32)
+    mid_ref[...] = mid
+    normed_two_ref[block_rows(me)] = (mid * norm_scale(mid) * all_gains_ref[1:2]).astype(BF16)
+    second = Gather(me, lambda j: normed_two_ref.at[block_rows(j)], n_sends, n_recv)
+    second.step(0)
+    relay_x(2)
+    relay_y(1)
+    second.step(1)
+    relay_x(3)
+    relay_y(2)
+    second.step(2)
+    relay_x(4)
+    relay_y(3)
+    second.step(3)
+    cot_gather.step(1)
+    cot_gather.step(2)
+    relay_x(5)
+    relay_y(4)
+    cot_gather.step(3)
+    relay_y(5)
+    for i in range(PIECES):
+        for way in (2, 3):
+            of_y = y if way == 2 else 1 - y
+            landed(weights_other_hbm.at[i // 2, piece(i, of_y), its_rows], piece_recv.at[way, i])
+        for way in range(4):
+            piece_copy(i, way).wait_send()
+    for i in range(len(swaps)):
+        swap_copy(i).wait_send()
+    for j in range(LINE):
+        kv_copy(j).wait_send()
+    gather.drain()
+    cot_gather.drain()
+    second.drain()
+    scatter.drain()
+
+
+def front_call(proj_cols, query_cols, hidden, *args):
+    heads = query_cols // HEAD_SIZE
+    outs = [
+        shape(BLOCK, MODEL_WIDTH),
+        shape(LOCAL, MODEL_WIDTH),
+        shape(LOCAL, query_cols),
+        shape(LOCAL, 2 * HEAD_SIZE),
+        shape(LOCAL, 2 * HEAD_SIZE),
+        shape(LOCAL, HEAD_SIZE, F32),
+        shape(LOCAL, HEAD_SIZE, F32),
+        shape(8, MODEL_WIDTH, F32),
+        shape(LOCAL, query_cols),
+        jax.ShapeDtypeStruct((2 * heads, 2 * BLOCK, 4 * BLOCK), BF16),
+        shape(BLOCK, MODEL_WIDTH, F32),
+        shape(LOCAL, MODEL_WIDTH),
+        shape(LOCAL, MODEL_WIDTH),
+        shape(HALF, proj_cols + query_cols),
+        jax.ShapeDtypeStruct((3, hidden, HALF), BF16),
+    ]
+    dma = pltpu.SemaphoreType.DMA
+    return pl.pallas_call(
+        front_body,
+        out_shape=outs,
+        in_specs=[VMEM_SPEC] * 8 + [ANY_SPEC] * 3,
+        out_specs=[VMEM_SPEC] * (len(outs) - 1) + [ANY_SPEC],
+        scratch_shapes=[
+            pltpu.VMEM((2, 2 * BLOCK, HEAD_SIZE), F32),
+            pltpu.VMEM((LINE, BLOCK, MODEL_WIDTH), BF16),
+            pltpu.VMEM((LINE, BLOCK, MODEL_WIDTH), BF16),
+            dma((8,)),
+            dma((8,)),
+            dma((4, PIECES)),
+            dma((4, PIECES)),
+            dma((LINE,)),
+            dma((LINE,)),
+        ]
+        + [dma((2, LINE)), dma((LINE,))] * 3
+        + [dma((2, LINE)), dma((2, LINE))],
+        compiler_params=pltpu.CompilerParams(
+            collective_id=1, has_side_effects=True, vmem_limit_bytes=60 * 1024 * 1024
+        ),
+        cost_estimate=pl.CostEstimate(
+            flops=4 * 10**9, bytes_accessed=40_000_000, transcendentals=0
+        ),
+        name="front",
+    )(*args)
 
 
 def fast_device(
@@ -782,34 +1030,28 @@
     out_cotangent,
 ):
     r, c = lax.axis_index("row"), lax.axis_index("col")
-    core = lax.axis_index("dp") % 2
     query_cols = query_weight.shape[1]
     hidden = gate_weight.shape[1]
     proj_cols = query_cols + 2 * HEAD_SIZE
-    quarter = HALF // 2
     kv_head = c // (LINE // KEYVALUE_HEADS)
     key_start = kv_head * HEAD_SIZE
     value_start = (KEYVALUE_HEADS + kv_head) * HEAD_SIZE
 
-    def mine(values):
-        keep = lax.dynamic_slice_in_dim(values, r * BLOCK, BLOCK, 1).T
-        send = lax.dynamic_slice_in_dim(values, (1 - r) * BLOCK, BLOCK, 1).T
-        return jnp.concatenate([keep, swap(send, "row", 1)], 1)
-
-    x_own = mine(block_input)
-    small = jnp.concatenate([attention_gain, feedforward_gain, position_ids.astype(F32)])
-    got_small = swap(small, "row", 1)
-    attn_gain = jnp.concatenate([attention_gain, got_small[:HALF]])[None]
-    ffn_gain = jnp.concatenate([feedforward_gain, got_small[HALF : 2 * HALF]])[None]
-    own_ids, other_ids = small[2 * HALF :], got_small[2 * HALF :]
-    ids = jnp.stack([jnp.where(r == 0, own_ids, other_ids), jnp.where(r == 0, other_ids, own_ids)])
-    ids = lax.dynamic_index_in_dim(ids.reshape(2, 2, 2, BLOCK), r, 2, keepdims=False).reshape(LOCAL)
+    def parts(values):
+        turned = values.T.reshape(2, BLOCK, HALF)
+        pick = lambda i: lax.dynamic_index_in_dim(turned, i, 0, keepdims=False)
+        return pick(r), pick(1 - r)
+
+    x_keep, x_pass = parts(block_input)
+    cot_keep, cot_pass = parts(out_cotangent)
     frequencies = THETA ** (-(jnp.arange(HEAD_SIZE // 2, dtype=F32) * 2.0 / HEAD_SIZE))
-    angles = ids[:, None] * frequencies[None, :]
-    cosine, sine = jnp.cos(angles), jnp.sin(angles)
-    cosine = jnp.concatenate([cosine, cosine], -1)
-    sine = jnp.concatenate([-sine, sine], -1)
-
+    angles = position_ids.astype(F32)[:, None] * frequencies[None, :]
+    table = jnp.concatenate([jnp.cos(angles), jnp.sin(angles)], -1).reshape(2, 2, BLOCK, HEAD_SIZE)
+    pick = lambda i: lax.dynamic_index_in_dim(table, i, 1, keepdims=False)
+    table = jnp.stack([pick(r), pick(1 - r)]).reshape(2, 2 * BLOCK, HEAD_SIZE)
+    gains = jnp.concatenate(
+        [attention_gain[None], feedforward_gain[None], jnp.zeros((6, HALF), F32)]
+    )
     own_proj = jnp.concatenate(
         [
             query_weight,
@@ -826,72 +1068,34 @@
             lax.dynamic_slice_in_dim(key_value_bias, value_start, HEAD_SIZE, 0),
         ]
     )[None]
-    here = swap(lax.dynamic_slice_in_dim(own_proj, core * quarter, quarter, 0), "row", 1)
-    there = swap(here, "dp", 1)
-    other_proj = jnp.where(
-        core == 0, jnp.concatenate([here, there]), jnp.concatenate([there, here])
-    )
+    (
+        x_own, normed_one, query_rot, kv_own, kv_other, cosine, sine, all_gains, attended, probs,
+        mid, normed_two, cot_all, other_proj, ffn_other,
+    ) = front_call(
+        proj_cols, query_cols, hidden,
+        x_keep, x_pass, cot_keep, cot_pass, table, gains, proj_bias, own_proj,
+        gate_weight.T, upper_weight.T, down_weight.T,
+    )
+    attn_gain, ffn_gain = all_gains[:1], all_gains[1:2]
     own_in, own_out = own_proj[:, :proj_cols], own_proj[:, proj_cols:]
     other_in, other_out = other_proj[:, :proj_cols], other_proj[:, proj_cols:]
-
-    ffn_send = jnp.stack(
-        [
-            lax.dynamic_slice_in_dim(w, core * quarter, quarter, 0)
-            for w in (gate_weight, upper_weight, down_weight)
-        ]
-    )
-    ffn_other = swap(ffn_send, "row", 1)
-    ffn_partner = swap(ffn_other, "dp", 1)
-
-    normed_one, query_rot, kv_own = comm_call(
-        project_body,
-        [shape(LOCAL, MODEL_WIDTH), shape(LOCAL, query_cols), shape(LOCAL, 2 * HEAD_SIZE)],
-        7,
-        gather_scratch(),
-        1,
-        10**9,
-        "project",
-    )(x_own, attn_gain, own_in, other_in, proj_bias, cosine, sine)
-    kv_other = swap(kv_own, "row", 1)
-    heads = query_cols // HEAD_SIZE
-    attended, probs = pl.pallas_call(
-        attend_body,
-        out_shape=[
-            shape(LOCAL, query_cols),
-            jax.ShapeDtypeStruct((2 * heads, 2 * BLOCK, 4 * BLOCK), BF16),
-        ],
-        in_specs=[VMEM_SPEC] * 3,
-        out_specs=[VMEM_SPEC] * 2,
-        cost_estimate=pl.CostEstimate(flops=10**9, bytes_accessed=20_000_000, transcendentals=0),
-        name="attend",
-    )(query_rot, kv_own, kv_other)
-    cot_own = mine(out_cotangent)
-    cot_all = lax.all_gather(cot_own, "col", axis=0, tiled=True)
-    mid, normed_two = comm_call(
-        residual_body,
-        [shape(BLOCK, MODEL_WIDTH, F32), shape(LOCAL, MODEL_WIDTH)],
-        5,
-        scatter_scratch() + gather_scratch(),
-        2,
-        10**9,
-        "residual",
-    )(attended, own_out, other_out, x_own, ffn_gain)
+    cot_own = lax.dynamic_slice_in_dim(cot_all, c * BLOCK, BLOCK, 0)
     activated, gate_grad, upper_grad, back_part, out_part = pl.pallas_call(
         feed_body,
         out_shape=[shape(LOCAL, hidden)] * 3 + [shape(LOCAL, MODEL_WIDTH)] * 2,
-        in_specs=[VMEM_SPEC] * 2 + [ANY_SPEC] * 5,
+        in_specs=[VMEM_SPEC] * 2 + [ANY_SPEC] * 4,
         out_specs=[VMEM_SPEC] * 5,
         scratch_shapes=[
-            pltpu.VMEM((3, MODEL_WIDTH, hidden), BF16),
+            pltpu.VMEM((3, hidden, MODEL_WIDTH), BF16),
             pltpu.VMEM((LOCAL, MODEL_WIDTH), F32),
             pltpu.VMEM((LOCAL, MODEL_WIDTH), F32),
-            pltpu.SemaphoreType.DMA((3, 3)),
+            pltpu.SemaphoreType.DMA((8, 3, 2)),
         ],
         cost_estimate=pl.CostEstimate(
             flops=2 * 10**10, bytes_accessed=40_000_000, transcendentals=0
         ),
         name="feed",
-    )(normed_two, cot_all, gate_weight, upper_weight, down_weight, ffn_other, ffn_partner)
+    )(normed_two, cot_all, gate_weight.T, upper_weight.T, down_weight.T, ffn_other)
     out_own = lax.psum_scatter(out_part, "col", scatter_dimension=0, tiled=True).astype(F32) + mid
     down_grad = lax.dot_general(cot_all, activated, PAIR_ROWS, preferred_element_type=F32).astype(
         BF16

time: 763 us -> 644 us (0.84)
  waiting for transfers between devices: 227 us -> 99.5 us
  Pallas kernels: 262 us -> 311 us
  local copies, waits for them, and re-layouts: 105 us -> 72.1 us
  starting transfers between devices: 23.5 us -> 14.6 us
    ppermute x26 -> x18, waiting for transfers between devices: 227 us -> 99.5 us  [swap(): return lax.ppermute(values, axis, [(i, i ^ bit) for i in range(size)])]
    pallas_call x3 -> x1, Pallas kernels: 106 us -> 146 us  [front_call(): pl.pallas_call(front_body, out_shape=outs, in_specs=[VMEM_SPEC] * 8 + [AN...]
    unnamed x73 -> x42, local copies, waits for them, and re-layouts: 23.3 us -> 4.36 us
    ppermute x2 -> x0, local copies, waits for them, and re-layouts: 17.5 us -> none  [swap(): return lax.ppermute(values, axis, [(i, i ^ bit) for i in range(size)])]
    ppermute x26 -> x18, starting transfers between devices: 23.5 us -> 14.6 us  [swap(): return lax.ppermute(values, axis, [(i, i ^ bit) for i in range(size)])]
  transfers between devices with their start and end apart: 28 -> 19, of which waited for: 11 -> 8; matrix products, arithmetic and copies ran while one was open for 20% -> 18% of each run, Pallas kernels for 30% -> 20%
where the time goes in v2:
time: 644 us; the launch traced here: 634 us
  Pallas kernels  311 us (48%)
  waiting for transfers between devices  99.5 us (15%)
  local copies, waits for them, and re-layouts  72.1 us (11%)
  blocking collectives  64.4 us (10%)
  other arithmetic  31.9 us (5%)
  matrix products  25.8 us (4%)
  between operations  15 us (2%)
  starting transfers between devices  14.6 us (2%)
    pallas_call x1, Pallas kernels, front_call(): pl.pallas_call(front_body, out_shape=outs, in_specs=[VMEM_SPEC] * 8 + [AN...  146 us
    ppermute x18, waiting for transfers between devices, swap(): return lax.ppermute(values, axis, [(i, i ^ bit) for i in range(size)])  99.5 us
    pallas_call x1, Pallas kernels, fast_device(): comm_call(middle_back_body, [shape(BLOCK, MODEL_WIDTH, F32), shape(1, MOD...  85.6 us
    psum x1, blocking collectives, fast_device(): vector = lax.psum(vector, ('dp', 'row', 'col'))  40.6 us
    pallas_call x1, Pallas kernels, fast_device(): pl.pallas_call(feed_body, out_shape=[shape(LOCAL, hidden)] * 3 + [shape(L...  38.2 us
    pallas_call x1, Pallas kernels, fast_device(): comm_call(input_back_body, [shape(LOCAL, proj_cols), shape(1, proj_cols,...  35.6 us
    all_gather x1, blocking collectives, fast_device(): lax.all_gather(proj_sum[:, query_cols:].astype(BF16), 'col', axis=0, tile...  15.1 us
    ppermute x18, starting transfers between devices, swap(): return lax.ppermute(values, axis, [(i, i ^ bit) for i in range(size)])  14.6 us
  transfers between devices with their start and end apart: 19, of which 8 were waited for; matrix products, arithmetic and copies ran while one was open for 18% of the time, Pallas kernels for 20%

profile of v2, /device:TPU:0, one launch (start us, length us, event | category | flops | bytes accessed | tf_op | source)
XLA Modules:
  0.0 634.1 jit_solution(6037276442890228751)
XLA Ops:
  19.8 145.9 %front.1 = (bf16[128,1536]{1,0:T(8,128)(2,1)}, bf16[512,1536]{1,0:T(8,128)(2,1)}, bf16[512,384]{1,0:T(8,128)(2,1)}, bf16[512,256]{1,0:T(8,128)(2,1)}, bf16[512,2...) custom-call(bf16[128,768]{1,0:T(8,128)(2,1)} %get-tuple-element.144., ...), custom_call_target="tpu_custom_call" | custom-call | flops 4000000000 | bytes 40000000 | tf_op jit(solution)/shard_map/front/pallas_call | solution.py:989
  165.8 38.2 %feed.1 = (bf16[512,2240]{1,0:T(8,128)(2,1)}, bf16[512,2240]{1,0:T(8,128)(2,1)}, bf16[512,2240]{1,0:T(8,128)(2,1)}, bf16[512,1536]{1,0:T(8,128)(2,1)}, bf16[512,1536]{1,0:T(8,128)(2,1)}) custom-call(bf16[512,1536]{1,0:T(8,128)(2,1)} %get-tuple-element.43.normed_ref, bf16[512,1536]{1,0:T(8,128)(2,1)} %get-tuple-element.44.cot_ref, ...), custom_call_target="tpu_custom_call" | custom-call | flops 20000000000 | bytes 40000000 | tf_op jit(solution)/shard_map/feed/pallas_call | solution.py:1083
  208.3 85.6 %middle_back.1 = (f32[128,1536]{1,0:T(8,128)}, f32[1,1536]{1,0:T(1,128)}, bf16[512,1536]{1,0:T(8,128)(2,1)}, bf16[512,384]{1,0:T(8,128)(2,1)}) custom-call(bf16[512,1536]{1,0:T(8,128)(2,1)} %get-tuple-element.53.part_ref, f32[128,1536]{1,0:T(8,128)} %get-tuple-element.47.mid_ref, bf16[128,1536]{1,0:T(8,128)(2,1)} %constant_dynamic-slice_fusion.2.cot_ref, ...), custom_call_target="tpu_custom_call" | custom-call | flops 1000000000 | bytes 40000000 | tf_op jit(solution)/shard_map/middle_back/pallas_call | solution.py:1109
  293.9 5.4 attend_back.1
  305.1 7.6 %convolution_convert_fusion.2 = bf16[1536,2240]{0,1:T(8,128)(2,1)} fusion(bf16[512,1536]{1,0:T(8,128)(2,1)S(1)} %copy-done.12, bf16[512,2240]{1,0:T(8,128)(2,1)} %get-tuple-element.71), kind=kOutput, calls=%fused_computation.2 | convolution fusion | flops 3526656000 | bytes 10747904 | tf_op jit(solution)/shard_map/dot_general | solution.py:1103
  312.7 9.7 %copy.75 = bf16[1536,2240]{1,0:T(8,128)(2,1)} copy(bf16[1536,2240]{0,1:T(8,128)(2,1)} %convolution_convert_fusion.2) | data formatting | bytes 13762560 | tf_op jit(solution)/shard_map/convert_element_type | solution.py:1105
  322.4 4.1 dynamic-slice_bitcast_fusion.2
  327.1 5.8 convolution_convert_fusion.1
  332.9 9.6 %copy.76 = bf16[1536,2240]{1,0:T(8,128)(2,1)} copy(bf16[1536,2240]{0,1:T(8,128)(2,1)} %convolution_convert_fusion.1) | data formatting | bytes 13762560 | tf_op jit(solution)/shard_map/convert_element_type | solution.py:1108
  342.5 4.2 dynamic-slice_bitcast_fusion.1
  347.8 5.9 convolution_convert_fusion
  353.7 9.9 %copy.77 = bf16[1536,2240]{1,0:T(8,128)(2,1)} copy(bf16[1536,2240]{0,1:T(8,128)(2,1)} %convolution_convert_fusion) | data formatting | bytes 13762560 | tf_op jit(solution)/shard_map/convert_element_type | solution.py:1100
  363.6 4.0 dynamic-slice_bitcast_fusion
  369.5 35.6 %input_back.1 = (bf16[512,640]{1,0:T(8,128)(2,1)}, f32[1,640]{1,0:T(1,128)}, f32[128,1536]{1,0:T(8,128)}, f32[1,1536]{1,0:T(1,128)}) custom-call(bf16[512,384]{1,0:T(8,128)(2,1)} %get-tuple-element.59.query_grad_ref, f32[512,256]{1,0:T(8,128)} %get-tuple-element.60.own_kv_ref, bf16[512,256]{1,0:T(8,128)(2,1)} %copy-done.6, ...), custom_call_target="tpu_custom_call" | custom-call | flops 1000000000 | bytes 40000000 | tf_op jit(solution)/shard_map/input_back/pallas_call | solution.py:1139
  418.5 40.6 %psum.7 = f32[5120]{0:T(1024)} all-reduce(f32[5120]{0:T(1024)} %pad_maximum_fusion.3), channel_id=1, replica_groups=mesh['dp'=4,'row'=2,'col'=4] {'dp','row','col'}, use_global_device_ids=true, to_apply=%region_1.2 | all-reduce | flops 5120 | bytes 40960 | tf_op jit(solution)/shard_map/psum | solution.py:1184
  471.2 5.7 collective-permute-done.4
  479.4 3.9 collective-permute-done.5
  484.2 15.1 %all-gather = bf16[768,256]{1,0:T(8,128)(2,1)S(1)} all-gather(bf16[192,256]{1,0:T(8,128)(2,1)S(1)} %slice.183), channel_id=2, replica_groups=mesh['dp'=4,'row'=2,'col'=4] {'col'}, dimensions={0}, use_global_device_ids=true | all-gather | bytes 491520 | tf_op jit(solution)/shard_map/all_gather | solution.py:1166
  502.3 8.7 %all_gather.11 = bf16[768,512]{1,0:T(8,128)(2,1)S(1)} all-gather(bf16[192,512]{1,0:T(8,128)(2,1)S(1)} %convert_element_type.233), channel_id=1, replica_groups=mesh['dp'=4,'row'=2,'col'=4] {'dp'}, dimensions={0}, use_global_device_ids=true | all-gather | bytes 983040 | tf_op jit(solution)/shard_map/all_gather | solution.py:1170
  515.8 4.0 fusion.2
  530.7 31.6 %collective-permute-done.10 = bf16[2,192,2240]{2,1,0:T(8,128)(2,1)S(1)} collective-permute-done((bf16[2,192,2240]{2,1,0:T(8,128)(2,1)}, bf16[2,192,2240]{2,1,0:T(8,128)(2,1)S(1)}, u32[]{:S(2)}, u32[]{:S(2)}) %collective-permute-start.10) | collective-permute-done | bytes 1720352 | tf_op jit(solution)/shard_map/ppermute | solution.py:759
  563.3 3.7 collective-permute-done.13
  568.3 36.6 %collective-permute-done.16 = bf16[2,192,2240]{2,1,0:T(8,128)(2,1)S(1)} collective-permute-done((bf16[2,192,2240]{2,1,0:T(8,128)(2,1)S(1)}, bf16[2,192,2240]{2,1,0:T(8,128)(2,1)S(1)}, u32[]{:S(2)}, u32[]{:S(2)}) %collective-permute-start.16) | collective-permute-done | bytes 1720352 | tf_op jit(solution)/shard_map/ppermute | solution.py:759
  607.6 15.4 %collective-permute-done.11 = bf16[192,2240]{1,0:T(8,128)(2,1)S(1)} collective-permute-done((bf16[192,2240]{1,0:T(8,128)(2,1)S(1)}, bf16[192,2240]{1,0:T(8,128)(2,1)S(1)}, u32[]{:S(2)}, u32[]{:S(2)}) %collective-permute-start.11) | collective-permute-done | bytes 860192 | tf_op jit(solution)/shard_map/ppermute | solution.py:759
  (162 shorter events, 82.1 us)
Async XLA Ops:
  7.2 493.5 %reduce-scatter.2.cloned.1.call-start = ((), (), s32[]{:S(2)}) async-start(), calls=%async_computation.1 | async-start | bytes 1966080 | tf_op jit(solution)/shard_map/reduce_scatter | solution.py:1099
  8.4 10.0 %copy-start.1 = (bf16[768,384]{1,0:T(8,128)(2,1)S(1)}, bf16[768,384]{1,0:T(8,128)(2,1)}, u32[]{:S(2)}) copy-start(bf16[768,384]{1,0:T(8,128)(2,1)} %own_ref.1) | copy-start | bytes 1769476
  8.5 10.0 %copy-start.2 = (bf16[768,384]{1,0:T(8,128)(2,1)S(1)}, bf16[768,384]{1,0:T(8,128)(2,1)}, u32[]{:S(2)}) copy-start(bf16[768,384]{1,0:T(8,128)(2,1)} %param.16) | copy-start | bytes 1769476
  299.3 69.5 %collective-permute-start.1 = (bf16[512,256]{1,0:T(8,128)(2,1)}, bf16[512,256]{1,0:T(8,128)(2,1)S(1)}, u32[]{:S(2)}, u32[]{:S(2)}) collective-permute-start(bf16[512,256]{1,0:T(8,128)(2,1)} %get-tuple-element.61), channel_id=1, source_target_pairs={{0,4},{4,0},{1,5},{5,1},{2,6},{6,2},{3,7},{7,3},{8,12},{12,8},{9,1... | collective-permute-start | bytes 786440 | tf_op jit(solution)/shard_map/ppermute | solution.py:759
  305.1 153.9 %collective-permute-start.6 = (bf16[2,2,192,384]{3,2,0,1:T(8,128)(2,1)}, bf16[2,2,192,384]{3,2,0,1:T(8,128)(2,1)}, u32[]{:S(2)}, u32[]{:S(2)}) collective-permute-start(bf16[2,2,192,384]{3,2,0,1:T(8,128)(2,1)} %bitcast.131), channel_id=1, source_target_pairs={{0,8},{8,0},{16,24},{24,16},{1,9},{9,1},{17,25},{25,17},{2,10},{10... | collective-permute-start | bytes 1769480 | tf_op jit(solution)/shard_map/ppermute | solution.py:759
  326.6 189.3 %collective-permute-start.9 = (bf16[2,2,192,2240]{3,2,1,0:T(8,128)(2,1)}, bf16[2,2,192,2240]{3,2,1,0:T(8,128)(2,1)}, u32[]{:S(2)}, u32[]{:S(2)}) collective-permute-start(bf16[2,2,192,2240]{3,2,1,0:T(8,128)(2,1)} %dynamic-slice_bitcast_fusion.2), channel_id=1, source_target_pairs={{0,8},{8,0},{16,24},{24,16},{1,9},{9,1},{17,25},{25,17},{2,10},{10... | collective-permute-start | bytes 10321928 | tf_op jit(solution)/shard_map/ppermute | solution.py:759
  346.7 175.2 %collective-permute-start.12 = (bf16[2,2,192,2240]{3,2,1,0:T(8,128)(2,1)}, bf16[2,2,192,2240]{3,2,1,0:T(8,128)(2,1)}, u32[]{:S(2)}, u32[]{:S(2)}) collective-permute-start(bf16[2,2,192,2240]{3,2,1,0:T(8,128)(2,1)} %dynamic-slice_bitcast_fusion.1), channel_id=1, source_target_pairs={{0,8},{8,0},{16,24},{24,16},{1,9},{9,1},{17,25},{25,17},{2,10},{10... | collective-permute-start | bytes 10321928 | tf_op jit(solution)/shard_map/ppermute | solution.py:759
  406.8 60.0 %collective-permute-start.2 = (bf16[128,768]{1,0:T(8,128)(2,1)}, bf16[128,768]{1,0:T(8,128)(2,1)}, u32[]{:S(2)}, u32[]{:S(2)}) collective-permute-start(bf16[128,768]{1,0:T(8,128)(2,1)} %slice.181), channel_id=1, source_target_pairs={{0,4},{4,0},{1,5},{5,1},{2,6},{6,2},{3,7},{7,3},{8,12},{12,8},{9,1... | collective-permute-start | bytes 589832 | tf_op jit(solution)/shard_map/ppermute | solution.py:759
  412.9 50.1 %collective-permute-start.3 = (bf16[2,2,192,640]{3,2,1,0:T(8,128)(2,1)}, bf16[2,2,192,640]{3,2,1,0:T(8,128)(2,1)S(1)}, u32[]{:S(2)}, u32[]{:S(2)}) collective-permute-start(bf16[2,2,192,640]{3,2,1,0:T(8,128)(2,1)} %dynamic-slice_bitcast_fusion.4), channel_id=1, source_target_pairs={{0,8},{8,0},{16,24},{24,16},{1,9},{9,1},{17,25},{25,17},{2,10},{10... | collective-permute-start | bytes 2949128 | tf_op jit(solution)/shard_map/ppermute | solution.py:759
  460.3 9.0 %collective-permute-start.7 = (bf16[2,192,384]{2,1,0:T(8,128)(2,1)S(1)}, bf16[2,192,384]{2,1,0:T(8,128)(2,1)S(1)}, u32[]{:S(2)}, u32[]{:S(2)}) collective-permute-start(bf16[2,192,384]{2,1,0:T(8,128)(2,1)S(1)} %dynamic-slice_bitcast_fusion.7), channel_id=1, source_target_pairs={{0,16},{8,24},{16,0},{24,8},{1,17},{9,25},{17,1},{25,9},{2,18},{10... | collective-permute-start | bytes 884744 | tf_op jit(solution)/shard_map/ppermute | solution.py:759
  463.3 13.6 %collective-permute-start.4 = (bf16[2,192,640]{2,1,0:T(8,128)(2,1)S(1)}, bf16[2,192,640]{2,1,0:T(8,128)(2,1)S(1)}, u32[]{:S(2)}, u32[]{:S(2)}) collective-permute-start(bf16[2,192,640]{2,1,0:T(8,128)(2,1)S(1)} %slice_bitcast_fusion.6), channel_id=1, source_target_pairs={{0,4},{4,0},{1,5},{5,1},{2,6},{6,2},{3,7},{7,3},{8,12},{12,8},{9,1... | collective-permute-start | bytes 1474568 | tf_op jit(solution)/shard_map/ppermute | solution.py:759
  466.8 59.6 %collective-permute-start.15 = (bf16[2,2,192,2240]{3,2,1,0:T(8,128)(2,1)}, bf16[2,2,192,2240]{3,2,1,0:T(8,128)(2,1)}, u32[]{:S(2)}, u32[]{:S(2)}) collective-permute-start(bf16[2,2,192,2240]{3,2,1,0:T(8,128)(2,1)} %dynamic-slice_bitcast_fusion), channel_id=1, source_target_pairs={{0,8},{8,0},{16,24},{24,16},{1,9},{9,1},{17,25},{25,17},{2,10},{10... | collective-permute-start | bytes 10321928 | tf_op jit(solution)/shard_map/ppermute | solution.py:759
  469.4 9.3 %collective-permute-start.8 = (bf16[192,384]{1,0:T(8,128)(2,1)S(1)}, bf16[192,384]{1,0:T(8,128)(2,1)S(1)}, u32[]{:S(2)}, u32[]{:S(2)}) collective-permute-start(bf16[192,384]{1,0:T(8,128)(2,1)S(1)} %slice_bitcast_fusion.8), channel_id=1, source_target_pairs={{0,4},{4,0},{1,5},{5,1},{2,6},{6,2},{3,7},{7,3},{8,12},{12,8},{9,1... | collective-permute-start | bytes 442376 | tf_op jit(solution)/shard_map/ppermute | solution.py:759
  477.1 6.3 collective-permute-start.5
  479.4 21.2 %copy-start = (f32[128,1536]{1,0:T(8,128)S(1)}, f32[128,1536]{1,0:T(8,128)}, u32[]{:S(2)}) copy-start(f32[128,1536]{1,0:T(8,128)} %get-tuple-element.47.mid_ref) | copy-start | bytes 2359300
  501.8 10.7 %collective-permute-start = (bf16[128,768]{1,0:T(8,128)(2,1)S(1)}, bf16[128,768]{1,0:T(8,128)(2,1)S(1)}, u32[]{:S(2)}, u32[]{:S(2)}) collective-permute-start(bf16[128,768]{1,0:T(8,128)(2,1)S(1)} %slice.182), channel_id=1, source_target_pairs={{0,4},{4,0},{1,5},{5,1},{2,6},{6,2},{3,7},{7,3},{8,12},{12,8},{9,1... | collective-permute-start | bytes 589832 | tf_op jit(solution)/shard_map/ppermute | solution.py:759
  513.4 8.5 %slice-start = ((s8[7077888]{0:T(1024)(128)(4,1)}), s8[2883584]{0:T(1024)(128)(4,1)S(1)}, s32[]{:S(2)}) async-start(s8[7077888]{0:T(1024)(128)(4,1)} %bitcast.133), calls=%async_computation.2 | async-start | bytes 5767168
  519.9 6.6 %slice-start.2 = ((s8[7077888]{0:T(1024)(128)(4,1)}), s8[4194304]{0:T(1024)(128)(4,1)S(1)}, s32[]{:S(2)}) async-start(s8[7077888]{0:T(1024)(128)(4,1)} %bitcast.137), calls=%async_computation.4 | async-start | bytes 8388608
  521.2 41.1 %collective-permute-start.10 = (bf16[2,192,2240]{2,1,0:T(8,128)(2,1)}, bf16[2,192,2240]{2,1,0:T(8,128)(2,1)S(1)}, u32[]{:S(2)}, u32[]{:S(2)}) collective-permute-start(bf16[2,192,2240]{2,1,0:T(8,128)(2,1)} %dynamic-slice_bitcast_fusion.3), channel_id=1, source_target_pairs={{0,16},{8,24},{16,0},{24,8},{1,17},{9,25},{17,1},{25,9},{2,18},{10... | collective-permute-start | bytes 5160968 | tf_op jit(solution)/shard_map/ppermute | solution.py:759
  525.5 41.5 %collective-permute-start.13 = (bf16[2,192,2240]{2,1,0:T(8,128)(2,1)S(1)}, bf16[2,192,2240]{2,1,0:T(8,128)(2,1)S(1)}, u32[]{:S(2)}, u32[]{:S(2)}) collective-permute-start(bf16[2,192,2240]{2,1,0:T(8,128)(2,1)S(1)} %slice_bitcast_fusion.2), channel_id=1, source_target_pairs={{0,4},{4,0},{1,5},{5,1},{2,6},{6,2},{3,7},{7,3},{8,12},{12,8},{9,1... | collective-permute-start | bytes 5160968 | tf_op jit(solution)/shard_map/ppermute | solution.py:759
  529.5 75.4 %collective-permute-start.16 = (bf16[2,192,2240]{2,1,0:T(8,128)(2,1)S(1)}, bf16[2,192,2240]{2,1,0:T(8,128)(2,1)S(1)}, u32[]{:S(2)}, u32[]{:S(2)}) collective-permute-start(bf16[2,192,2240]{2,1,0:T(8,128)(2,1)S(1)} %slice_bitcast_fusion), channel_id=1, source_target_pairs={{0,4},{4,0},{1,5},{5,1},{2,6},{6,2},{3,7},{7,3},{8,12},{12,8},{9,1... | collective-permute-start | bytes 5160968 | tf_op jit(solution)/shard_map/ppermute | solution.py:759
  562.8 60.2 %collective-permute-start.11 = (bf16[192,2240]{1,0:T(8,128)(2,1)S(1)}, bf16[192,2240]{1,0:T(8,128)(2,1)S(1)}, u32[]{:S(2)}, u32[]{:S(2)}) collective-permute-start(bf16[192,2240]{1,0:T(8,128)(2,1)S(1)} %slice_bitcast_fusion.4), channel_id=1, source_target_pairs={{0,4},{4,0},{1,5},{5,1},{2,6},{6,2},{3,7},{7,3},{8,12},{12,8},{9,1... | collective-permute-start | bytes 2580488 | tf_op jit(solution)/shard_map/ppermute | solution.py:759
  567.5 38.7 %collective-permute-start.14 = (bf16[192,2240]{1,0:T(8,128)(2,1)S(1)}, bf16[192,2240]{1,0:T(8,128)(2,1)S(1)}, u32[]{:S(2)}, u32[]{:S(2)}) collective-permute-start(bf16[192,2240]{1,0:T(8,128)(2,1)S(1)} %dynamic-slice_bitcast_fusion.6), channel_id=1, source_target_pairs={{0,16},{8,24},{16,0},{24,8},{1,17},{9,25},{17,1},{25,9},{2,18},{10... | collective-permute-start | bytes 2580488 | tf_op jit(solution)/shard_map/ppermute | solution.py:759
  605.5 20.0 %collective-permute-start.17 = (bf16[192,2240]{1,0:T(8,128)(2,1)S(1)}, bf16[192,2240]{1,0:T(8,128)(2,1)S(1)}, u32[]{:S(2)}, u32[]{:S(2)}) collective-permute-start(bf16[192,2240]{1,0:T(8,128)(2,1)S(1)} %dynamic-slice_bitcast_fusion.5), channel_id=1, source_target_pairs={{0,16},{8,24},{16,0},{24,8},{1,17},{9,25},{17,1},{25,9},{2,18},{10... | collective-permute-start | bytes 2580488 | tf_op jit(solution)/shard_map/ppermute | solution.py:759
  (15 other events, 61.7 us)
Sparse Core Ops, SparseCore 0:
  204.1 58.8 reduce-scatter.1

commit v3 on v0

--- a/solution.py
+++ b/solution.py
@@ -1,6 +1,8 @@
 import jax
 import jax.numpy as jnp
 from jax import lax
+from jax.experimental import pallas as pl
+from jax.experimental.pallas import tpu as pltpu
 from jax.sharding import PartitionSpec as P
 
 MODEL_WIDTH = 1536
@@ -145,7 +147,7 @@
     return (query_grad, key_grad, value_grad)
 
 
-def per_device(
+def general_device(
     block_input,
     position_ids,
     attention_gain,
@@ -322,6 +324,1290 @@
     )
 
 
+MESH_ID = pl.DeviceIdType.MESH
+F32 = jnp.float32
+BF16 = jnp.bfloat16
+LINE = 4
+BLOCK = 128
+SUB = 2
+PART = BLOCK // SUB
+LOCAL = LINE * BLOCK
+HALF = MODEL_WIDTH // 2
+UNIT = MODEL_WIDTH // 8
+VMEM_SPEC = pl.BlockSpec(memory_space=pltpu.VMEM)
+ANY_SPEC = pl.BlockSpec(memory_space=pl.ANY)
+PAIR_ROWS = (((0,), (0,)), ((), ()))
+PAIR_COLS = (((1,), (1,)), ((), ()))
+SCALE = HEAD_SIZE ** (-0.5)
+DMA = pltpu.SemaphoreType.DMA
+
+
+def greet(me, others):
+    barrier = pltpu.get_barrier_semaphore()
+    for axis, index in others:
+        pl.semaphore_signal(barrier, 1, device_id={axis: index}, device_id_type=MESH_ID)
+
+    @pl.when(me > 0)
+    def _():
+        pl.semaphore_signal(barrier, 1, device_id={"col": me - 1}, device_id_type=MESH_ID)
+
+    @pl.when(me < LINE - 1)
+    def _():
+        pl.semaphore_signal(barrier, 1, device_id={"col": me + 1}, device_id_type=MESH_ID)
+
+    @pl.when((me > 0) & (me < LINE - 1))
+    def _():
+        pl.semaphore_wait(barrier, 2 + len(others))
+
+    @pl.when((me == 0) | (me == LINE - 1))
+    def _():
+        pl.semaphore_wait(barrier, 1 + len(others))
+
+
+def aligned(start, size, to=BLOCK):
+    return pl.ds(pl.multiple_of(start, to), size)
+
+
+def block_rows(index):
+    return aligned(index * BLOCK, BLOCK)
+
+
+def send(src, dst, send_sem, recv_sem, axis, to):
+    return pltpu.make_async_remote_copy(
+        src, dst, send_sem, recv_sem, device_id={axis: to}, device_id_type=MESH_ID
+    )
+
+
+def landed(ref, sem):
+    pltpu.make_async_copy(ref, ref, sem).wait()
+
+
+class Gather:
+    def __init__(self, me, all_ref, sends, recv):
+        self.me, self.all_ref, self.sends, self.recv = me, all_ref, sends, recv
+
+    def rows(self, j, p):
+        return self.all_ref.at[aligned(j * BLOCK + p * PART, PART, PART)]
+
+    def copy(self, j, p, s, side):
+        rows = self.rows(j, p)
+        return send(
+            rows, rows, self.sends.at[side, s, p], self.recv.at[j, p], "col",
+            self.me + 1 - 2 * side,
+        )
+
+    def has_next(self, side):
+        to = self.me + 1 - 2 * side
+        return (to >= 0) & (to < LINE)
+
+    def step(self, s, wait=True, forward=True):
+        @pl.loop(0, 2 * SUB)
+        def _(i):
+            side, p = lax.rem(i, 2), i // 2
+            j = self.me - (1 - 2 * side) * s
+
+            @pl.when((j >= 0) & (j < LINE))
+            def _():
+                if s and wait:
+                    landed(self.rows(j, p), self.recv.at[j, p])
+
+                if forward and s < LINE - 1:
+
+                    @pl.when(self.has_next(side))
+                    def _():
+                        self.copy(j, p, s, side).start()
+
+    def run_each(self, s, each):
+        if s == 0:
+            each(self.me)
+            return
+
+        @pl.loop(0, 2)
+        def _(side):
+            j = self.me - (1 - 2 * side) * s
+
+            @pl.when((j >= 0) & (j < LINE))
+            def _():
+                each(j)
+
+    def drain(self, first=0, last=LINE - 1):
+        for s in range(first, last):
+
+            @pl.loop(0, 2)
+            def _(side):
+                j = self.me - (1 - 2 * side) * s
+
+                @pl.when((j >= 0) & (j < LINE) & self.has_next(side))
+                def _():
+                    for p in range(SUB):
+                        self.copy(self.me, p, s, side).wait_send()
+
+
+class Scatter:
+    def __init__(self, me, block_of, landing, sends, recv):
+        self.me, self.block_of, self.landing = me, block_of, landing
+        self.sends, self.recv = sends, recv
+
+    def rows(self, side, j, p):
+        return self.landing.at[side, j, pl.ds(p * PART, PART)]
+
+    def copy(self, side, j, p):
+        rows = self.rows(side, j, p)
+        return send(
+            rows, rows, self.sends.at[side, j, p], self.recv.at[side, j, p], "col",
+            self.me + 1 - 2 * side,
+        )
+
+    def has_last(self, side):
+        came = self.me - 1 + 2 * side
+        return (came >= 0) & (came < LINE)
+
+    def step(self, s):
+        @pl.loop(0, 2)
+        def _(side):
+            j = self.me + (1 - 2 * side) * s
+
+            @pl.when((j >= 0) & (j < LINE))
+            def _():
+                mine = self.block_of(j)
+                for p in range(SUB):
+                    term = mine[p * PART : (p + 1) * PART]
+                    rows = self.rows(side, j, p)
+
+                    @pl.when(self.has_last(side))
+                    def _():
+                        landed(rows, self.recv.at[side, j, p])
+                        rows[...] = (term + rows[...].astype(F32)).astype(BF16)
+
+                    @pl.when(jnp.logical_not(self.has_last(side)))
+                    def _():
+                        rows[...] = term.astype(BF16)
+
+                    self.copy(side, j, p).start()
+
+    def finish(self, out_ref):
+        me = self.me
+        out_ref[...] = self.block_of(me)
+
+        @pl.loop(0, 2)
+        def _(side):
+            @pl.when(self.has_last(side))
+            def _():
+                for p in range(SUB):
+                    rows = self.rows(side, me, p)
+                    landed(rows, self.recv.at[side, me, p])
+                    out_ref[p * PART : (p + 1) * PART] += rows[...].astype(F32)
+
+    def drain(self):
+        for s in range(1, LINE):
+
+            @pl.loop(0, 2)
+            def _(side):
+                j = self.me + (1 - 2 * side) * s
+
+                @pl.when((j >= 0) & (j < LINE))
+                def _():
+                    for p in range(SUB):
+                        self.copy(side, j, p).wait_send()
+
+
+def gather_sems():
+    return [DMA((2, LINE, SUB)), DMA((LINE, SUB))]
+
+
+def scatter_sems():
+    return [DMA((2, LINE, SUB)), DMA((2, LINE, SUB))]
+
+
+def dot(a, b, dims=(((1,), (0,)), ((), ()))):
+    return lax.dot_general(a, b, dims, preferred_element_type=F32)
+
+
+def turn(values):
+    return pltpu.roll(values, HEAD_SIZE // 2, 1)
+
+
+def norm_scale(values):
+    return lax.rsqrt(jnp.sum(values * values, -1, keepdims=True) / MODEL_WIDTH + EPS)
+
+
+def shape(rows, cols, dtype=BF16):
+    return jax.ShapeDtypeStruct((rows, cols), dtype)
+
+
+def attend_local(query_ref, own_ref, other_ref, attended_ref, probs_ref, r):
+    rows = 2 * BLOCK
+    shape = (rows, rows)
+    at_row = lax.broadcasted_iota(jnp.int32, shape, 0)
+    at_col = lax.broadcasted_iota(jnp.int32, shape, 1)
+    own_mask = at_row >= at_col
+    other_mask = at_col // BLOCK < at_row // BLOCK + r
+    heads = query_ref.shape[1] // HEAD_SIZE
+    for s in range(2):
+        part = slice(s * rows, (s + 1) * rows)
+        for h in range(heads):
+            cols = slice(h * HEAD_SIZE, (h + 1) * HEAD_SIZE)
+            query = query_ref[part, cols]
+            own = jnp.where(own_mask, dot(query, own_ref[part, :HEAD_SIZE], PAIR_COLS) * SCALE, NEG)
+            other = jnp.where(
+                other_mask, dot(query, other_ref[part, :HEAD_SIZE], PAIR_COLS) * SCALE, NEG
+            )
+            top = jnp.maximum(
+                jnp.max(own, -1, keepdims=True), jnp.max(other, -1, keepdims=True)
+            )
+            total = jnp.sum(jnp.exp(own - top), -1, keepdims=True) + jnp.sum(
+                jnp.exp(other - top), -1, keepdims=True
+            )
+            log_total = top + jnp.log(total)
+            own = jnp.exp(own - log_total).astype(BF16)
+            other = jnp.exp(other - log_total).astype(BF16)
+            attended_ref[part, cols] = (
+                dot(own, own_ref[part, HEAD_SIZE:]) + dot(other, other_ref[part, HEAD_SIZE:])
+            ).astype(BF16)
+            probs_ref[s * heads + h, :, :rows] = own
+            probs_ref[s * heads + h, :, rows:] = other
+
+
+def attend_back_body(
+    query_ref, own_ref, other_ref, attended_ref, probs_ref, grad_ref, cos_ref, sin_ref,
+    query_grad_ref, own_grad_ref, other_grad_ref,
+):
+    rows = 2 * BLOCK
+    heads = query_ref.shape[1] // HEAD_SIZE
+    for s in range(2):
+        part = slice(s * rows, (s + 1) * rows)
+        own_key, other_key = own_ref[part, :HEAD_SIZE], other_ref[part, :HEAD_SIZE]
+        own_value, other_value = own_ref[part, HEAD_SIZE:], other_ref[part, HEAD_SIZE:]
+        sums = [jnp.zeros((rows, HEAD_SIZE), F32) for _ in range(4)]
+        for h in range(heads):
+            cols = slice(h * HEAD_SIZE, (h + 1) * HEAD_SIZE)
+            query, grad = query_ref[part, cols], grad_ref[part, cols]
+            own_p = probs_ref[s * heads + h, :, :rows]
+            other_p = probs_ref[s * heads + h, :, rows:]
+            delta = jnp.sum(
+                grad.astype(F32) * attended_ref[part, cols].astype(F32), -1, keepdims=True
+            )
+            own_s = (own_p.astype(F32) * (dot(grad, own_value, PAIR_COLS) - delta)).astype(BF16)
+            other_s = (other_p.astype(F32) * (dot(grad, other_value, PAIR_COLS) - delta)).astype(BF16)
+            query_grad = (dot(own_s, own_key) + dot(other_s, other_key)) * SCALE
+            query_grad_ref[part, cols] = (
+                query_grad * cos_ref[part] - turn(query_grad) * sin_ref[part]
+            ).astype(BF16)
+            for i, (weights, partner) in enumerate(
+                ((own_s, query), (own_p, grad), (other_s, query), (other_p, grad))
+            ):
+                sums[i] = sums[i] + dot(weights, partner, PAIR_ROWS)
+        own_grad_ref[part, :HEAD_SIZE] = sums[0] * SCALE
+        own_grad_ref[part, HEAD_SIZE:] = sums[1]
+        other_grad_ref[part, :HEAD_SIZE] = (sums[2] * SCALE).astype(BF16)
+        other_grad_ref[part, HEAD_SIZE:] = sums[3].astype(BF16)
+
+
+PIECES = 6
+
+
+def front_body(
+    input_ref, cot_in_ref, table_ref, small_ref, query_w_ref, kv_w_ref, output_w_ref,
+    gate_hbm, upper_hbm, down_hbm,
+    x_ref, normed_ref, query_ref, kv_ref, kv_other_ref, cos_ref, sin_ref, gains_ref,
+    attended_ref, probs_ref, mid_ref, normed_two_ref, turned_ref, cot_ref, proj_ref, proj_other_ref, weights_other_hbm,
+    passing, tables, bias_ref, landing,
+    swap_sends, swap_recv, piece_sends, piece_recv, kv_sends, kv_recv,
+    g_sends, g_recv, c_sends, c_recv, n_sends, n_recv, s_sends, s_recv,
+):
+    me, r, d = lax.axis_index("col"), lax.axis_index("row"), lax.axis_index("dp")
+    y, core = d // 2, lax.rem(d, 2)
+    x_to, y_to, core_to = 1 - r, 2 * (1 - y) + core, 2 * y + 1 - core
+    query_cols = query_ref.shape[1]
+    proj_cols = query_cols + 2 * HEAD_SIZE
+    quarter = HALF // 2
+    my_rows = aligned(core * quarter, quarter, quarter)
+    its_rows = aligned((1 - core) * quarter, quarter, quarter)
+    eighth = quarter // 2
+    to_y = aligned(core * quarter + y * eighth, eighth, eighth)
+    in_cols, out_cols = pl.ds(0, proj_cols), pl.ds(proj_cols, query_cols)
+    kv_width = KEYVALUE_HEADS * HEAD_SIZE
+    kv_at = me // (LINE // KEYVALUE_HEADS) * HEAD_SIZE
+
+    passing[0] = input_ref[:, block_rows(1 - r)].T
+    x_ref[:, :HALF] = input_ref[:, block_rows(r)].T
+    proj_ref[:, :query_cols] = query_w_ref[...]
+    for i in range(2):
+        proj_ref[:, query_cols + i * HEAD_SIZE : query_cols + (i + 1) * HEAD_SIZE] = kv_w_ref[
+            :, aligned(i * kv_width + kv_at, HEAD_SIZE)
+        ]
+    greet(me, [("row", x_to), ("dp", y_to), ("dp", core_to)])
+
+    swaps = [
+        (passing.at[0], x_ref.at[:, HALF:], "row", x_to),
+        (small_ref.at[:, :HALF], gains_ref.at[pl.ds(0, 1), HALF:], "row", x_to),
+        (small_ref.at[:, HALF : 2 * HALF], gains_ref.at[pl.ds(1, 1), HALF:], "row", x_to),
+        (proj_ref.at[to_y, in_cols], proj_other_ref.at[to_y, in_cols], "row", x_to),
+        (table_ref.at[block_rows(1 - r)], tables.at[pl.ds(0, BLOCK)], "row", x_to),
+        (table_ref.at[block_rows(3 - r)], tables.at[pl.ds(BLOCK, BLOCK)], "row", x_to),
+        (passing.at[1], cot_ref.at[block_rows(me), HALF:], "row", x_to),
+        (proj_ref.at[to_y, out_cols], proj_other_ref.at[to_y, out_cols], "row", x_to),
+        (proj_other_ref.at[to_y, in_cols], proj_other_ref.at[to_y, in_cols], "dp", y_to),
+        (proj_other_ref.at[to_y, out_cols], proj_other_ref.at[to_y, out_cols], "dp", y_to),
+        (proj_other_ref.at[my_rows, in_cols], proj_other_ref.at[my_rows, in_cols], "dp", core_to),
+        (proj_other_ref.at[my_rows, out_cols], proj_other_ref.at[my_rows, out_cols], "dp", core_to),
+    ]
+
+    def swap_copy(i):
+        src, dst, axis, to = swaps[i]
+        return send(src, dst, swap_sends.at[i], swap_recv.at[i], axis, to)
+
+    def swap_landed(i):
+        swap_copy(i).wait_recv()
+
+    rows = gate_hbm.shape[0] // 4
+    owns = (gate_hbm, upper_hbm, down_hbm)
+
+    def piece(i, of_y):
+        return aligned((of_y * 2 + i % 2) * rows, rows, rows)
+
+    def piece_copy(i, way):
+        m = i // 2
+        of_y = 1 - y if way == 3 else y
+        at = weights_other_hbm.at[m, piece(i, of_y), my_rows]
+        src = owns[m].at[piece(i, of_y), my_rows] if way == 0 else at
+        axis, to = (("row", x_to), ("dp", y_to), ("dp", core_to), ("dp", core_to))[way]
+        return send(src, at, piece_sends.at[way, i], piece_recv.at[way, i], axis, to)
+
+    def relay_x(i):
+        piece_copy(i, 0).wait_recv()
+        piece_copy(i, 1).start()
+        piece_copy(i, 2).start()
+
+    def relay_y(i):
+        piece_copy(i, 1).wait_recv()
+        piece_copy(i, 3).start()
+
+    for i in range(6):
+        swap_copy(i).start()
+    passing[1] = cot_in_ref[:, block_rows(1 - r)].T
+    proj_ref[:, proj_cols:] = output_w_ref[...]
+    swap_copy(6).start()
+    swap_copy(7).start()
+    cot_ref[block_rows(me), :HALF] = cot_in_ref[:, block_rows(r)].T
+    gains_ref[0:1, :HALF] = small_ref[:, :HALF]
+    gains_ref[1:2, :HALF] = small_ref[:, HALF : 2 * HALF]
+    bias_ref[:, :query_cols] = small_ref[:, 2 * HALF : 2 * HALF + query_cols]
+    for i in range(2):
+        bias_ref[:, query_cols + i * HEAD_SIZE : query_cols + (i + 1) * HEAD_SIZE] = small_ref[
+            :, aligned(2 * HALF + query_cols + i * kv_width + kv_at, HEAD_SIZE)
+        ]
+    swap_landed(0)
+    swap_landed(1)
+    swap_landed(2)
+    x = x_ref[...].astype(F32)
+    normed_ref[block_rows(me)] = (x * norm_scale(x) * gains_ref[0:1]).astype(BF16)
+    gather = Gather(me, normed_ref, g_sends, g_recv)
+    gather.step(0)
+
+    lane = lax.broadcasted_iota(jnp.int32, (BLOCK, HEAD_SIZE), 1)
+    first = lane < HEAD_SIZE // 2
+    swap_landed(3)
+    swap_copy(8).start()
+    gather.step(1)
+    swap_landed(8)
+    swap_copy(10).start()
+    swap_landed(4)
+    swap_landed(5)
+    for i in range(4):
+        if i < 2:
+            table = table_ref[block_rows(r + 2 * i)]
+        else:
+            table = tables[(i - 2) * BLOCK : (i - 1) * BLOCK]
+        turned = turn(table)
+        at = block_rows((r if i < 2 else 1 - r) * 2 + i % 2)
+        cos_ref[at] = jnp.where(first, table, turned)
+        sin_ref[at] = jnp.where(first, -turned, table)
+    swap_landed(10)
+
+    def kv_copy(j):
+        at = block_rows(j)
+        return send(
+            kv_ref.at[at], kv_other_ref.at[at], kv_sends.at[j], kv_recv.at[j], "row", x_to
+        )
+
+    def each(j):
+        at = block_rows(j)
+        block = normed_ref[at]
+        out = dot(block[:, :HALF], proj_ref[:, :proj_cols])
+        out = out + dot(block[:, HALF:], proj_other_ref[:, :proj_cols]) + bias_ref[...]
+        cosine, sine = cos_ref[at], sin_ref[at]
+        for h in range(query_cols // HEAD_SIZE + 1):
+            head = out[:, h * HEAD_SIZE : (h + 1) * HEAD_SIZE]
+            turned = (head * cosine + turn(head) * sine).astype(BF16)
+            if h * HEAD_SIZE < query_cols:
+                query_ref[at, h * HEAD_SIZE : (h + 1) * HEAD_SIZE] = turned
+            else:
+                kv_ref[at, :HEAD_SIZE] = turned
+        kv_ref[at, HEAD_SIZE:] = out[:, query_cols + HEAD_SIZE :].astype(BF16)
+        kv_copy(j).start()
+
+    gather.run_each(0, each)
+    gather.run_each(1, each)
+    gather.step(2)
+    gather.run_each(2, each)
+    swap_landed(7)
+    swap_copy(9).start()
+    gather.step(3)
+    gather.run_each(3, each)
+    for i in range(PIECES):
+        piece_copy(i, 0).start()
+    swap_landed(6)
+    cot_gather = Gather(me, cot_ref, c_sends, c_recv)
+    cot_gather.step(0)
+    swap_landed(9)
+    swap_copy(11).start()
+    for j in range(LINE):
+        kv_copy(j).wait_recv()
+    attend_local(query_ref, kv_ref, kv_other_ref, attended_ref, probs_ref, r)
+    swap_landed(11)
+
+    def block_of(j):
+        block = attended_ref[block_rows(j)]
+        return jnp.concatenate(
+            [
+                dot(block, proj_ref[:, proj_cols:], PAIR_COLS),
+                dot(block, proj_other_ref[:, proj_cols:], PAIR_COLS),
+            ],
+            1,
+        )
+
+    scatter = Scatter(me, block_of, landing, s_sends, s_recv)
+    scatter.step(3)
+    scatter.step(2)
+    scatter.step(1)
+    relay_x(0)
+    relay_x(1)
+    scatter.finish(mid_ref)
+    mid = mid_ref[...] + x_ref[...].astype(F32)
+    mid_ref[...] = mid
+    normed_two_ref[block_rows(me)] = (mid * norm_scale(mid) * gains_ref[1:2]).astype(BF16)
+
+    def turn_block(j):
+        turned_ref[:, block_rows(j)] = normed_two_ref[block_rows(j)].T
+
+    second = Gather(me, normed_two_ref, n_sends, n_recv)
+    second.step(0)
+    second.run_each(0, turn_block)
+    relay_x(2)
+    relay_y(0)
+    second.step(1)
+    second.run_each(1, turn_block)
+    relay_x(3)
+    relay_y(1)
+    second.step(2)
+    second.run_each(2, turn_block)
+    relay_x(4)
+    relay_y(2)
+    second.step(3)
+    second.run_each(3, turn_block)
+    relay_x(5)
+    relay_y(3)
+    relay_y(4)
+    relay_y(5)
+    cot_gather.step(1, forward=False)
+    for i in range(PIECES):
+        for way in (2, 3):
+            of_y = y if way == 2 else 1 - y
+            landed(weights_other_hbm.at[i // 2, piece(i, of_y), its_rows], piece_recv.at[way, i])
+        for way in range(4):
+            piece_copy(i, way).wait_send()
+    for i in range(len(swaps)):
+        swap_copy(i).wait_send()
+    for j in range(LINE):
+        kv_copy(j).wait_send()
+    gather.drain()
+    cot_gather.drain(0, 1)
+    second.drain()
+    scatter.drain()
+
+
+def front_call(proj_cols, query_cols, hidden, *args):
+    heads = query_cols // HEAD_SIZE
+    outs = [
+        shape(BLOCK, MODEL_WIDTH),
+        shape(LOCAL, MODEL_WIDTH),
+        shape(LOCAL, query_cols),
+        shape(LOCAL, 2 * HEAD_SIZE),
+        shape(LOCAL, 2 * HEAD_SIZE),
+        shape(LOCAL, HEAD_SIZE, F32),
+        shape(LOCAL, HEAD_SIZE, F32),
+        shape(2, MODEL_WIDTH, F32),
+        shape(LOCAL, query_cols),
+        jax.ShapeDtypeStruct((2 * heads, 2 * BLOCK, 4 * BLOCK), BF16),
+        shape(BLOCK, MODEL_WIDTH, F32),
+        shape(LOCAL, MODEL_WIDTH),
+        shape(MODEL_WIDTH, LOCAL),
+        shape(LOCAL, MODEL_WIDTH),
+        shape(HALF, proj_cols + query_cols),
+        shape(HALF, proj_cols + query_cols),
+        jax.ShapeDtypeStruct((3, hidden, HALF), BF16),
+    ]
+    return pl.pallas_call(
+        front_body,
+        out_shape=outs,
+        in_specs=[VMEM_SPEC] * 7 + [ANY_SPEC] * 3,
+        out_specs=[VMEM_SPEC] * (len(outs) - 1) + [ANY_SPEC],
+        scratch_shapes=[
+            pltpu.VMEM((2, BLOCK, HALF), BF16),
+            pltpu.VMEM((2 * BLOCK, HEAD_SIZE), F32),
+            pltpu.VMEM((1, proj_cols), F32),
+            pltpu.VMEM((2, LINE, BLOCK, MODEL_WIDTH), BF16),
+            DMA((12,)),
+            DMA((12,)),
+            DMA((4, PIECES)),
+            DMA((4, PIECES)),
+            DMA((LINE,)),
+            DMA((LINE,)),
+        ]
+        + gather_sems() * 3
+        + scatter_sems(),
+        compiler_params=pltpu.CompilerParams(
+            collective_id=1, has_side_effects=True, vmem_limit_bytes=67_043_328
+        ),
+        cost_estimate=pl.CostEstimate(
+            flops=4 * 10**9, bytes_accessed=40_000_000, transcendentals=0
+        ),
+        name="front",
+    )(*args)
+
+
+DOWN, GATE, UPPER, CHAIN = 0, 1, 2, 3
+UNITS = ((1, 1), (1, 0), (0, 1), (0, 0))
+TILE = 256
+
+
+def add_into(total_ref, term_ref, cols):
+    @pl.loop(0, total_ref.shape[0] // 32)
+    def _(i):
+        at = aligned(i * 32, 32, 32)
+        total_ref[at, cols] = (
+            total_ref[at, cols].astype(F32) + term_ref[at, cols].astype(F32)
+        ).astype(BF16)
+
+
+def rear_body(
+    mid_ref, gains_ref,
+    normed_two_hbm, turned_hbm, cot_hbm, gate_hbm, upper_hbm, down_hbm, other_hbm, proj_hbm, proj_other_hbm, query_hbm, kv_hbm,
+    kv_other_hbm, attended_hbm, probs_hbm, cos_hbm, sin_hbm, x_hbm, normed_one_hbm,
+    out_ref, in_ref, small_ref, query_w_ref, output_w_ref, kv_all_ref, kept_hbm, land2_hbm, land3_hbm,
+    cot_ref, activated_ref, gate_grad_ref, upper_grad_ref, out_part_ref, back_part_ref, turned_ref,
+    kv_got_ref, got_ref, out_landing, landing, sums, gives, gots,
+    chain_gots, chain_land2, chain_land3, kv_line, small_line, small_swap,
+    load_sems, w_sems, c_sends, c_recv, o_sends, o_recv, r_sends, r_recv, a_sends, a_recv,
+    give_sends, give_recv, two_sends, two_recv, three_sends, three_recv, stage_sem, kept_sems,
+    swap_sends, swap_recv, kv_sends, kv_recv, kvd_sends, kvd_recv, line_sends, line_recv,
+    small_sends, small_recv, credit,
+):
+    me, r, d = lax.axis_index("col"), lax.axis_index("row"), lax.axis_index("dp")
+    y, core = d // 2, lax.rem(d, 2)
+    x_to, y_to, core_to = 1 - r, 2 * (1 - y) + core, 2 * y + 1 - core
+    diagonal_to = 2 * (1 - y) + 1 - core
+    hidden = activated_ref.shape[1]
+    query_cols = query_w_ref.shape[1]
+    proj_cols = query_cols + 2 * HEAD_SIZE
+    chain_cols = proj_cols + query_cols
+    owns = (gate_hbm, upper_hbm, down_hbm)
+
+    def cot_loads(act):
+        for i in range(3):
+            j = me - 1 + i
+
+            @pl.when((j >= 0) & (j < LINE))
+            def _():
+                rows = block_rows(j)
+                act(pltpu.make_async_copy(cot_hbm.at[rows], cot_ref.at[rows], load_sems.at[i]))
+
+    turned_load = pltpu.make_async_copy(turned_hbm, turned_ref.at[1], load_sems.at[14])
+    turned_load.start()
+    cot_loads(lambda copy: copy.start())
+
+    halves = {m: (hidden // 2 + BLOCK - 1) // BLOCK * BLOCK for m in (DOWN, GATE, UPPER)}
+    halves[CHAIN] = chain_cols // 2
+
+    def columns(m, axis):
+        width = chain_cols if m == CHAIN else hidden
+        return pl.ds(0, halves[m]) if axis == "row" else pl.ds(halves[m], width - halves[m])
+
+    def unit_rows(h, rel):
+        of_y = 1 - y if rel else y
+        return aligned(h * HALF + of_y * 2 * UNIT, 2 * UNIT)
+
+    def split(res, keep_ref, give_ref, at):
+        low, high = res[:UNIT], res[UNIT:]
+        keep_ref[:, at] = jnp.where(core == 0, low, high).astype(BF16)
+        give_ref[:, at] = jnp.where(core == 0, high, low).astype(BF16)
+
+    order = [
+        (DOWN, 0), (DOWN, 1), (DOWN, 2), (UPPER, 0), (UPPER, 1), (UPPER, 2), (DOWN, 3),
+        (GATE, 0), (GATE, 1), (GATE, 2), (UPPER, 3), (GATE, 3),
+    ]
+    columns_of = {DOWN: activated_ref, GATE: gate_grad_ref, UPPER: upper_grad_ref}
+    ring = 3
+
+    def total_of(m, h, rel):
+        return sums.at[m * 4 + h * 2 + rel]
+
+    def give_copy(u):
+        return send(
+            gives.at[u % 2], gots.at[u % ring], give_sends.at[u], give_recv.at[u], "dp", core_to
+        )
+
+    def compute(u):
+        m, i = order[u]
+        h, rel = UNITS[i]
+        if u >= 2:
+            give_copy(u - 2).wait_send()
+        left = 0 if m == DOWN else 1
+        rows = unit_rows(h, rel)
+        tile = 512
+
+        def run(at):
+            res = dot(turned_ref[left, rows], columns_of[m][:, at])
+            split(res, total_of(m, h, rel), gives.at[u % 2], at)
+
+        @pl.loop(0, hidden // tile)
+        def _(i):
+            run(aligned(i * tile, tile))
+
+        if hidden % tile:
+            run(pl.ds(hidden // tile * tile, hidden % tile))
+        if u >= ring:
+            pl.semaphore_wait(credit, 1)
+        give_copy(u).start()
+
+    def two_copy(m, k, chain_sums=None):
+        h, rel = ((1, 0), (1, 1), (0, 1), (1, 1))[k]
+        axis, to = (("row", x_to), ("dp", y_to))[k // 2]
+        at = columns(m, axis)
+        if m == CHAIN:
+            src, dst = chain_sums.at[h * 2 + rel, :, at], chain_land2.at[k % 2, :, at]
+        else:
+            src, dst = total_of(m, h, rel).at[:, at], land2_hbm.at[m * 2 + k % 2, :, at]
+        return send(src, dst, two_sends.at[m, k], two_recv.at[m, k], axis, to)
+
+    def combine(u):
+        m, i = order[u]
+        h, rel = UNITS[i]
+        give_copy(u).wait_recv()
+        add_into(total_of(m, h, rel), gots.at[u % ring], pl.ds(0, hidden))
+        if u < len(order) - ring:
+            pl.semaphore_signal(credit, 1, device_id={"dp": core_to}, device_id_type=MESH_ID)
+        for k in {(1, 1): (1, 3), (1, 0): (0,), (0, 1): (2,), (0, 0): ()}[h, rel]:
+            two_copy(m, k).start()
+
+    def three_copy(m, k, chain_sums=None):
+        h, rel = ((0, 1), (1, 0))[k]
+        axis, to = (("dp", y_to), ("row", x_to))[k]
+        at = columns(m, ("row", "dp")[k])
+        if m == CHAIN:
+            src, dst = chain_sums.at[h * 2 + rel, :, at], chain_land3.at[:, at]
+        else:
+            src, dst = total_of(m, h, rel).at[:, at], land3_hbm.at[m, :, at]
+        return send(src, dst, three_sends.at[m, k], three_recv.at[m, k], axis, to)
+
+    def kept_copy(m):
+        return pltpu.make_async_copy(total_of(m, 0, 0), kept_hbm.at[m], kept_sems.at[m])
+
+    def stage(m, i):
+        return pltpu.make_async_copy(land2_hbm.at[m * 2 + i], gots.at[i], stage_sem.at[m, i])
+
+    def second_stage(m):
+        for k in range(4):
+            two_copy(m, k).wait_recv()
+        for i in (1, 0):
+            stage(m, i).start()
+        stage(m, 1).wait()
+        add_into(total_of(m, 0, 1), gots.at[1], columns(m, "row"))
+        three_copy(m, 0).start()
+        add_into(total_of(m, 1, 0), gots.at[1], columns(m, "dp"))
+        three_copy(m, 1).start()
+        stage(m, 0).wait()
+        add_into(total_of(m, 0, 0), gots.at[0], pl.ds(0, hidden))
+        kept_copy(m).start()
+
+    barrier = pltpu.get_barrier_semaphore()
+    others = [("row", x_to), ("dp", y_to), ("dp", core_to)]
+    for axis, index in others:
+        pl.semaphore_signal(barrier, 1, device_id={axis: index}, device_id_type=MESH_ID)
+    for s in range(1, LINE):
+        pl.semaphore_signal(
+            barrier, 1, device_id={"col": lax.rem(me + s, LINE)}, device_id_type=MESH_ID
+        )
+
+    cot_gather = Gather(me, cot_ref, c_sends, c_recv)
+    out_scatter = Scatter(
+        me, lambda j: out_part_ref[block_rows(j)].astype(F32), out_landing, o_sends, o_recv
+    )
+
+    def feed(weights, gates, total, normed_two_ref):
+        tiles = hidden // TILE
+        rest = hidden % TILE
+
+        def loads(t, slot, size):
+            rows = aligned(t * TILE, size, TILE)
+            for m in range(3):
+                for i, src in enumerate((owns[m].at[rows], other_hbm.at[m, rows])):
+                    yield pltpu.make_async_copy(
+                        src,
+                        weights.at[slot, m, pl.ds(0, size), pl.ds(i * HALF, HALF)],
+                        w_sems.at[slot, m, i],
+                    )
+
+        def start(t, slot, size):
+            for copy in loads(t, slot, size):
+                copy.start()
+
+        def ready(t, slot, size):
+            for copy in loads(t, slot, size):
+                copy.wait()
+
+        def sweep(body, first_slot, hooks, again):
+            @pl.loop(0, tiles)
+            def _(t):
+                slot = lax.rem(t + first_slot, 2)
+                ready(t, slot, TILE)
+
+                @pl.when(t < tiles - 1)
+                def _():
+                    start(t + 1, 1 - slot, TILE)
+
+                @pl.when(t == tiles - 1)
+                def _():
+                    start(tiles, 1 - slot, rest)
+
+                body(aligned(t * TILE, TILE), slot, TILE)
+                for at, hook in hooks:
+                    pl.when(t == at)(hook)
+
+            slot = (tiles + first_slot) % 2
+            ready(tiles, slot, rest)
+            if again:
+                start(0, 1 - slot, TILE)
+            body(pl.ds(tiles * TILE, rest), slot, rest)
+
+        def add_products(slot, size, factors, cols):
+            width = 512
+
+            @pl.loop(0, MODEL_WIDTH // width)
+            def _(i):
+                at = aligned(i * width, width)
+                term = sum(
+                    dot(factor[:, cols], weights[slot, m, pl.ds(0, size), at])
+                    for factor, m in factors
+                )
+                total[:, at] += term
+
+        def forward(cols, slot, size):
+            here = pl.ds(0, size)
+            gate = dot(normed_two_ref[...], weights[slot, 0, here], PAIR_COLS)
+            upper = dot(normed_two_ref[...], weights[slot, 1, here], PAIR_COLS)
+            activated = (gate * jax.nn.sigmoid(gate) * upper).astype(BF16)
+            gates[0, :, cols] = gate.astype(BF16)
+            gates[1, :, cols] = upper.astype(BF16)
+            activated_ref[:, cols] = activated
+            total[...] += dot(activated, weights[slot, 2, here])
+
+        def backward(cols, slot, size):
+            here = pl.ds(0, size)
+            act_grad = dot(cot_ref[...], weights[slot, 2, here], PAIR_COLS)
+            gate, upper = gates[0, :, cols].astype(F32), gates[1, :, cols].astype(F32)
+            sig = jax.nn.sigmoid(gate)
+            gate_grad = (act_grad * upper * sig * (1.0 + gate * (1.0 - sig))).astype(BF16)
+            upper_grad = (act_grad * gate * sig).astype(BF16)
+            gate_grad_ref[:, cols] = gate_grad
+            upper_grad_ref[:, cols] = upper_grad
+            add_products(slot, size, ((gate_grad_ref, 0), (upper_grad_ref, 1)), cols)
+
+        load = pltpu.make_async_copy(normed_two_hbm, normed_two_ref, load_sems.at[15])
+        load.start()
+        start(0, 0, TILE)
+        total[...] = jnp.zeros_like(total)
+        pl.semaphore_wait(barrier, len(others) + LINE - 1)
+        cot_loads(lambda copy: copy.wait())
+        cot_gather.step(1, wait=False)
+        load.wait()
+        turned_load.wait()
+        sweep(forward, 0, [(4, lambda: cot_gather.step(2))], True)
+        out_part_ref[...] = total[...].astype(BF16)
+        out_scatter.step(3)
+        cot_gather.step(3)
+        turned_ref[0] = cot_ref[...].T
+        total[...] = jnp.zeros_like(total)
+        compute(0)
+        compute(1)
+        combine(0)
+        combine(1)
+        sweep(backward, (tiles + 1) % 2, [(3, lambda: out_scatter.step(2))], False)
+        back_part_ref[...] = total[...].astype(BF16)
+        cot_gather.drain(1, LINE - 1)
+
+    pl.run_scoped(
+        feed,
+        pltpu.VMEM((2, 3, TILE, MODEL_WIDTH), BF16),
+        pltpu.VMEM((2, LOCAL, hidden), BF16),
+        pltpu.VMEM((LOCAL, MODEL_WIDTH), F32),
+        pltpu.VMEM((LOCAL, MODEL_WIDTH), BF16),
+    )
+
+    def rest(
+        proj_ref, proj_other_ref, query_ref, kv_ref, kv_other_ref, attended_ref, probs_ref, cos_ref,
+        sin_ref, x_ref, normed_one_ref, mid_grad_ref, own_ref, att_grad_ref,
+        kv_grad_ref, kv_give_ref, proj_grad_ref, chain_sums, back_give,
+    ):
+        pairs = (
+            (proj_hbm, proj_ref), (proj_other_hbm, proj_other_ref), (query_hbm, query_ref),
+            (kv_hbm, kv_ref), (kv_other_hbm, kv_other_ref), (attended_hbm, attended_ref),
+            (probs_hbm, probs_ref), (cos_hbm, cos_ref), (sin_hbm, sin_ref), (x_hbm, x_ref),
+            (normed_one_hbm, normed_one_ref),
+        )
+        reads = [
+            pltpu.make_async_copy(src, dst, load_sems.at[3 + i])
+            for i, (src, dst) in enumerate(pairs)
+        ]
+
+        mid_half_ref = cot_ref
+
+        scatter = Scatter(
+            me, lambda j: back_part_ref[block_rows(j)].astype(F32), landing, r_sends, r_recv
+        )
+        scatter.step(3)
+        for read in reads:
+            read.start()
+        compute(2)
+        compute(3)
+        combine(2)
+        scatter.step(2)
+        compute(4)
+        combine(3)
+        compute(5)
+        combine(4)
+        scatter.step(1)
+        compute(6)
+        combine(5)
+        compute(7)
+        combine(6)
+        scatter.finish(mid_grad_ref)
+        mid, grad = mid_ref[...], mid_grad_ref[...]
+        rinv = norm_scale(mid)
+        small_line[me] = jnp.zeros_like(small_line[me])
+        small_line[me, 1:2] = jnp.sum(grad * mid * rinv, 0, keepdims=True)
+        scaled = grad * gains_ref[1:2]
+        inner = jnp.sum(scaled * mid, -1, keepdims=True)
+        mid_grad = (
+            cot_ref[block_rows(me)].astype(F32)
+            + rinv * scaled
+            - mid * rinv**3 * inner / MODEL_WIDTH
+        )
+        mid_grad_ref[...] = mid_grad
+        mid_half_ref[block_rows(me)] = mid_grad.astype(BF16)
+
+        gather = Gather(me, mid_half_ref, a_sends, a_recv)
+        gather.step(0)
+        scatter.drain()
+        for read in reads:
+            read.wait()
+
+        def each(j):
+            block = mid_half_ref[block_rows(j)]
+            att_grad_ref[block_rows(j)] = (
+                dot(block[:, :HALF], proj_ref[:, proj_cols:])
+                + dot(block[:, HALF:], proj_other_ref[:, proj_cols:])
+            ).astype(BF16)
+
+        gather.run_each(0, each)
+        compute(8)
+        combine(7)
+        compute(9)
+        combine(8)
+        gather.step(1)
+        gather.run_each(1, each)
+        compute(10)
+        combine(9)
+        compute(11)
+        combine(10)
+        combine(11)
+        gather.step(2)
+        gather.run_each(2, each)
+        second_stage(DOWN)
+        gather.step(3)
+        gather.run_each(3, each)
+        out_scatter.step(1)
+        attend_back_body(
+            query_ref, kv_ref, kv_other_ref, attended_ref, probs_ref, att_grad_ref, cos_ref,
+            sin_ref, proj_grad_ref, kv_grad_ref, kv_give_ref,
+        )
+
+        def swap_copy(i):
+            src, dst = (
+                (kv_give_ref, kv_got_ref),
+                (back_give.at[0], got_ref.at[0]),
+                (back_give.at[1], got_ref.at[1]),
+            )[i]
+            return send(src, dst, swap_sends.at[i], swap_recv.at[i], "row", x_to)
+
+        swap_copy(0).start()
+        second_stage(UPPER)
+        swap_copy(0).wait_recv()
+        kv = kv_grad_ref[...] + kv_got_ref[...].astype(F32)
+        key = kv[:, :HEAD_SIZE]
+        proj_grad_ref[:, query_cols : query_cols + HEAD_SIZE] = (
+            key * cos_ref[...] - turn(key) * sin_ref[...]
+        ).astype(BF16)
+        proj_grad_ref[:, query_cols + HEAD_SIZE :] = kv[:, HEAD_SIZE:].astype(BF16)
+
+        def block_of(j):
+            block = proj_grad_ref[block_rows(j)]
+            return jnp.concatenate(
+                [
+                    dot(block, proj_ref[:, :proj_cols], PAIR_COLS),
+                    dot(block, proj_other_ref[:, :proj_cols], PAIR_COLS),
+                ],
+                1,
+            )
+
+        def chain_from(i):
+            return gives.at[i // 2, :, pl.ds(i % 2 * chain_cols, chain_cols)]
+
+        def chain_give(i):
+            return send(
+                chain_from(i), chain_gots.at[i], give_sends.at[12 + i], give_recv.at[12 + i],
+                "dp", core_to,
+            )
+
+        def chain_compute(i):
+            h, rel = UNITS[i]
+            rows = unit_rows(h, rel)
+            keep = chain_sums.at[h * 2 + rel]
+            res = dot(normed_one_ref[:, rows], proj_grad_ref[...], PAIR_ROWS)
+            split(res, keep, chain_from(i), pl.ds(0, proj_cols))
+            res = dot(mid_half_ref[:, rows], attended_ref[...], PAIR_ROWS)
+            split(res, keep, chain_from(i), pl.ds(proj_cols, query_cols))
+            chain_give(i).start()
+
+        def chain_combine(i):
+            h, rel = UNITS[i]
+            chain_give(i).wait_recv()
+            add_into(chain_sums.at[h * 2 + rel], chain_gots.at[i], pl.ds(0, chain_cols))
+            for k in {(1, 1): (1, 3), (1, 0): (0,), (0, 1): (2,), (0, 0): ()}[h, rel]:
+                two_copy(CHAIN, k, chain_sums).start()
+
+        second = Scatter(me, block_of, landing, r_sends, r_recv)
+        second.step(3)
+        for u in (len(order) - 2, len(order) - 1):
+            give_copy(u).wait_send()
+        for i in range(4):
+            chain_compute(i)
+        for i in range(4):
+            chain_combine(i)
+        small_line[me, 2:3, :proj_cols] = jnp.sum(
+            proj_grad_ref[...].astype(F32), 0, keepdims=True
+        )
+        second.step(2)
+        second_stage(GATE)
+        out_scatter.finish(own_ref)
+        out = own_ref[...] + mid_ref[...]
+        out_ref[:, block_rows(r)] = out[:, :HALF].T
+        back_give[1] = out[:, HALF:].astype(BF16)
+        second.step(1)
+        swap_copy(2).start()
+        for k in range(4):
+            two_copy(CHAIN, k, chain_sums).wait_recv()
+        add_into(chain_sums.at[1], chain_land2.at[1], columns(CHAIN, "row"))
+        three_copy(CHAIN, 0, chain_sums).start()
+        add_into(chain_sums.at[2], chain_land2.at[1], columns(CHAIN, "dp"))
+        three_copy(CHAIN, 1, chain_sums).start()
+        add_into(chain_sums.at[0], chain_land2.at[0], pl.ds(0, chain_cols))
+        second.finish(own_ref)
+        x, grad = x_ref[...].astype(F32), own_ref[...]
+        rinv = norm_scale(x)
+        scaled = grad * gains_ref[0:1]
+        inner = jnp.sum(scaled * x, -1, keepdims=True)
+        input_grad = mid_grad_ref[...] + rinv * scaled - x * rinv**3 * inner / MODEL_WIDTH
+        back_give[0] = input_grad[:, HALF:].astype(BF16)
+        swap_copy(1).start()
+        small_line[me, 0:1] = jnp.sum(grad * x * rinv, 0, keepdims=True)
+
+        def small_line_copy(s):
+            to = lax.rem(me + s, LINE)
+            return send(
+                small_line.at[me], small_line.at[me], line_sends.at[s], line_recv.at[me], "col", to
+            )
+
+        for s in range(1, LINE):
+            small_line_copy(s).start()
+        in_ref[:, block_rows(r)] = input_grad[:, :HALF].T
+
+        for s in range(1, LINE):
+            landed(small_line.at[me], line_recv.at[lax.rem(me + s, LINE)])
+        group = LINE // KEYVALUE_HEADS
+        lines = [small_line[j] for j in range(LINE)]
+        gain_sum = lines[0][:2] + lines[1][:2] + lines[2][:2] + lines[3][:2]
+        small_swap[0] = jnp.zeros_like(small_swap[0])
+        small_swap[0, 0:2] = gain_sum
+        small_swap[0, 2:3, :query_cols] = small_line[me, 2:3, :query_cols]
+        for i in range(2):
+            for h in range(KEYVALUE_HEADS):
+                at = query_cols + i * HEAD_SIZE
+                part = lines[h * group][2:3, at : at + HEAD_SIZE]
+                for j in range(1, group):
+                    part = part + lines[h * group + j][2:3, at : at + HEAD_SIZE]
+                at = (i * KEYVALUE_HEADS + h) * HEAD_SIZE
+                small_swap[0, 3:4, at : at + HEAD_SIZE] = part
+
+        def small_copy(i):
+            axis, to = (("dp", core_to), ("dp", y_to), ("row", x_to))[i]
+            return send(
+                small_swap.at[2 * i], small_swap.at[2 * i + 1], small_sends.at[i],
+                small_recv.at[i], axis, to,
+            )
+
+        small_copy(0).start()
+        small_copy(0).wait_recv()
+        small_swap[2] = small_swap[0] + small_swap[1]
+        small_copy(1).start()
+
+        for k in range(2):
+            three_copy(CHAIN, k, chain_sums).wait_recv()
+        total = chain_sums[0].astype(F32) + chain_land3[...].astype(F32)
+        query_w_ref[...] = total[:, :query_cols]
+        output_w_ref[...] = total[:, proj_cols:]
+        kv_line[me] = total[:, query_cols:proj_cols].astype(BF16)
+
+        def kv_line_copy(s):
+            to = lax.rem(me + s, LINE)
+            return send(kv_line.at[me], kv_line.at[me], kv_sends.at[s], kv_recv.at[me], "col", to)
+
+        for s in range(1, LINE):
+            kv_line_copy(s).start()
+        small_copy(1).wait_recv()
+        both = small_swap[2] + small_swap[3]
+        small_swap[4, :2, :HALF] = both[:2, HALF:]
+        small_swap[4, 2:, :HALF] = both[2:, :HALF]
+        small_copy(2).start()
+        for s in range(1, LINE):
+            landed(kv_line.at[me], kv_recv.at[lax.rem(me + s, LINE)])
+        dp_rows = aligned(d * UNIT, UNIT, UNIT)
+        for h in range(KEYVALUE_HEADS):
+            pair = kv_line[h * group].astype(F32)
+            for i in range(1, group):
+                pair = pair + kv_line[h * group + i].astype(F32)
+            for i in range(2):
+                at = (i * KEYVALUE_HEADS + h) * HEAD_SIZE
+                kv_all_ref[dp_rows, at : at + HEAD_SIZE] = pair[
+                    :, i * HEAD_SIZE : (i + 1) * HEAD_SIZE
+                ].astype(BF16)
+
+        def kv_rows(of):
+            return kv_all_ref.at[aligned(of * UNIT, UNIT, UNIT)]
+
+        def kv_dp_copy(i):
+            rows = kv_rows(y_to if i == 2 else d)
+            to = y_to if i == 1 else core_to
+            return send(rows, rows, kvd_sends.at[i], kvd_recv.at[i], "dp", to)
+
+        kv_dp_copy(1).start()
+        kv_dp_copy(0).start()
+        for i in (2, 1):
+            swap_copy(i).wait_recv()
+            to_ref = (in_ref, out_ref)[i - 1]
+            to_ref[:, block_rows(1 - r)] = got_ref[i - 1].astype(F32).T
+        small_copy(2).wait_recv()
+        small_ref[...] = both[:, :HALF] + small_swap[5, :, :HALF]
+
+        landed(kv_rows(y_to), kvd_recv.at[1])
+        kv_dp_copy(2).start()
+        landed(kv_rows(core_to), kvd_recv.at[0])
+        landed(kv_rows(diagonal_to), kvd_recv.at[2])
+        for m in (DOWN, GATE, UPPER):
+            for k in range(2):
+                three_copy(m, k).wait_recv()
+                three_copy(m, k).wait_send()
+            kept_copy(m).wait()
+            for k in range(4):
+                two_copy(m, k).wait_send()
+        for i in range(4):
+            chain_give(i).wait_send()
+            two_copy(CHAIN, i, chain_sums).wait_send()
+        for k in range(2):
+            three_copy(CHAIN, k, chain_sums).wait_send()
+        for i in range(3):
+            swap_copy(i).wait_send()
+            small_copy(i).wait_send()
+            kv_dp_copy(i).wait_send()
+            kv_line_copy(1 + i).wait_send()
+            small_line_copy(1 + i).wait_send()
+        gather.drain()
+        out_scatter.drain()
+        second.drain()
+
+    wide = (HALF, chain_cols)
+    pl.run_scoped(
+        rest,
+        pltpu.VMEM(wide, BF16),
+        pltpu.VMEM(wide, BF16),
+        pltpu.VMEM((LOCAL, query_cols), BF16),
+        pltpu.VMEM((LOCAL, 2 * HEAD_SIZE), BF16),
+        pltpu.VMEM((LOCAL, 2 * HEAD_SIZE), BF16),
+        pltpu.VMEM((LOCAL, query_cols), BF16),
+        pltpu.VMEM(probs_hbm.shape, BF16),
+        pltpu.VMEM((LOCAL, HEAD_SIZE), F32),
+        pltpu.VMEM((LOCAL, HEAD_SIZE), F32),
+        pltpu.VMEM((BLOCK, MODEL_WIDTH), BF16),
+        pltpu.VMEM((LOCAL, MODEL_WIDTH), BF16),
+        pltpu.VMEM((BLOCK, MODEL_WIDTH), F32),
+        pltpu.VMEM((BLOCK, MODEL_WIDTH), F32),
+        pltpu.VMEM((LOCAL, query_cols), BF16),
+        pltpu.VMEM((LOCAL, 2 * HEAD_SIZE), F32),
+        pltpu.VMEM((LOCAL, 2 * HEAD_SIZE), BF16),
+        pltpu.VMEM((LOCAL, proj_cols), BF16),
+        pltpu.VMEM((4, UNIT, chain_cols), BF16),
+        pltpu.VMEM((2, BLOCK, HALF), BF16),
+    )
+
+
+def rear_call(hidden, proj_cols, query_cols, *args):
+    chain_cols = proj_cols + query_cols
+    outs = [
+        shape(HALF, 2 * BLOCK, F32),
+        shape(HALF, 2 * BLOCK, F32),
+        shape(8, HALF, F32),
+        shape(UNIT, query_cols, F32),
+        shape(UNIT, query_cols, F32),
+        shape(4 * UNIT, 2 * KEYVALUE_HEADS * HEAD_SIZE),
+        jax.ShapeDtypeStruct((3, UNIT, hidden), BF16),
+        jax.ShapeDtypeStruct((6, UNIT, hidden), BF16),
+        jax.ShapeDtypeStruct((3, UNIT, hidden), BF16),
+    ]
+    local = (LOCAL, MODEL_WIDTH)
+    line = (2, LINE, BLOCK, MODEL_WIDTH)
+    return pl.pallas_call(
+        rear_body,
+        out_shape=outs,
+        in_specs=[VMEM_SPEC] * 2 + [ANY_SPEC] * (len(args) - 2),
+        out_specs=[VMEM_SPEC] * 6 + [ANY_SPEC] * 3,
+        scratch_shapes=[
+            pltpu.VMEM(local, BF16),
+            pltpu.VMEM((LOCAL, hidden), BF16),
+            pltpu.VMEM((LOCAL, hidden), BF16),
+            pltpu.VMEM((LOCAL, hidden), BF16),
+            pltpu.VMEM(local, BF16),
+            pltpu.VMEM(local, BF16),
+            pltpu.VMEM((2, MODEL_WIDTH, LOCAL), BF16),
+            pltpu.VMEM((LOCAL, 2 * HEAD_SIZE), BF16),
+            pltpu.VMEM((2, BLOCK, HALF), BF16),
+            pltpu.VMEM(line, BF16),
+            pltpu.VMEM(line, BF16),
+            pltpu.VMEM((12, UNIT, hidden), BF16),
+            pltpu.VMEM((2, UNIT, hidden), BF16),
+            pltpu.VMEM((3, UNIT, hidden), BF16),
+            pltpu.VMEM((4, UNIT, chain_cols), BF16),
+            pltpu.VMEM((2, UNIT, chain_cols), BF16),
+            pltpu.VMEM((UNIT, chain_cols), BF16),
+            pltpu.VMEM((LINE, UNIT, 2 * HEAD_SIZE), BF16),
+            pltpu.VMEM((LINE, 8, MODEL_WIDTH), F32),
+            pltpu.VMEM((6, 8, MODEL_WIDTH), F32),
+            DMA((16,)),
+            DMA((2, 3, 2)),
+        ]
+        + gather_sems()
+        + scatter_sems()
+        + scatter_sems()
+        + gather_sems()
+        + [
+            DMA((16,)), DMA((16,)),
+            DMA((4, 4)), DMA((4, 4)),
+            DMA((4, 2)), DMA((4, 2)),
+            DMA((3, 2)), DMA((3,)),
+            DMA((3,)), DMA((3,)),
+            DMA((LINE,)), DMA((LINE,)),
+            DMA((3,)), DMA((3,)),
+            DMA((LINE,)), DMA((LINE,)),
+            DMA((3,)), DMA((3,)),
+            pltpu.SemaphoreType.REGULAR,
+        ],
+        compiler_params=pltpu.CompilerParams(
+            collective_id=2, has_side_effects=True, vmem_limit_bytes=67_043_328
+        ),
+        cost_estimate=pl.CostEstimate(
+            flops=4 * 10**10, bytes_accessed=80_000_000, transcendentals=0
+        ),
+        name="rear",
+    )(*args)
+
+
+def fast_device(
+    block_input,
+    position_ids,
+    attention_gain,
+    query_weight,
+    query_bias,
+    key_value_weight,
+    key_value_bias,
+    output_weight,
+    feedforward_gain,
+    gate_weight,
+    upper_weight,
+    down_weight,
+    out_cotangent,
+):
+    query_cols = query_weight.shape[1]
+    hidden = gate_weight.shape[1]
+    proj_cols = query_cols + 2 * HEAD_SIZE
+    frequencies = THETA ** (-(jnp.arange(HEAD_SIZE // 2, dtype=F32) * 2.0 / HEAD_SIZE))
+    angles = position_ids.astype(F32)[:, None] * frequencies[None, :]
+    table = jnp.concatenate([jnp.cos(angles), jnp.sin(angles)], -1)
+    small = jnp.concatenate([attention_gain, feedforward_gain, query_bias, key_value_bias])[None]
+    gate_t, upper_t, down_t = gate_weight.T, upper_weight.T, down_weight.T
+    (
+        x_own, normed_one, query_rot, kv_own, kv_other, cosine, sine, gains, attended, probs,
+        mid, normed_two, normed_turned, cot_part, own_proj, other_proj, other_weights,
+    ) = front_call(
+        proj_cols, query_cols, hidden,
+        block_input, out_cotangent, table, small, query_weight, key_value_weight, output_weight,
+        gate_t, upper_t, down_t,
+    )
+    out, input_grad, sums, query_sum, output_sum, kv_all, kept, _, landing = rear_call(
+        hidden, proj_cols, query_cols,
+        mid, gains,
+        normed_two, normed_turned, cot_part, gate_t, upper_t, down_t, other_weights, own_proj, other_proj, query_rot, kv_own,
+        kv_other, attended, probs, cosine, sine, x_own, normed_one,
+    )
+    down_sum, gate_sum, upper_sum = (
+        kept[m].astype(F32) + landing[m].astype(F32) for m in range(3)
+    )
+    bias_rows = query_cols // lax.axis_size("dp")
+    query_bias_grad = lax.dynamic_slice_in_dim(
+        sums[2], lax.axis_index("dp") * bias_rows, bias_rows, 0
+    )
+    return (
+        out,
+        input_grad,
+        sums[0],
+        query_sum,
+        query_bias_grad,
+        kv_all.astype(F32),
+        sums[3, : 2 * KEYVALUE_HEADS * HEAD_SIZE],
+        output_sum,
+        sums[1],
+        gate_sum,
+        upper_sum,
+        down_sum,
+    )
+
+
+def per_device(*arrays):
+    sizes = tuple(lax.axis_size(axis) for axis in ("dp", "row", "col"))
+    if sizes == (4, 2, LINE) and arrays[0].shape == (HALF, 2 * BLOCK):
+        return fast_device(*arrays)
+    return general_device(*arrays)
+
+
 def solution(mesh):
     placed = (
         P("row", ("dp", "col")),

time: 1150 us -> 324 us (0.28)
  waiting for transfers between devices: 838 us -> 0 us
  Pallas kernels: 0 us -> 305 us
  matrix products: 91.4 us -> 0 us
  blocking collectives: 69.8 us -> 0 us
  local copies, waits for them, and re-layouts: 63.2 us -> 7.16 us
  other arithmetic: 63.2 us -> 9.74 us
  between operations: 15.7 us -> 0.69 us
    reduce_scatter x12 -> x0, waiting for transfers between devices: 448 us -> none  [the longest x4 188 us: row_product(): lax.psum_scatter(jnp.dot(gathered, weight, preferred_element_type=jnp.flo...]
    pallas_call x0 -> x2, Pallas kernels: none -> 305 us  [the longest x1 184 us: rear_call(): pl.pallas_call(rear_body, out_shape=outs, in_specs=[VMEM_SPEC] * 2 + [ANY...]
    all_gather x7 -> x0, waiting for transfers between devices: 288 us -> none  [the longest x4 126 us: column_gather(): return lax.all_gather(values, 'col', axis=0, tiled=True)]
    dot_general x18 -> x0, matrix products: 91.4 us -> none  [the longest x4 26.7 us: accumulate(): lax.dot_general(partner, block_rows, pair_dims, preferred_element_type=jn...]
    psum x1 -> x0, waiting for transfers between devices: 87 us -> none  [per_device(): lax.psum(key_value_gradient.astype(jnp.bfloat16), ('dp', 'col'))]
    psum x5 -> x0, blocking collectives: 52.6 us -> none  [the longest x1 31.9 us: per_device(): lax.psum(attn_gain_part.astype(jnp.bfloat16), ('dp', 'col'))]
    convert_element_type x18 -> x2, other arithmetic: 30.3 us -> 2.04 us  [the longest x1 1.35 us: fast_device(): kv_all.astype(F32)]
    unnamed x63 -> x14, local copies, waits for them, and re-layouts: 27.8 us -> 3.21 us
  transfers between devices with their start and end apart: 21 -> 0, of which waited for: 20 -> 0; matrix products, arithmetic and copies ran while one was open for 11% -> 0% of each run, Pallas kernels for 0% -> 0%
where the time goes in v3:
time: 324 us; the launch traced here: 323 us
  Pallas kernels  305 us (94%)
  other arithmetic  9.74 us (3%)
  local copies, waits for them, and re-layouts  7.16 us (2%)
    pallas_call x1, Pallas kernels, rear_call(): pl.pallas_call(rear_body, out_shape=outs, in_specs=[VMEM_SPEC] * 2 + [ANY...  184 us
    pallas_call x1, Pallas kernels, front_call(): pl.pallas_call(front_body, out_shape=outs, in_specs=[VMEM_SPEC] * 7 + [AN...  122 us

profile of v3, /device:TPU:0, one launch (start us, length us, event | category | flops | bytes accessed | tf_op | source)
XLA Modules:
  0.0 323.1 jit_solution(15342937265686585386)
XLA Ops:
  0.6 0.7 convert_element_type.30
  1.3 1.0 multiply_cosine_fusion
  2.3 0.8 pad_maximum_fusion.table_ref
  3.2 0.7 pad_maximum_fusion.1
  3.9 0.6 broadcast_in_dim.2.small_ref
  4.5 121.8 %front.1 = (bf16[128,1536]{1,0:T(8,128)(2,1)}, bf16[512,1536]{1,0:T(8,128)(2,1)}, bf16[512,384]{1,0:T(8,128)(2,1)}, bf16[512,256]{1,0:T(8,128)(2,1)}, bf16[512,2...) custom-call(bf16[768,256]{1,0:T(8,128)(2,1)} %input_ref.1, ...), custom_call_target="tpu_custom_call" | custom-call | flops 4000000000 | bytes 40000000 | tf_op jit(solution)/shard_map/front/pallas_call | solution.py:851
  126.3 183.7 %rear.1 = (f32[768,256]{1,0:T(8,128)}, f32[768,256]{1,0:T(8,128)}, f32[8,768]{1,0:T(8,128)}, f32[192,384]{1,0:T(8,128)}, f32[192,384]{1,0:T(8,128)}, /*index=5*/...) custom-call(f32[128,1536]{1,0:T(8,128)} %get-tuple-element.37.mid_re, ...), custom_call_target="tpu_custom_call" | custom-call | flops 40000000000 | bytes 80000000 | tf_op jit(solution)/shard_map/rear/pallas_call | solution.py:1489
  310.0 0.0 copy-start.2
  310.0 5.1 %add_bitcast_fusion = (f32[192,2240]{1,0:T(8,128)}, f32[192,2240]{1,0:T(8,128)}, f32[192,2240]{1,0:T(8,128)}) fusion(bf16[3,192,2240]{2,1,0:T(8,128)(2,1)} %get-tuple-element.61, bf16[3,192,2240]{2,1,0:T(8,128)(2,1)} %get-tuple-element.60), kind=kLoop, calls=%fused_computation | loop fusion | flops 3870720 | bytes 10321920 | tf_op jit(solution)/shard_map/add | solution.py:1582
  315.2 0.0 copy-start.1
  315.2 0.0 copy-done.2
  315.2 0.0 copy-start
  315.2 1.4 convert_element_type.31
  316.5 1.5 slice_reduce_fusion
  318.0 0.6 dynamic-slice_bitcast_fusion
  318.6 1.3 slice.32
  319.9 0.0 copy-done.1
  319.9 0.9 copy.29
  320.8 0.0 copy-done
  320.8 0.9 copy.30
  321.6 0.0 copy-done.4
  321.6 0.7 copy.31
  322.4 0.0 copy-done.3
  322.4 0.7 copy.32
  (3 shorter events, 0.0 us)
Async XLA Ops:
  310.0 5.1 %copy-start.2 = (bf16[768,512]{1,0:T(8,128)(2,1)S(1)}, bf16[768,512]{1,0:T(8,128)(2,1)}, u32[]{:S(2)}) copy-start(bf16[768,512]{1,0:T(8,128)(2,1)} %get-tuple-element.58) | copy-start | bytes 2359300
  315.2 4.7 %copy-start.1 = (f32[768,256]{1,0:T(8,128)S(1)}, f32[768,256]{1,0:T(8,128)}, u32[]{:S(2)}) copy-start(f32[768,256]{1,0:T(8,128)} %get-tuple-element.82) | copy-start | bytes 2359300
  315.2 5.6 %copy-start = (f32[768,256]{1,0:T(8,128)S(1)}, f32[768,256]{1,0:T(8,128)}, u32[]{:S(2)}) copy-start(f32[768,256]{1,0:T(8,128)} %get-tuple-element.83) | copy-start | bytes 2359300
  316.5 5.1 %copy-start.4 = (f32[192,384]{1,0:T(8,128)S(1)}, f32[192,384]{1,0:T(8,128)}, u32[]{:S(2)}) copy-start(f32[192,384]{1,0:T(8,128)} %get-tuple-element.85) | copy-start | bytes 884740
  319.9 2.5 copy-start.3

commit v4 on v3

--- a/solution.py
+++ b/solution.py
@@ -609,9 +609,12 @@
 def front_body(
     input_ref, cot_in_ref, table_ref, small_ref, query_w_ref, kv_w_ref, output_w_ref,
     gate_hbm, upper_hbm, down_hbm,
-    x_ref, normed_ref, query_ref, kv_ref, kv_other_ref, cos_ref, sin_ref, gains_ref,
-    attended_ref, probs_ref, mid_ref, normed_two_ref, turned_ref, cot_ref, proj_ref, proj_other_ref, weights_other_hbm,
-    passing, tables, bias_ref, landing,
+    x_hbm, normed_hbm, query_hbm, kv_hbm, kv_other_hbm, cos_hbm, sin_hbm, gains_ref,
+    attended_hbm, probs_hbm, mid_hbm, normed_two_hbm, turned_hbm, cot_hbm, proj_hbm, proj_other_hbm,
+    weights_other_hbm,
+    x_ref, normed_ref, query_ref, kv_ref, kv_other_ref, cos_ref, sin_ref,
+    attended_ref, probs_ref, mid_ref, normed_two_ref, turned_ref, cot_ref, proj_ref, proj_other_ref,
+    passing, tables, bias_ref, landing, store_sems,
     swap_sends, swap_recv, piece_sends, piece_recv, kv_sends, kv_recv,
     g_sends, g_recv, c_sends, c_recv, n_sends, n_recv, s_sends, s_recv,
 ):
@@ -629,6 +632,19 @@
     kv_width = KEYVALUE_HEADS * HEAD_SIZE
     kv_at = me // (LINE // KEYVALUE_HEADS) * HEAD_SIZE
 
+    stores = [
+        pltpu.make_async_copy(src, dst, store_sems.at[i])
+        for i, (src, dst) in enumerate(
+            (
+                (x_ref, x_hbm), (cos_ref, cos_hbm), (sin_ref, sin_hbm), (proj_ref, proj_hbm),
+                (normed_ref, normed_hbm), (query_ref, query_hbm), (kv_ref, kv_hbm),
+                (kv_other_ref, kv_other_hbm), (probs_ref, probs_hbm), (attended_ref, attended_hbm),
+                (proj_other_ref, proj_other_hbm), (mid_ref, mid_hbm),
+                (normed_two_ref, normed_two_hbm), (turned_ref, turned_hbm), (cot_ref, cot_hbm),
+            )
+        )
+    ]
+
     passing[0] = input_ref[:, block_rows(1 - r)].T
     x_ref[:, :HALF] = input_ref[:, block_rows(r)].T
     proj_ref[:, :query_cols] = query_w_ref[...]
@@ -689,6 +705,7 @@
     proj_ref[:, proj_cols:] = output_w_ref[...]
     swap_copy(6).start()
     swap_copy(7).start()
+    piece_copy(0, 0).start()
     cot_ref[block_rows(me), :HALF] = cot_in_ref[:, block_rows(r)].T
     gains_ref[0:1, :HALF] = small_ref[:, :HALF]
     gains_ref[1:2, :HALF] = small_ref[:, HALF : 2 * HALF]
@@ -755,13 +772,14 @@
     swap_copy(9).start()
     gather.step(3)
     gather.run_each(3, each)
-    for i in range(PIECES):
+    for i in range(1, PIECES):
         piece_copy(i, 0).start()
     swap_landed(6)
     cot_gather = Gather(me, cot_ref, c_sends, c_recv)
     cot_gather.step(0)
     swap_landed(9)
     swap_copy(11).start()
+    relay_x(0)
     for j in range(LINE):
         kv_copy(j).wait_recv()
     attend_local(query_ref, kv_ref, kv_other_ref, attended_ref, probs_ref, r)
@@ -779,10 +797,14 @@
 
     scatter = Scatter(me, block_of, landing, s_sends, s_recv)
     scatter.step(3)
+    for store in stores[:11]:
+        store.start()
+    relay_x(1)
     scatter.step(2)
+    relay_x(2)
     scatter.step(1)
-    relay_x(0)
-    relay_x(1)
+    relay_y(0)
+    relay_x(3)
     scatter.finish(mid_ref)
     mid = mid_ref[...] + x_ref[...].astype(F32)
     mid_ref[...] = mid
@@ -793,24 +815,25 @@
 
     second = Gather(me, normed_two_ref, n_sends, n_recv)
     second.step(0)
+    stores[11].start()
     second.run_each(0, turn_block)
-    relay_x(2)
-    relay_y(0)
+    relay_y(1)
+    relay_x(4)
     second.step(1)
     second.run_each(1, turn_block)
-    relay_x(3)
-    relay_y(1)
+    relay_y(2)
+    relay_x(5)
     second.step(2)
     second.run_each(2, turn_block)
-    relay_x(4)
-    relay_y(2)
+    relay_y(3)
     second.step(3)
     second.run_each(3, turn_block)
-    relay_x(5)
-    relay_y(3)
     relay_y(4)
+    stores[12].start()
+    stores[13].start()
+    cot_gather.step(1, forward=False)
+    stores[14].start()
     relay_y(5)
-    cot_gather.step(1, forward=False)
     for i in range(PIECES):
         for way in (2, 3):
             of_y = y if way == 2 else 1 - y
@@ -821,6 +844,8 @@
         swap_copy(i).wait_send()
     for j in range(LINE):
         kv_copy(j).wait_send()
+    for store in stores:
+        store.wait()
     gather.drain()
     cot_gather.drain(0, 1)
     second.drain()
@@ -829,6 +854,7 @@
 
 def front_call(proj_cols, query_cols, hidden, *args):
     heads = query_cols // HEAD_SIZE
+    gains = shape(2, MODEL_WIDTH, F32)
     outs = [
         shape(BLOCK, MODEL_WIDTH),
         shape(LOCAL, MODEL_WIDTH),
@@ -837,7 +863,7 @@
         shape(LOCAL, 2 * HEAD_SIZE),
         shape(LOCAL, HEAD_SIZE, F32),
         shape(LOCAL, HEAD_SIZE, F32),
-        shape(2, MODEL_WIDTH, F32),
+        gains,
         shape(LOCAL, query_cols),
         jax.ShapeDtypeStruct((2 * heads, 2 * BLOCK, 4 * BLOCK), BF16),
         shape(BLOCK, MODEL_WIDTH, F32),
@@ -852,12 +878,14 @@
         front_body,
         out_shape=outs,
         in_specs=[VMEM_SPEC] * 7 + [ANY_SPEC] * 3,
-        out_specs=[VMEM_SPEC] * (len(outs) - 1) + [ANY_SPEC],
-        scratch_shapes=[
+        out_specs=[VMEM_SPEC if out is gains else ANY_SPEC for out in outs],
+        scratch_shapes=[pltpu.VMEM(out.shape, out.dtype) for out in outs[:-1] if out is not gains]
+        + [
             pltpu.VMEM((2, BLOCK, HALF), BF16),
             pltpu.VMEM((2 * BLOCK, HEAD_SIZE), F32),
             pltpu.VMEM((1, proj_cols), F32),
             pltpu.VMEM((2, LINE, BLOCK, MODEL_WIDTH), BF16),
+            DMA((15,)),
             DMA((12,)),
             DMA((12,)),
             DMA((4, PIECES)),
@@ -1017,7 +1045,7 @@
     def stage(m, i):
         return pltpu.make_async_copy(land2_hbm.at[m * 2 + i], gots.at[i], stage_sem.at[m, i])
 
-    def second_stage(m):
+    def second_stage(m, over_row=True):
         for k in range(4):
             two_copy(m, k).wait_recv()
         for i in (1, 0):
@@ -1026,7 +1054,8 @@
         add_into(total_of(m, 0, 1), gots.at[1], columns(m, "row"))
         three_copy(m, 0).start()
         add_into(total_of(m, 1, 0), gots.at[1], columns(m, "dp"))
-        three_copy(m, 1).start()
+        if over_row:
+            three_copy(m, 1).start()
         stage(m, 0).wait()
         add_into(total_of(m, 0, 0), gots.at[0], pl.ds(0, hidden))
         kept_copy(m).start()
@@ -1180,18 +1209,17 @@
         for read in reads:
             read.start()
         compute(2)
-        compute(3)
-        combine(2)
+        for u in (3, 4, 5):
+            compute(u)
+            combine(u - 1)
         scatter.step(2)
-        compute(4)
-        combine(3)
-        compute(5)
-        combine(4)
+        for u in (6, 7):
+            compute(u)
+            combine(u - 1)
         scatter.step(1)
-        compute(6)
-        combine(5)
-        compute(7)
-        combine(6)
+        for u in (8, 9):
+            compute(u)
+            combine(u - 1)
         scatter.finish(mid_grad_ref)
         mid, grad = mid_ref[...], mid_grad_ref[...]
         rinv = norm_scale(mid)
@@ -1221,20 +1249,16 @@
             ).astype(BF16)
 
         gather.run_each(0, each)
-        compute(8)
-        combine(7)
-        compute(9)
-        combine(8)
+        for u in (10, 11):
+            compute(u)
+            combine(u - 1)
+        combine(11)
         gather.step(1)
         gather.run_each(1, each)
-        compute(10)
-        combine(9)
-        compute(11)
-        combine(10)
-        combine(11)
+        second_stage(DOWN)
         gather.step(2)
         gather.run_each(2, each)
-        second_stage(DOWN)
+        second_stage(UPPER, False)
         gather.step(3)
         gather.run_each(3, each)
         out_scatter.step(1)
@@ -1252,7 +1276,6 @@
             return send(src, dst, swap_sends.at[i], swap_recv.at[i], "row", x_to)
 
         swap_copy(0).start()
-        second_stage(UPPER)
         swap_copy(0).wait_recv()
         kv = kv_grad_ref[...] + kv_got_ref[...].astype(F32)
         key = kv[:, :HEAD_SIZE]
@@ -1305,17 +1328,17 @@
             chain_compute(i)
         for i in range(4):
             chain_combine(i)
+        three_copy(UPPER, 1).start()
         small_line[me, 2:3, :proj_cols] = jnp.sum(
             proj_grad_ref[...].astype(F32), 0, keepdims=True
         )
         second.step(2)
-        second_stage(GATE)
+        second_stage(GATE, False)
         out_scatter.finish(own_ref)
         out = own_ref[...] + mid_ref[...]
         out_ref[:, block_rows(r)] = out[:, :HALF].T
         back_give[1] = out[:, HALF:].astype(BF16)
         second.step(1)
-        swap_copy(2).start()
         for k in range(4):
             two_copy(CHAIN, k, chain_sums).wait_recv()
         add_into(chain_sums.at[1], chain_land2.at[1], columns(CHAIN, "row"))
@@ -1323,6 +1346,8 @@
         add_into(chain_sums.at[2], chain_land2.at[1], columns(CHAIN, "dp"))
         three_copy(CHAIN, 1, chain_sums).start()
         add_into(chain_sums.at[0], chain_land2.at[0], pl.ds(0, chain_cols))
+        three_copy(GATE, 1).start()
+        swap_copy(2).start()
         second.finish(own_ref)
         x, grad = x_ref[...].astype(F32), own_ref[...]
         rinv = norm_scale(x)

time: 324 us -> 293 us (0.904)
  Pallas kernels: 305 us -> 273 us
    pallas_call x1, Pallas kernels: 184 us -> 167 us  [rear_call(): pl.pallas_call(rear_body, out_shape=outs, in_specs=[VMEM_SPEC] * 2 + [ANY...]
    pallas_call x1, Pallas kernels: 122 us -> 106 us  [front_call(): pl.pallas_call(front_body, out_shape=outs, in_specs=[VMEM_SPEC] * 7 + [AN...]
where the time goes in v4:
time: 293 us; the launch traced here: 291 us
  Pallas kernels  273 us (93%)
  other arithmetic  9.74 us (3%)
  local copies, waits for them, and re-layouts  7.16 us (2%)
    pallas_call x1, Pallas kernels, rear_call(): pl.pallas_call(rear_body, out_shape=outs, in_specs=[VMEM_SPEC] * 2 + [ANY...  167 us
    pallas_call x1, Pallas kernels, front_call(): pl.pallas_call(front_body, out_shape=outs, in_specs=[VMEM_SPEC] * 7 + [AN...  106 us

profile of v4, /device:TPU:0, one launch (start us, length us, event | category | flops | bytes accessed | tf_op | source)
XLA Modules:
  0.0 290.7 jit_solution(7376345621872273021)
XLA Ops:
  0.6 0.7 convert_element_type.30
  1.3 1.0 multiply_cosine_fusion
  2.3 0.8 pad_maximum_fusion.table_ref
  3.2 0.7 pad_maximum_fusion.1
  3.9 0.6 broadcast_in_dim.2.small_ref
  4.5 105.7 %front.1 = (bf16[128,1536]{1,0:T(8,128)(2,1)}, bf16[512,1536]{1,0:T(8,128)(2,1)}, bf16[512,384]{1,0:T(8,128)(2,1)}, bf16[512,256]{1,0:T(8,128)(2,1)}, bf16[512,2...) custom-call(bf16[768,256]{1,0:T(8,128)(2,1)} %input_ref.1, ...), custom_call_target="tpu_custom_call" | custom-call | flops 4000000000 | bytes 40000000 | tf_op jit(solution)/shard_map/front/pallas_call | solution.py:877
  110.2 167.4 %rear.1 = (f32[768,256]{1,0:T(8,128)}, f32[768,256]{1,0:T(8,128)}, f32[8,768]{1,0:T(8,128)}, f32[192,384]{1,0:T(8,128)}, f32[192,384]{1,0:T(8,128)}, /*index=5*/...) custom-call(f32[128,1536]{1,0:T(8,128)} %get-tuple-element.37.mid_re, ...), custom_call_target="tpu_custom_call" | custom-call | flops 40000000000 | bytes 80000000 | tf_op jit(solution)/shard_map/rear/pallas_call | solution.py:1514
  277.7 0.0 copy-start.2
  277.7 5.1 %add_bitcast_fusion = (f32[192,2240]{1,0:T(8,128)}, f32[192,2240]{1,0:T(8,128)}, f32[192,2240]{1,0:T(8,128)}) fusion(bf16[3,192,2240]{2,1,0:T(8,128)(2,1)} %get-tuple-element.61, bf16[3,192,2240]{2,1,0:T(8,128)(2,1)} %get-tuple-element.60), kind=kLoop, calls=%fused_computation | loop fusion | flops 3870720 | bytes 10321920 | tf_op jit(solution)/shard_map/add | solution.py:1607
  282.8 0.0 copy-start.1
  282.8 0.0 copy-done.2
  282.8 0.0 copy-start
  282.8 1.4 convert_element_type.31
  284.2 1.5 slice_reduce_fusion
  285.6 0.6 dynamic-slice_bitcast_fusion
  286.2 1.3 slice.32
  287.5 0.0 copy-done.1
  287.5 0.9 copy.29
  288.4 0.0 copy-done
  288.4 0.9 copy.30
  289.3 0.0 copy-done.4
  289.3 0.7 copy.31
  290.0 0.0 copy-done.3
  290.0 0.7 copy.32
  (3 shorter events, 0.0 us)
Async XLA Ops:
  277.7 5.1 %copy-start.2 = (bf16[768,512]{1,0:T(8,128)(2,1)S(1)}, bf16[768,512]{1,0:T(8,128)(2,1)}, u32[]{:S(2)}) copy-start(bf16[768,512]{1,0:T(8,128)(2,1)} %get-tuple-element.58) | copy-start | bytes 2359300
  282.8 4.7 %copy-start.1 = (f32[768,256]{1,0:T(8,128)S(1)}, f32[768,256]{1,0:T(8,128)}, u32[]{:S(2)}) copy-start(f32[768,256]{1,0:T(8,128)} %get-tuple-element.82) | copy-start | bytes 2359300
  282.8 5.6 %copy-start = (f32[768,256]{1,0:T(8,128)S(1)}, f32[768,256]{1,0:T(8,128)}, u32[]{:S(2)}) copy-start(f32[768,256]{1,0:T(8,128)} %get-tuple-element.83) | copy-start | bytes 2359300
  284.2 5.1 %copy-start.4 = (f32[192,384]{1,0:T(8,128)S(1)}, f32[192,384]{1,0:T(8,128)}, u32[]{:S(2)}) copy-start(f32[192,384]{1,0:T(8,128)} %get-tuple-element.85) | copy-start | bytes 884740
  287.5 2.5 copy-start.3

commit v5 on v4

--- a/solution.py
+++ b/solution.py
@@ -463,8 +463,11 @@
         return (came >= 0) & (came < LINE)
 
     def step(self, s):
+        far = jnp.where(self.me < LINE // 2, 1, 0)
+
         @pl.loop(0, 2)
-        def _(side):
+        def _(i):
+            side = lax.rem(i + far, 2)
             j = self.me + (1 - 2 * side) * s
 
             @pl.when((j >= 0) & (j < LINE))
@@ -926,7 +929,8 @@
     out_ref, in_ref, small_ref, query_w_ref, output_w_ref, kv_all_ref, kept_hbm, land2_hbm, land3_hbm,
     cot_ref, activated_ref, gate_grad_ref, upper_grad_ref, out_part_ref, back_part_ref, turned_ref,
     kv_got_ref, got_ref, out_landing, landing, sums, gives, gots,
-    chain_gots, chain_land2, chain_land3, kv_line, small_line, small_swap,
+    chain_gots, chain_land2, chain_land3, kv_line, small_line, small_swap, small_give,
+    small_group,
     load_sems, w_sems, c_sends, c_recv, o_sends, o_recv, r_sends, r_recv, a_sends, a_recv,
     give_sends, give_recv, two_sends, two_recv, three_sends, three_recv, stage_sem, kept_sems,
     swap_sends, swap_recv, kv_sends, kv_recv, kvd_sends, kvd_recv, line_sends, line_recv,
@@ -955,7 +959,7 @@
     turned_load.start()
     cot_loads(lambda copy: copy.start())
 
-    halves = {m: (hidden // 2 + BLOCK - 1) // BLOCK * BLOCK for m in (DOWN, GATE, UPPER)}
+    halves = {m: (hidden // 2 // BLOCK + 2) * BLOCK for m in (DOWN, GATE, UPPER)}
     halves[CHAIN] = chain_cols // 2
 
     def columns(m, axis):
@@ -1045,25 +1049,32 @@
     def stage(m, i):
         return pltpu.make_async_copy(land2_hbm.at[m * 2 + i], gots.at[i], stage_sem.at[m, i])
 
-    def second_stage(m, over_row=True):
+    def second_stage(m, now=(0, 1)):
         for k in range(4):
             two_copy(m, k).wait_recv()
         for i in (1, 0):
             stage(m, i).start()
         stage(m, 1).wait()
         add_into(total_of(m, 0, 1), gots.at[1], columns(m, "row"))
-        three_copy(m, 0).start()
+        if 0 in now:
+            three_copy(m, 0).start()
         add_into(total_of(m, 1, 0), gots.at[1], columns(m, "dp"))
-        if over_row:
+        if 1 in now:
             three_copy(m, 1).start()
         stage(m, 0).wait()
         add_into(total_of(m, 0, 0), gots.at[0], pl.ds(0, hidden))
         kept_copy(m).start()
 
     barrier = pltpu.get_barrier_semaphore()
-    others = [("row", x_to), ("dp", y_to), ("dp", core_to)]
-    for axis, index in others:
-        pl.semaphore_signal(barrier, 1, device_id={axis: index}, device_id_type=MESH_ID)
+    group_size = 8
+    own = r * 4 + d
+
+    def member(i):
+        index = lax.rem(own + i, group_size)
+        return {"row": index // 4, "dp": lax.rem(index, 4)}
+
+    for i in range(1, group_size):
+        pl.semaphore_signal(barrier, 1, device_id=member(i), device_id_type=MESH_ID)
     for s in range(1, LINE):
         pl.semaphore_signal(
             barrier, 1, device_id={"col": lax.rem(me + s, LINE)}, device_id_type=MESH_ID
@@ -1157,7 +1168,7 @@
         load.start()
         start(0, 0, TILE)
         total[...] = jnp.zeros_like(total)
-        pl.semaphore_wait(barrier, len(others) + LINE - 1)
+        pl.semaphore_wait(barrier, group_size - 1 + LINE - 1)
         cot_loads(lambda copy: copy.wait())
         cot_gather.step(1, wait=False)
         load.wait()
@@ -1170,9 +1181,10 @@
         total[...] = jnp.zeros_like(total)
         compute(0)
         compute(1)
-        combine(0)
-        combine(1)
-        sweep(backward, (tiles + 1) % 2, [(3, lambda: out_scatter.step(2))], False)
+        hooks = [
+            (0, lambda: combine(0)), (1, lambda: combine(1)), (4, lambda: out_scatter.step(2)),
+        ]
+        sweep(backward, (tiles + 1) % 2, hooks, False)
         back_part_ref[...] = total[...].astype(BF16)
         cot_gather.drain(1, LINE - 1)
 
@@ -1223,8 +1235,7 @@
         scatter.finish(mid_grad_ref)
         mid, grad = mid_ref[...], mid_grad_ref[...]
         rinv = norm_scale(mid)
-        small_line[me] = jnp.zeros_like(small_line[me])
-        small_line[me, 1:2] = jnp.sum(grad * mid * rinv, 0, keepdims=True)
+        small_line[me, :, MODEL_WIDTH : 2 * MODEL_WIDTH] = jnp.sum(grad * mid * rinv, 0, keepdims=True)
         scaled = grad * gains_ref[1:2]
         inner = jnp.sum(scaled * mid, -1, keepdims=True)
         mid_grad = (
@@ -1258,7 +1269,7 @@
         second_stage(DOWN)
         gather.step(2)
         gather.run_each(2, each)
-        second_stage(UPPER, False)
+        second_stage(UPPER, (0,))
         gather.step(3)
         gather.run_each(3, each)
         out_scatter.step(1)
@@ -1329,11 +1340,11 @@
         for i in range(4):
             chain_combine(i)
         three_copy(UPPER, 1).start()
-        small_line[me, 2:3, :proj_cols] = jnp.sum(
+        small_line[me, :, 2 * MODEL_WIDTH :] = jnp.sum(
             proj_grad_ref[...].astype(F32), 0, keepdims=True
         )
         second.step(2)
-        second_stage(GATE, False)
+        second_stage(GATE, (0,))
         out_scatter.finish(own_ref)
         out = own_ref[...] + mid_ref[...]
         out_ref[:, block_rows(r)] = out[:, :HALF].T
@@ -1348,6 +1359,19 @@
         add_into(chain_sums.at[0], chain_land2.at[0], pl.ds(0, chain_cols))
         three_copy(GATE, 1).start()
         swap_copy(2).start()
+        for k in range(2):
+            three_copy(CHAIN, k, chain_sums).wait_recv()
+        total = chain_sums[0].astype(F32) + chain_land3[...].astype(F32)
+        query_w_ref[...] = total[:, :query_cols]
+        output_w_ref[...] = total[:, proj_cols:]
+        kv_line[me] = total[:, query_cols:proj_cols].astype(BF16)
+
+        def kv_line_copy(s):
+            to = lax.rem(me + s, LINE)
+            return send(kv_line.at[me], kv_line.at[me], kv_sends.at[s], kv_recv.at[me], "col", to)
+
+        for s in range(1, LINE):
+            kv_line_copy(s).start()
         second.finish(own_ref)
         x, grad = x_ref[...].astype(F32), own_ref[...]
         rinv = norm_scale(x)
@@ -1356,7 +1380,7 @@
         input_grad = mid_grad_ref[...] + rinv * scaled - x * rinv**3 * inner / MODEL_WIDTH
         back_give[0] = input_grad[:, HALF:].astype(BF16)
         swap_copy(1).start()
-        small_line[me, 0:1] = jnp.sum(grad * x * rinv, 0, keepdims=True)
+        small_line[me, :, :MODEL_WIDTH] = jnp.sum(grad * x * rinv, 0, keepdims=True)
 
         def small_line_copy(s):
             to = lax.rem(me + s, LINE)
@@ -1368,53 +1392,7 @@
             small_line_copy(s).start()
         in_ref[:, block_rows(r)] = input_grad[:, :HALF].T
 
-        for s in range(1, LINE):
-            landed(small_line.at[me], line_recv.at[lax.rem(me + s, LINE)])
         group = LINE // KEYVALUE_HEADS
-        lines = [small_line[j] for j in range(LINE)]
-        gain_sum = lines[0][:2] + lines[1][:2] + lines[2][:2] + lines[3][:2]
-        small_swap[0] = jnp.zeros_like(small_swap[0])
-        small_swap[0, 0:2] = gain_sum
-        small_swap[0, 2:3, :query_cols] = small_line[me, 2:3, :query_cols]
-        for i in range(2):
-            for h in range(KEYVALUE_HEADS):
-                at = query_cols + i * HEAD_SIZE
-                part = lines[h * group][2:3, at : at + HEAD_SIZE]
-                for j in range(1, group):
-                    part = part + lines[h * group + j][2:3, at : at + HEAD_SIZE]
-                at = (i * KEYVALUE_HEADS + h) * HEAD_SIZE
-                small_swap[0, 3:4, at : at + HEAD_SIZE] = part
-
-        def small_copy(i):
-            axis, to = (("dp", core_to), ("dp", y_to), ("row", x_to))[i]
-            return send(
-                small_swap.at[2 * i], small_swap.at[2 * i + 1], small_sends.at[i],
-                small_recv.at[i], axis, to,
-            )
-
-        small_copy(0).start()
-        small_copy(0).wait_recv()
-        small_swap[2] = small_swap[0] + small_swap[1]
-        small_copy(1).start()
-
-        for k in range(2):
-            three_copy(CHAIN, k, chain_sums).wait_recv()
-        total = chain_sums[0].astype(F32) + chain_land3[...].astype(F32)
-        query_w_ref[...] = total[:, :query_cols]
-        output_w_ref[...] = total[:, proj_cols:]
-        kv_line[me] = total[:, query_cols:proj_cols].astype(BF16)
-
-        def kv_line_copy(s):
-            to = lax.rem(me + s, LINE)
-            return send(kv_line.at[me], kv_line.at[me], kv_sends.at[s], kv_recv.at[me], "col", to)
-
-        for s in range(1, LINE):
-            kv_line_copy(s).start()
-        small_copy(1).wait_recv()
-        both = small_swap[2] + small_swap[3]
-        small_swap[4, :2, :HALF] = both[:2, HALF:]
-        small_swap[4, 2:, :HALF] = both[2:, :HALF]
-        small_copy(2).start()
         for s in range(1, LINE):
             landed(kv_line.at[me], kv_recv.at[lax.rem(me + s, LINE)])
         dp_rows = aligned(d * UNIT, UNIT, UNIT)
@@ -1438,15 +1416,51 @@
 
         kv_dp_copy(1).start()
         kv_dp_copy(0).start()
+
+        for s in range(1, LINE):
+            landed(small_line.at[me], line_recv.at[lax.rem(me + s, LINE)])
+        lines = [small_line[j] for j in range(LINE)]
+        total_line = lines[0] + lines[1] + lines[2] + lines[3]
+        small_swap[...] = jnp.zeros_like(small_swap)
+        small_swap[0:1] = total_line[:, :MODEL_WIDTH]
+        small_swap[1:2] = total_line[:, MODEL_WIDTH : 2 * MODEL_WIDTH]
+        bias_at = 2 * MODEL_WIDTH
+        small_swap[2:3, :query_cols] = small_line[me, :, bias_at : bias_at + query_cols]
+        for i in range(2):
+            for h in range(KEYVALUE_HEADS):
+                at = bias_at + query_cols + i * HEAD_SIZE
+                part = lines[h * group][:, at : at + HEAD_SIZE]
+                for j in range(1, group):
+                    part = part + lines[h * group + j][:, at : at + HEAD_SIZE]
+                at = (i * KEYVALUE_HEADS + h) * HEAD_SIZE
+                small_swap[3:4, at : at + HEAD_SIZE] = part
+
+        small_give[0] = small_swap[:, :HALF]
+        small_give[1, :2] = small_swap[:2, HALF:]
+        small_give[1, 2:] = small_swap[2:, :HALF]
+        small_group[own] = small_give[0]
+
+        def small_copy(i):
+            to = member(i)
+            kind = jnp.where(to["row"] == r, 0, 1)
+            return pltpu.make_async_remote_copy(
+                small_give.at[kind], small_group.at[own], small_sends.at[i], small_recv.at[own],
+                device_id=to, device_id_type=MESH_ID,
+            )
+
+        for i in range(1, group_size):
+            small_copy(i).start()
+        landed(kv_rows(y_to), kvd_recv.at[1])
+        kv_dp_copy(2).start()
         for i in (2, 1):
             swap_copy(i).wait_recv()
             to_ref = (in_ref, out_ref)[i - 1]
             to_ref[:, block_rows(1 - r)] = got_ref[i - 1].astype(F32).T
-        small_copy(2).wait_recv()
-        small_ref[...] = both[:, :HALF] + small_swap[5, :, :HALF]
-
-        landed(kv_rows(y_to), kvd_recv.at[1])
-        kv_dp_copy(2).start()
+        for i in range(1, group_size):
+            source = lax.rem(own + i, group_size)
+            landed(small_group.at[source], small_recv.at[source])
+        small_ref[...] = sum(small_group[i] for i in range(group_size))
+
         landed(kv_rows(core_to), kvd_recv.at[0])
         landed(kv_rows(diagonal_to), kvd_recv.at[2])
         for m in (DOWN, GATE, UPPER):
@@ -1463,10 +1477,11 @@
             three_copy(CHAIN, k, chain_sums).wait_send()
         for i in range(3):
             swap_copy(i).wait_send()
-            small_copy(i).wait_send()
             kv_dp_copy(i).wait_send()
             kv_line_copy(1 + i).wait_send()
             small_line_copy(1 + i).wait_send()
+        for i in range(1, group_size):
+            small_copy(i).wait_send()
         gather.drain()
         out_scatter.drain()
         second.drain()
@@ -1535,8 +1550,10 @@
             pltpu.VMEM((2, UNIT, chain_cols), BF16),
             pltpu.VMEM((UNIT, chain_cols), BF16),
             pltpu.VMEM((LINE, UNIT, 2 * HEAD_SIZE), BF16),
-            pltpu.VMEM((LINE, 8, MODEL_WIDTH), F32),
-            pltpu.VMEM((6, 8, MODEL_WIDTH), F32),
+            pltpu.VMEM((LINE, 1, 2 * MODEL_WIDTH + proj_cols), F32),
+            pltpu.VMEM((8, MODEL_WIDTH), F32),
+            pltpu.VMEM((2, 8, HALF), F32),
+            pltpu.VMEM((8, 8, HALF), F32),
             DMA((16,)),
             DMA((2, 3, 2)),
         ]
@@ -1553,7 +1570,7 @@
             DMA((LINE,)), DMA((LINE,)),
             DMA((3,)), DMA((3,)),
             DMA((LINE,)), DMA((LINE,)),
-            DMA((3,)), DMA((3,)),
+            DMA((8,)), DMA((8,)),
             pltpu.SemaphoreType.REGULAR,
         ],
         compiler_params=pltpu.CompilerParams(

time: 293 us -> 284 us (0.969)
  Pallas kernels: 273 us -> 266 us
    pallas_call x1, Pallas kernels: 167 us -> 160 us  [rear_call(): pl.pallas_call(rear_body, out_shape=outs, in_specs=[VMEM_SPEC] * 2 + [ANY...]
where the time goes in v5:
time: 284 us; the launch traced here: 283 us
  Pallas kernels  266 us (94%)
  other arithmetic  9.74 us (3%)
  local copies, waits for them, and re-layouts  7.16 us (3%)
    pallas_call x1, Pallas kernels, rear_call(): pl.pallas_call(rear_body, out_shape=outs, in_specs=[VMEM_SPEC] * 2 + [ANY...  160 us
    pallas_call x1, Pallas kernels, front_call(): pl.pallas_call(front_body, out_shape=outs, in_specs=[VMEM_SPEC] * 7 + [AN...  105 us

profile of v5, /device:TPU:0, one launch (start us, length us, event | category | flops | bytes accessed | tf_op | source)
XLA Modules:
  0.0 283.5 jit_solution(13670115493037685386)
XLA Ops:
  0.6 0.7 convert_element_type.30
  1.3 1.0 multiply_cosine_fusion
  2.3 0.8 pad_maximum_fusion.table_ref
  3.2 0.7 pad_maximum_fusion.1
  3.9 0.6 broadcast_in_dim.2.small_ref
  4.5 105.4 %front.1 = (bf16[128,1536]{1,0:T(8,128)(2,1)}, bf16[512,1536]{1,0:T(8,128)(2,1)}, bf16[512,384]{1,0:T(8,128)(2,1)}, bf16[512,256]{1,0:T(8,128)(2,1)}, bf16[512,2...) custom-call(bf16[768,256]{1,0:T(8,128)(2,1)} %input_ref.1, ...), custom_call_target="tpu_custom_call" | custom-call | flops 4000000000 | bytes 40000000 | tf_op jit(solution)/shard_map/front/pallas_call | solution.py:880
  110.0 160.4 %rear.1 = (f32[768,256]{1,0:T(8,128)}, f32[768,256]{1,0:T(8,128)}, f32[8,768]{1,0:T(8,128)}, f32[192,384]{1,0:T(8,128)}, f32[192,384]{1,0:T(8,128)}, /*index=5*/...) custom-call(f32[128,1536]{1,0:T(8,128)} %get-tuple-element.37.mid_re, ...), custom_call_target="tpu_custom_call" | custom-call | flops 40000000000 | bytes 80000000 | tf_op jit(solution)/shard_map/rear/pallas_call | solution.py:1529
  270.4 0.0 copy-start.2
  270.4 5.1 %add_bitcast_fusion = (f32[192,2240]{1,0:T(8,128)}, f32[192,2240]{1,0:T(8,128)}, f32[192,2240]{1,0:T(8,128)}) fusion(bf16[3,192,2240]{2,1,0:T(8,128)(2,1)} %get-tuple-element.61, bf16[3,192,2240]{2,1,0:T(8,128)(2,1)} %get-tuple-element.60), kind=kLoop, calls=%fused_computation | loop fusion | flops 3870720 | bytes 10321920 | tf_op jit(solution)/shard_map/add | solution.py:1624
  275.5 0.0 copy-start.1
  275.5 0.0 copy-done.2
  275.5 0.0 copy-start
  275.6 1.4 convert_element_type.31
  276.9 1.5 slice_reduce_fusion
  278.4 0.6 dynamic-slice_bitcast_fusion
  279.0 1.3 slice.32
  280.3 0.0 copy-done.1
  280.3 0.9 copy.29
  281.1 0.0 copy-done
  281.1 0.9 copy.30
  282.0 0.0 copy-done.4
  282.0 0.7 copy.31
  282.7 0.0 copy-done.3
  282.7 0.7 copy.32
  (3 shorter events, 0.0 us)
Async XLA Ops:
  270.4 5.1 %copy-start.2 = (bf16[768,512]{1,0:T(8,128)(2,1)S(1)}, bf16[768,512]{1,0:T(8,128)(2,1)}, u32[]{:S(2)}) copy-start(bf16[768,512]{1,0:T(8,128)(2,1)} %get-tuple-element.58) | copy-start | bytes 2359300
  275.5 4.7 %copy-start.1 = (f32[768,256]{1,0:T(8,128)S(1)}, f32[768,256]{1,0:T(8,128)}, u32[]{:S(2)}) copy-start(f32[768,256]{1,0:T(8,128)} %get-tuple-element.82) | copy-start | bytes 2359300
  275.5 5.6 %copy-start = (f32[768,256]{1,0:T(8,128)S(1)}, f32[768,256]{1,0:T(8,128)}, u32[]{:S(2)}) copy-start(f32[768,256]{1,0:T(8,128)} %get-tuple-element.83) | copy-start | bytes 2359300
  276.9 5.1 %copy-start.4 = (f32[192,384]{1,0:T(8,128)S(1)}, f32[192,384]{1,0:T(8,128)}, u32[]{:S(2)}) copy-start(f32[192,384]{1,0:T(8,128)} %get-tuple-element.85) | copy-start | bytes 884740
  280.3 2.5 copy-start.3

commit v6 on v5

--- a/solution.py
+++ b/solution.py
@@ -610,14 +610,15 @@
 
 
 def front_body(
-    input_ref, cot_in_ref, table_ref, small_ref, query_w_ref, kv_w_ref, output_w_ref,
+    input_ref, cot_in_ref, table_ref, attention_gain_ref, feedforward_gain_ref, query_bias_ref,
+    kv_bias_ref, query_w_ref, kv_w_ref, output_w_ref,
     gate_hbm, upper_hbm, down_hbm,
     x_hbm, normed_hbm, query_hbm, kv_hbm, kv_other_hbm, cos_hbm, sin_hbm, gains_ref,
     attended_hbm, probs_hbm, mid_hbm, normed_two_hbm, turned_hbm, cot_hbm, proj_hbm, proj_other_hbm,
     weights_other_hbm,
     x_ref, normed_ref, query_ref, kv_ref, kv_other_ref, cos_ref, sin_ref,
     attended_ref, probs_ref, mid_ref, normed_two_ref, turned_ref, cot_ref, proj_ref, proj_other_ref,
-    passing, tables, bias_ref, landing, store_sems,
+    passing, tables, bias_ref, small_ref, landing, store_sems,
     swap_sends, swap_recv, piece_sends, piece_recv, kv_sends, kv_recv,
     g_sends, g_recv, c_sends, c_recv, n_sends, n_recv, s_sends, s_recv,
 ):
@@ -647,6 +648,12 @@
             )
         )
     ]
+
+    low = 0
+    for vector_ref in (attention_gain_ref, feedforward_gain_ref, query_bias_ref, kv_bias_ref):
+        size = vector_ref.shape[0]
+        small_ref[0, low : low + size] = vector_ref[...]
+        low += size
 
     passing[0] = input_ref[:, block_rows(1 - r)].T
     x_ref[:, :HALF] = input_ref[:, block_rows(r)].T
@@ -880,13 +887,14 @@
     return pl.pallas_call(
         front_body,
         out_shape=outs,
-        in_specs=[VMEM_SPEC] * 7 + [ANY_SPEC] * 3,
+        in_specs=[VMEM_SPEC] * 10 + [ANY_SPEC] * 3,
         out_specs=[VMEM_SPEC if out is gains else ANY_SPEC for out in outs],
         scratch_shapes=[pltpu.VMEM(out.shape, out.dtype) for out in outs[:-1] if out is not gains]
         + [
             pltpu.VMEM((2, BLOCK, HALF), BF16),
             pltpu.VMEM((2 * BLOCK, HEAD_SIZE), F32),
             pltpu.VMEM((1, proj_cols), F32),
+            pltpu.VMEM((1, 2 * HALF + query_cols + 2 * KEYVALUE_HEADS * HEAD_SIZE), F32),
             pltpu.VMEM((2, LINE, BLOCK, MODEL_WIDTH), BF16),
             DMA((15,)),
             DMA((12,)),
@@ -1132,16 +1140,16 @@
             body(pl.ds(tiles * TILE, rest), slot, rest)
 
         def add_products(slot, size, factors, cols):
-            width = 512
+            width = 768
 
             @pl.loop(0, MODEL_WIDTH // width)
             def _(i):
                 at = aligned(i * width, width)
-                term = sum(
-                    dot(factor[:, cols], weights[slot, m, pl.ds(0, size), at])
-                    for factor, m in factors
+                left = jnp.concatenate([factor[:, cols] for factor, _ in factors], 1)
+                right = jnp.concatenate(
+                    [weights[slot, m, pl.ds(0, size), at] for _, m in factors], 0
                 )
-                total[:, at] += term
+                total[:, at] += dot(left, right)
 
         def forward(cols, slot, size):
             here = pl.ds(0, size)
@@ -1583,6 +1591,81 @@
     )(*args)
 
 
+def finish_body(
+    out_hbm, in_hbm, query_hbm, output_hbm, kv_hbm, kept_hbm, landing_hbm, small_ref,
+    out_to, in_to, query_to, output_to, kv_to, down_to, gate_to, upper_to,
+    attention_gain_to, feedforward_gain_to, query_bias_to, kv_bias_to,
+    out_ref, in_ref, query_ref, output_ref, kv_ref, kv_wide, kept, landing, wide, load_sems, store_sems,
+):
+    passed = (
+        (out_hbm, out_ref, out_to), (in_hbm, in_ref, in_to), (query_hbm, query_ref, query_to),
+        (output_hbm, output_ref, output_to),
+    )
+    sums = (down_to, gate_to, upper_to)
+    loads = []
+    for m in range(3):
+        loads.append(pltpu.make_async_copy(kept_hbm.at[m], kept.at[m], load_sems.at[2 * m]))
+        loads.append(pltpu.make_async_copy(landing_hbm.at[m], landing.at[m], load_sems.at[2 * m + 1]))
+    loads.append(pltpu.make_async_copy(kv_hbm, kv_ref, load_sems.at[6]))
+    for i, (src, here, _) in enumerate(passed):
+        loads.append(pltpu.make_async_copy(src, here, load_sems.at[7 + i]))
+    stores = [pltpu.make_async_copy(wide.at[m], sums[m], store_sems.at[m]) for m in range(3)]
+    stores.append(pltpu.make_async_copy(kv_wide, kv_to, store_sems.at[3]))
+    for i, (_, here, to) in enumerate(passed):
+        stores.append(pltpu.make_async_copy(here, to, store_sems.at[4 + i]))
+    for load in loads:
+        load.start()
+    for m in range(3):
+        loads[2 * m].wait()
+        loads[2 * m + 1].wait()
+
+        @pl.loop(0, UNIT // 32)
+        def _(i):
+            at = aligned(i * 32, 32, 32)
+            wide[m, at] = kept[m, at].astype(F32) + landing[m, at].astype(F32)
+
+        stores[m].start()
+    loads[6].wait()
+    kv_wide[...] = kv_ref[...].astype(F32)
+    stores[3].start()
+    for i in range(4):
+        loads[7 + i].wait()
+        stores[4 + i].start()
+    attention_gain_to[...] = small_ref[0]
+    feedforward_gain_to[...] = small_ref[1]
+    query_bias_to[...] = small_ref[2, : query_bias_to.shape[0]]
+    kv_bias_to[...] = small_ref[3, : kv_bias_to.shape[0]]
+    for store in stores:
+        store.wait()
+
+
+def finish_call(out, input_grad, query_sum, output_sum, kv_all, kept, landing, sums):
+    like = lambda v, dtype: jax.ShapeDtypeStruct(v.shape, dtype)
+    unit = jax.ShapeDtypeStruct(kept.shape[1:], F32)
+    vector = lambda n: jax.ShapeDtypeStruct((n,), F32)
+    passed = [like(v, F32) for v in (out, input_grad, query_sum, output_sum)]
+    outs = passed + [like(kv_all, F32)] + [unit] * 3
+    small = [vector(HALF), vector(HALF), vector(query_sum.shape[1]), vector(kv_all.shape[1])]
+    return pl.pallas_call(
+        finish_body,
+        out_shape=outs + small,
+        in_specs=[ANY_SPEC] * 7 + [VMEM_SPEC],
+        out_specs=[ANY_SPEC] * 8 + [VMEM_SPEC] * 4,
+        scratch_shapes=[pltpu.VMEM(v.shape, F32) for v in passed]
+        + [
+            pltpu.VMEM(kv_all.shape, BF16),
+            pltpu.VMEM(kv_all.shape, F32),
+            pltpu.VMEM(kept.shape, BF16),
+            pltpu.VMEM(kept.shape, BF16),
+            pltpu.VMEM(kept.shape, F32),
+            DMA((11,)),
+            DMA((8,)),
+        ],
+        compiler_params=pltpu.CompilerParams(vmem_limit_bytes=67_043_328),
+        name="finish",
+    )(out, input_grad, query_sum, output_sum, kv_all, kept, landing, sums)
+
+
 def fast_device(
     block_input,
     position_ids,
@@ -1604,14 +1687,14 @@
     frequencies = THETA ** (-(jnp.arange(HEAD_SIZE // 2, dtype=F32) * 2.0 / HEAD_SIZE))
     angles = position_ids.astype(F32)[:, None] * frequencies[None, :]
     table = jnp.concatenate([jnp.cos(angles), jnp.sin(angles)], -1)
-    small = jnp.concatenate([attention_gain, feedforward_gain, query_bias, key_value_bias])[None]
     gate_t, upper_t, down_t = gate_weight.T, upper_weight.T, down_weight.T
     (
         x_own, normed_one, query_rot, kv_own, kv_other, cosine, sine, gains, attended, probs,
         mid, normed_two, normed_turned, cot_part, own_proj, other_proj, other_weights,
     ) = front_call(
         proj_cols, query_cols, hidden,
-        block_input, out_cotangent, table, small, query_weight, key_value_weight, output_weight,
+        block_input, out_cotangent, table, attention_gain, feedforward_gain, query_bias,
+        key_value_bias, query_weight, key_value_weight, output_weight,
         gate_t, upper_t, down_t,
     )
     out, input_grad, sums, query_sum, output_sum, kv_all, kept, _, landing = rear_call(
@@ -1620,23 +1703,24 @@
         normed_two, normed_turned, cot_part, gate_t, upper_t, down_t, other_weights, own_proj, other_proj, query_rot, kv_own,
         kv_other, attended, probs, cosine, sine, x_own, normed_one,
     )
-    down_sum, gate_sum, upper_sum = (
-        kept[m].astype(F32) + landing[m].astype(F32) for m in range(3)
-    )
+    (
+        out, input_grad, query_sum, output_sum, kv_sum, down_sum, gate_sum, upper_sum,
+        attention_gain_sum, feedforward_gain_sum, query_bias_sum, kv_bias_sum,
+    ) = finish_call(out, input_grad, query_sum, output_sum, kv_all, kept, landing, sums)
     bias_rows = query_cols // lax.axis_size("dp")
     query_bias_grad = lax.dynamic_slice_in_dim(
-        sums[2], lax.axis_index("dp") * bias_rows, bias_rows, 0
+        query_bias_sum, lax.axis_index("dp") * bias_rows, bias_rows, 0
     )
     return (
         out,
         input_grad,
-        sums[0],
+        attention_gain_sum,
         query_sum,
         query_bias_grad,
-        kv_all.astype(F32),
-        sums[3, : 2 * KEYVALUE_HEADS * HEAD_SIZE],
+        kv_sum,
+        kv_bias_sum,
         output_sum,
-        sums[1],
+        feedforward_gain_sum,
         gate_sum,
         upper_sum,
         down_sum,

time: 284 us -> 277 us (0.975)
  other arithmetic: 9.74 us -> 2.53 us
  Pallas kernels: 266 us -> 272 us
  local copies, waits for them, and re-layouts: 7.16 us -> 1.2 us
    pallas_call x1 -> x2, Pallas kernels: 105 us -> 113 us  [the longest x1 105 us: front_call(): pl.pallas_call(front_body, out_shape=outs, in_specs=[VMEM_SPEC] * 10 + [A...]
    add x1 -> x0, other arithmetic: 5.12 us -> none  [fast_device(): kept[m].astype(F32) + landing[m].astype(F32)]
    unnamed x14 -> x0, local copies, waits for them, and re-layouts: 3.21 us -> none
where the time goes in v6:
time: 277 us; the launch traced here: 276 us
  Pallas kernels  272 us (98%)
    pallas_call x1, Pallas kernels, rear_call(): pl.pallas_call(rear_body, out_shape=outs, in_specs=[VMEM_SPEC] * 2 + [ANY...  159 us
    pallas_call x1, Pallas kernels, front_call(): pl.pallas_call(front_body, out_shape=outs, in_specs=[VMEM_SPEC] * 10 + [A...  105 us
    pallas_call x1, Pallas kernels, finish_call(): pl.pallas_call(finish_body, out_shape=outs + small, in_specs=[ANY_SPEC] *...  7.49 us

profile of v6, /device:TPU:0, one launch (start us, length us, event | category | flops | bytes accessed | tf_op | source)
XLA Modules:
  0.0 276.4 jit_solution(16903392160796586590)
XLA Ops:
  0.6 0.7 convert_element_type.3
  1.3 1.0 multiply_cosine_fusion
  2.3 0.8 pad_maximum_fusion.table_ref
  3.2 105.4 %front.1 = (bf16[128,1536]{1,0:T(8,128)(2,1)}, bf16[512,1536]{1,0:T(8,128)(2,1)}, bf16[512,384]{1,0:T(8,128)(2,1)}, bf16[512,256]{1,0:T(8,128)(2,1)}, bf16[512,2...) custom-call(bf16[768,256]{1,0:T(8,128)(2,1)} %input_ref.1, ...), custom_call_target="tpu_custom_call" | custom-call | flops 4000000000 | bytes 40000000 | tf_op jit(solution)/shard_map/front/pallas_call | solution.py:887
  108.6 159.1 %rear.1 = (f32[768,256]{1,0:T(8,128)}, f32[768,256]{1,0:T(8,128)}, f32[8,768]{1,0:T(8,128)}, f32[192,384]{1,0:T(8,128)}, f32[192,384]{1,0:T(8,128)}, /*index=5*/...) custom-call(f32[128,1536]{1,0:T(8,128)} %get-tuple-element.49.mid_re, ...), custom_call_target="tpu_custom_call" | custom-call | flops 40000000000 | bytes 80000000 | tf_op jit(solution)/shard_map/rear/pallas_call | solution.py:1537
  267.7 7.5 %finish.1 = (f32[768,256]{1,0:T(8,128)}, f32[768,256]{1,0:T(8,128)}, f32[192,384]{1,0:T(8,128)}, f32[192,384]{1,0:T(8,128)}, f32[768,512]{1,0:T(8,128)}, /*index...) custom-call(f32[768,256]{1,0:T(8,128)} %get-tuple-element.66.out_hbm, ...), custom_call_target="tpu_custom_call" | custom-call | tf_op jit(solution)/shard_map/finish/pallas_call | solution.py:1649
  275.2 1.2 dynamic_slice.3
  (1 shorter events, 0.0 us)

commit v7 on v6

--- a/solution.py
+++ b/solution.py
@@ -1633,7 +1633,13 @@
         stores[4 + i].start()
     attention_gain_to[...] = small_ref[0]
     feedforward_gain_to[...] = small_ref[1]
-    query_bias_to[...] = small_ref[2, : query_bias_to.shape[0]]
+    rows = query_bias_to.shape[0]
+    for i in range(4):
+
+        @pl.when(lax.axis_index("dp") == i)
+        def _():
+            query_bias_to[...] = small_ref[2, i * rows : (i + 1) * rows]
+
     kv_bias_to[...] = small_ref[3, : kv_bias_to.shape[0]]
     for store in stores:
         store.wait()
@@ -1645,7 +1651,7 @@
     vector = lambda n: jax.ShapeDtypeStruct((n,), F32)
     passed = [like(v, F32) for v in (out, input_grad, query_sum, output_sum)]
     outs = passed + [like(kv_all, F32)] + [unit] * 3
-    small = [vector(HALF), vector(HALF), vector(query_sum.shape[1]), vector(kv_all.shape[1])]
+    small = [vector(HALF), vector(HALF), vector(query_sum.shape[1] // 4), vector(kv_all.shape[1])]
     return pl.pallas_call(
         finish_body,
         out_shape=outs + small,
@@ -1707,16 +1713,12 @@
         out, input_grad, query_sum, output_sum, kv_sum, down_sum, gate_sum, upper_sum,
         attention_gain_sum, feedforward_gain_sum, query_bias_sum, kv_bias_sum,
     ) = finish_call(out, input_grad, query_sum, output_sum, kv_all, kept, landing, sums)
-    bias_rows = query_cols // lax.axis_size("dp")
-    query_bias_grad = lax.dynamic_slice_in_dim(
-        query_bias_sum, lax.axis_index("dp") * bias_rows, bias_rows, 0
-    )
     return (
         out,
         input_grad,
         attention_gain_sum,
         query_sum,
-        query_bias_grad,
+        query_bias_sum,
         kv_sum,
         kv_bias_sum,
         output_sum,

time: 277 us -> 276 us (level)
  no operation moved by 1% of the time
where the time goes in v7:
time: 276 us; the launch traced here: 275 us
  Pallas kernels  272 us (99%)
    pallas_call x1, Pallas kernels, rear_call(): pl.pallas_call(rear_body, out_shape=outs, in_specs=[VMEM_SPEC] * 2 + [ANY...  159 us
    pallas_call x1, Pallas kernels, front_call(): pl.pallas_call(front_body, out_shape=outs, in_specs=[VMEM_SPEC] * 10 + [A...  105 us
    pallas_call x1, Pallas kernels, finish_call(): pl.pallas_call(finish_body, out_shape=outs + small, in_specs=[ANY_SPEC] *...  7.49 us

profile of v7, /device:TPU:0, one launch (start us, length us, event | category | flops | bytes accessed | tf_op | source)
XLA Modules:
  0.0 275.3 jit_solution(13079802493833578971)
XLA Ops:
  0.7 0.7 convert_element_type.3
  1.3 1.0 multiply_cosine_fusion
  2.3 0.8 pad_maximum_fusion.table_ref
  3.2 105.4 %front.1 = (bf16[128,1536]{1,0:T(8,128)(2,1)}, bf16[512,1536]{1,0:T(8,128)(2,1)}, bf16[512,384]{1,0:T(8,128)(2,1)}, bf16[512,256]{1,0:T(8,128)(2,1)}, bf16[512,2...) custom-call(bf16[768,256]{1,0:T(8,128)(2,1)} %input_ref.1, ...), custom_call_target="tpu_custom_call" | custom-call | flops 4000000000 | bytes 40000000 | tf_op jit(solution)/shard_map/front/pallas_call | solution.py:887
  108.6 159.0 %rear.1 = (f32[768,256]{1,0:T(8,128)}, f32[768,256]{1,0:T(8,128)}, f32[8,768]{1,0:T(8,128)}, f32[192,384]{1,0:T(8,128)}, f32[192,384]{1,0:T(8,128)}, /*index=5*/...) custom-call(f32[128,1536]{1,0:T(8,128)} %get-tuple-element.49.mid_re, ...), custom_call_target="tpu_custom_call" | custom-call | flops 40000000000 | bytes 80000000 | tf_op jit(solution)/shard_map/rear/pallas_call | solution.py:1537
  267.7 7.5 %finish.1 = (f32[768,256]{1,0:T(8,128)}, f32[768,256]{1,0:T(8,128)}, f32[192,384]{1,0:T(8,128)}, f32[192,384]{1,0:T(8,128)}, f32[768,512]{1,0:T(8,128)}, /*index...) custom-call(f32[768,256]{1,0:T(8,128)} %get-tuple-element.66.out_hbm, ...), custom_call_target="tpu_custom_call" | custom-call | tf_op jit(solution)/shard_map/finish/pallas_call | solution.py:1655
  (1 shorter events, 0.0 us)
